TPU v7x, 256 devices: a whole 4x4x8 slice. The times are simulated.
256 devices in a mesh: seq: 16 (over z, core), grp: 2 (over y_hi), dp: 8 (over y_lo, x).
Axes of the slice: x: 4, y: 4 (y_hi: 2, y_lo: 2; y = y_hi * 2 + y_lo), z: 8, core: 2. Of those that a mesh axis runs over, the one named last changes fastest.
Arguments:
- clips: bfloat16 [8, 2048, 1408], P('dp', 'seq'), may hold values from -6 to 6
- context: int32 [8, 2048], P('dp', 'seq'), may hold values from 0 to 1, as said below
- predict_index: int32 [8, 3072], P('dp', 'seq'), may hold values from -1 to 2047, as said below
- target_qkv: bfloat16 [3, 1408, 1408], P(None, 'dp', 'grp'), may hold values from -8 to 8
- target_out: bfloat16 [1408, 1408], P('grp'), may hold values from -0.15625 to 0.15625
- student_qkv: bfloat16 [3, 1408, 1408], P(None, 'dp', 'grp'), may hold values from -8 to 8
- student_out: bfloat16 [1408, 1408], P('grp', 'dp'), may hold values from -0.15625 to 0.15625
- mask_token: float32 [1408], replicated, may hold values from -4 to 4
Outputs:
- out_grad: float32 [1408, 1408], P('grp', 'dp')
- target_blend: float32 [1408, 1408], P('grp')
Inputs may be any that keep to these rules, and one draw needn't show every extreme that they name: In every aligned block of 128 tokens of a clip exactly 32 tokens have context 1 and the others 0. `predict_index`: each device's 192 slots name distinct target positions (context 0) of its clip, followed by -1 in the unused slots; different devices' lists may name the same position. In every clip one list is full.
All inputs are finite; a program needn't handle non-finite values.
Results may differ from a plain program's by a relative error of at most 0.014.
Values may be sent and summed in bfloat16 or wider, within the bound.
No kernel may reach another device: no remote copies, remote signals or barrier semaphores. Data moves between devices by JAX's collectives and lax.ppermute only.
A program may use at most 128 MiB of HBM per device.

v0:
```python
import functools
import math

import jax
import jax.numpy as jnp
from jax import lax
from jax.experimental import pallas as pl
from jax.experimental.pallas import tpu as pltpu
from jax.sharding import Mesh, PartitionSpec as P

HEAD_DIM = 88
LANES = 128
CTX = 32
BLOCK = 128
TGT = 96
OWN = 48
N_Z = 8
N_DP = 8
STRIPE = 11
EPSILON = 1e-06
MOMENTUM = 0.99
SCALE = HEAD_DIM ** (-0.5)
BF = jnp.bfloat16
F32 = jnp.float32
I32 = jnp.int32
SWAP = [(0, 1), (1, 0)]
DP = ("ylo", "x")
SMEM = pl.BlockSpec(memory_space=pltpu.SMEM)


def iota(shape, dim):
    return lax.broadcasted_iota(I32, shape, dim)


def mm(a, b):
    return jnp.dot(a, b, preferred_element_type=F32)


def mm_nt(a, b):
    return lax.dot_general(a, b, (((1,), (1,)), ((), ())), preferred_element_type=F32)


def sds(shape, dtype):
    return jax.ShapeDtypeStruct(shape, dtype)


def call(kernel, outs, scratch=(), flops=10**8, name=None, **specs):
    return pl.pallas_call(
        kernel,
        out_shape=outs,
        scratch_shapes=list(scratch),
        **specs,
        cost_estimate=pl.CostEstimate(flops=flops, bytes_accessed=10**6, transcendentals=0),
        name=name,
    )


def to_all(shard, axes, count):
    copies = jnp.broadcast_to(shard[None], (count, *shard.shape))
    return lax.all_to_all(copies, axes, split_axis=0, concat_axis=0, tiled=True)


def normalized(values):
    center = values - jnp.mean(values, axis=-1, keepdims=True)
    factor = lax.rsqrt(jnp.mean(center * center, axis=-1, keepdims=True) + EPSILON)
    return (center * factor, factor)


def sorted_norm_kernel(tokens_ref, context_ref, first_ref, second_ref, perm_ref):
    normed = normalized(tokens_ref[...].astype(F32))[0].astype(BF)
    flag = jnp.where(context_ref[...] == 1, 1.0, 0.0)
    upto = jnp.where(iota((BLOCK, BLOCK), 0) <= iota((BLOCK, BLOCK), 1), 1.0, 0.0).astype(BF)
    before = mm(jnp.broadcast_to(flag, (16, BLOCK)).astype(BF), upto)[:1]
    spot = iota((1, BLOCK), 1).astype(F32)
    rank = jnp.where(flag == 1.0, before - 1.0, CTX + spot - before).astype(I32)
    perm = jnp.where(rank == iota((BLOCK, BLOCK), 0), 1.0, 0.0).astype(BF)
    moved = mm(perm, normed).astype(BF)
    first_ref[...] = moved[: BLOCK // 2]
    second_ref[...] = moved[BLOCK // 2 :]
    perm_ref[...] = perm


def seed_query_kernel(sin_ref, cos_ref, bsin_ref, bcos_ref, mask_ref, weight_ref, out_ref):
    half = sin_ref.shape[1]

    def one(j, carry):
        bsin = bsin_ref[pl.ds(j, 1), :]
        bcos = bcos_ref[pl.ds(j, 1), :]
        t_sin = sin_ref[...]
        t_cos = cos_ref[...]
        a = bsin * t_cos + bcos * t_sin + mask_ref[0:1, :]
        b = bcos * t_cos - bsin * t_sin + mask_ref[1:2, :]
        mean = (jnp.sum(a, -1, keepdims=True) + jnp.sum(b, -1, keepdims=True)) / (2 * half)
        a = a - mean
        b = b - mean
        var = (jnp.sum(a * a, -1, keepdims=True) + jnp.sum(b * b, -1, keepdims=True)) / (2 * half)
        inv = lax.rsqrt(var + EPSILON)
        at = pl.multiple_of(j * BLOCK, BLOCK)
        query = mm((a * inv).astype(BF), weight_ref[:half, 3 * LANES : 4 * LANES])
        query = query + mm((b * inv).astype(BF), weight_ref[half:, 3 * LANES : 4 * LANES])
        out_ref[pl.ds(at, BLOCK), :] = query.astype(BF)
        return carry

    lax.fori_loop(0, N_Z, one, 0)


def project_kernel(z_ref, *refs):
    pieces = refs[: 2 * N_Z]
    weight_ref, query_ref, kv_ref, kvs_ref, rows_ref, ctx_ref = refs[2 * N_Z :]
    for d in range(N_Z):
        for c in range(2):
            at = d * BLOCK + c * BLOCK // 2
            rows_ref[at : at + BLOCK // 2, :] = pieces[2 * d + c][...]
        ctx_ref[d * CTX : (d + 1) * CTX, :] = pieces[2 * d][:CTX, :]
    for i in range(N_Z // 2):
        at = 2 * i * BLOCK
        got = mm(rows_ref[at : at + 2 * BLOCK, :], weight_ref[:, : 3 * LANES]).astype(BF)
        kv_ref[at : at + 2 * BLOCK, :] = got[:, LANES:]
        for k in range(2):
            dest = lax.rem(z_ref[0] - (2 * i + k) + N_Z, N_Z)
            query_ref[dest] = got[k * BLOCK + CTX : (k + 1) * BLOCK, :LANES]
    kvs_ref[...] = mm(ctx_ref[...], weight_ref[:, 4 * LANES :]).astype(BF)


def softmax_rows(query, pairs):
    scores = [mm_nt(query, pair[:, :LANES]) * SCALE for pair in pairs]
    peak = functools.reduce(jnp.maximum, [jnp.max(s, axis=1, keepdims=True) for s in scores])
    total, mixed = (0.0, 0.0)
    for s, pair in zip(scores, pairs):
        raised = jnp.exp(s - peak)
        total = total + jnp.sum(raised, axis=1, keepdims=True)
        mixed = mixed + mm(raised.astype(BF), pair[:, LANES:])
    return mixed / total


def attention_kernel(
    core_ref, query_ref, kv_ref, kv_other_ref, query_s_ref, kvs_ref, kvs_other_ref, listed_ref, out_ref
):
    lane = iota((BLOCK, LANES), 1)

    def one(j, carry):
        pairs = (kv_ref[...], kv_other_ref[...])
        out_ref[j, :TGT, :] = softmax_rows(query_ref[j], pairs).astype(BF)
        at = pl.multiple_of(j * BLOCK, BLOCK)
        pairs = (kvs_ref[...], kvs_other_ref[...])
        mixed = softmax_rows(query_s_ref[pl.ds(at, BLOCK), :], pairs)
        place = (2 * j + core_ref[0]) * BLOCK + iota((BLOCK, listed_ref.shape[1]), 0)
        same = jnp.where(place == listed_ref[...], 1.0, 0.0)
        count = jnp.sum(same, axis=1, keepdims=True)
        out_ref[j, TGT:, :] = jnp.where(lane == HEAD_DIM, count, mixed).astype(BF)
        return carry

    lax.fori_loop(0, N_Z, one, 0)


def output_kernel(
    grp_ref, got_ref, perm_ref, out_ref, student_ref, keep_ref, send_ref, mixed_ref, count_ref,
    wide_ref, thin_ref, part_ref, all_count_ref,
):
    for h in range(N_Z):
        wide_ref[:, h * LANES : (h + 1) * LANES] = got_ref[h, TGT:, :]
        thin_ref[:TGT, h * HEAD_DIM : (h + 1) * HEAD_DIM] = got_ref[h, :TGT, :HEAD_DIM].astype(F32)
    chosen = mm(perm_ref[CTX:, :], wide_ref[...])
    lane = lax.rem(iota(chosen.shape, 1), LANES)
    all_count_ref[...] = jnp.broadcast_to(
        jnp.sum(jnp.where(lane == HEAD_DIM, chosen, 0.0), axis=1, keepdims=True), (TGT, LANES)
    )
    for h in range(N_Z):
        thin_ref[TGT:, h * HEAD_DIM : (h + 1) * HEAD_DIM] = chosen[
            :, h * LANES : h * LANES + HEAD_DIM
        ]
    part_ref[:TGT, :] = mm(thin_ref[:TGT, :].astype(BF), out_ref[...])
    mixed = thin_ref[TGT:, :].astype(BF)
    mixed_ref[...] = mixed
    part_ref[TGT:, :] = mm_nt(mixed, student_ref[...])
    mine = pl.multiple_of(grp_ref[0] * OWN, OWN)
    other = pl.multiple_of((1 - grp_ref[0]) * OWN, OWN)
    keep_ref[:OWN, :] = part_ref[pl.ds(mine, OWN), :].astype(BF)
    keep_ref[OWN:, :] = part_ref[pl.ds(TGT + mine, OWN), :].astype(BF)
    send_ref[:OWN, :] = part_ref[pl.ds(other, OWN), :].astype(BF)
    send_ref[OWN:, :] = part_ref[pl.ds(TGT + other, OWN), :].astype(BF)
    count_ref[...] = all_count_ref[pl.ds(mine, OWN), :]


def slope_kernel(keep_ref, got_ref, tokens_ref, seeds_ref, count_ref, out_ref, back_ref):
    both = keep_ref[...].astype(F32) + got_ref[...].astype(F32)
    wanted = normalized(tokens_ref[...] + both[:OWN])[0].astype(BF).astype(F32)
    predicted, factor = normalized(seeds_ref[...] + both[OWN:])
    slope = jnp.clip(predicted - wanted, -1.0, 1.0) * count_ref[:, :1]
    back_ref[...] = (
        slope
        - jnp.mean(slope, axis=1, keepdims=True)
        - predicted * jnp.mean(slope * predicted, axis=1, keepdims=True)
    ) * factor
    columns = STRIPE * 2 * N_Z
    row = iota((columns, 2 * LANES), 0)
    col = iota((columns, 2 * LANES), 1)
    stripe = lax.div(col, 16)
    inner = lax.rem(col, 16)
    spread = jnp.where((inner < STRIPE) & (row == stripe * STRIPE + inner), 1.0, 0.0).astype(BF)
    for d in range(N_DP):
        part = back_ref[:, d * columns : (d + 1) * columns].astype(BF)
        part = mm(part, spread).astype(BF)
        out_ref[2 * d] = part
        out_ref[2 * d + 1] = part


def finish_kernel(core_ref, mine_ref, other_ref, out_ref):
    total = jnp.zeros(out_ref.shape, F32)
    for ref, flip in ((mine_ref, 0), (other_ref, 1)):
        side = core_ref[0] * (1 - 2 * flip) + flip
        row = iota((out_ref.shape[0], 16 * N_Z), 0)
        col = iota((out_ref.shape[0], 16 * N_Z), 1)
        stripe = side * N_Z + lax.div(col, 16)
        inner = lax.rem(col, 16)
        gather = jnp.where((inner < STRIPE) & (row == stripe * STRIPE + inner), 1.0, 0.0)
        total = total + mm(gather.astype(BF), ref[...])
    out_ref[...] = total


def blend_kernel(target_ref, student_ref, out_ref):
    turned = jnp.transpose(student_ref[...].astype(F32))
    out_ref[...] = MOMENTUM * target_ref[...].astype(F32) + (1.0 - MOMENTUM) * turned


def ring(pieces):
    up = [(i, (i + 1) % N_Z) for i in range(N_Z)]
    down = [(i, (i - 1) % N_Z) for i in range(N_Z)]
    slots = [[None, None] for _ in range(N_Z)]
    slots[0] = list(pieces)
    ups, downs = list(pieces), list(pieces)
    for step in range(1, N_Z // 2 + 1):
        for c in range(2):
            if step < N_Z // 2 or c == 0:
                ups[c] = lax.ppermute(ups[c], "z", up)
                slots[step][c] = ups[c]
            if step < N_Z // 2 or c == 1:
                downs[c] = lax.ppermute(downs[c], "z", down)
                slots[N_Z - step][c] = downs[c]
    return [piece for slot in slots for piece in slot]


def body(
    clips, context, predict_index, target_qkv, target_out, student_qkv, student_out, mask_token
):
    tokens = clips[0]
    width = tokens.shape[1]
    half = width // 2
    z = lax.axis_index("z")
    core = lax.axis_index("core")
    grp = lax.axis_index("grp")
    z_at, core_at, grp_at = (v.astype(I32).reshape(1) for v in (z, core, grp))

    col = jnp.arange(target_qkv.shape[2], dtype=I32)[:, None]
    lane = jnp.arange(LANES, dtype=I32)[None, :]
    picked = ((col == z * HEAD_DIM + lane) & (lane < HEAD_DIM)).astype(BF)
    head = [mm(w[k], picked).astype(BF) for w in (target_qkv, student_qkv) for k in range(3)]
    weights = to_all(jnp.concatenate(head, axis=1), DP, N_DP).reshape(width, 6 * LANES)

    first, second, perm = call(
        sorted_norm_kernel,
        (
            sds((BLOCK // 2, width), BF),
            sds((BLOCK // 2, width), BF),
            sds((BLOCK, BLOCK), BF),
        ),
        name="sorted_norm",
    )(tokens, context)
    pieces = ring((first, second))

    spacing = jnp.exp(jnp.arange(half, dtype=F32) * (-math.log(10000.0) / half))
    spot = jnp.arange(BLOCK, dtype=F32)
    t_angle = spot[:, None] * spacing[None, :]
    base = ((2 * jnp.arange(N_Z, dtype=I32) + core) * BLOCK).astype(F32)
    b_angle = base[:, None] * spacing[None, :]
    listed = predict_index
    listed = jnp.concatenate([listed, lax.ppermute(listed, "core", SWAP)], axis=1)
    rows_own = lax.dynamic_slice_in_dim(perm, CTX + grp * OWN, OWN, axis=0)
    tokens_own = mm(rows_own, tokens)
    places_own = jnp.sum(rows_own.astype(F32) * spot[None, :], axis=1)
    places_own = places_own + ((2 * z + core) * BLOCK).astype(F32)
    angle = places_own[:, None] * spacing[None, :]
    seeds = mask_token[None, :] + jnp.concatenate([jnp.sin(angle), jnp.cos(angle)], axis=1)

    query_s = call(seed_query_kernel, sds((N_Z * BLOCK, LANES), BF), flops=4 * 10**9, name="seed_query")(
        jnp.sin(t_angle),
        jnp.cos(t_angle),
        jnp.sin(b_angle),
        jnp.cos(b_angle),
        mask_token.reshape(2, half),
        weights,
    )

    student_t, weights = lax.optimization_barrier((student_out.T, weights))
    relaid_t = to_all(student_t, DP, N_DP).reshape(width, student_out.shape[0])

    query_t, kv, kvs = call(
        project_kernel,
        (
            sds((N_Z, TGT, LANES), BF),
            sds((N_Z * BLOCK, 2 * LANES), BF),
            sds((N_Z * CTX, 2 * LANES), BF),
        ),
        scratch=(pltpu.VMEM((N_Z * BLOCK, width), BF), pltpu.VMEM((N_Z * CTX, width), BF)),
        in_specs=[SMEM] + [pl.BlockSpec()] * (2 * N_Z + 1),
        flops=2 * 10**9,
        name="project",
    )(z_at, *pieces, weights)
    kv_other = lax.ppermute(kv, "core", SWAP)
    kvs_other = lax.ppermute(kvs, "core", SWAP)
    mixed = call(
        attention_kernel,
        sds((N_Z, TGT + BLOCK, LANES), BF),
        in_specs=[SMEM] + [pl.BlockSpec()] * 7,
        flops=4 * 10**9,
        name="attention",
    )(core_at, query_t, kv, kv_other, query_s, kvs, kvs_other, listed)
    mixed = lax.all_to_all(mixed, "z", split_axis=0, concat_axis=0, tiled=True)

    keep, send, mixed_c, count = call(
        output_kernel,
        (
            sds((2 * OWN, width), BF),
            sds((2 * OWN, width), BF),
            sds((TGT, N_Z * HEAD_DIM), BF),
            sds((OWN, LANES), F32),
        ),
        scratch=(
            pltpu.VMEM((BLOCK, N_Z * LANES), BF),
            pltpu.VMEM((2 * TGT, N_Z * HEAD_DIM), F32),
            pltpu.VMEM((2 * TGT, width), F32),
            pltpu.VMEM((TGT, LANES), F32),
        ),
        in_specs=[SMEM] + [pl.BlockSpec()] * 4,
        flops=10**9,
        name="output",
    )(grp_at, mixed, perm, target_out, relaid_t)
    got = lax.ppermute(send, "grp", SWAP)
    mixed_all = to_all(mixed_c, DP, N_DP).reshape(N_DP * TGT, N_Z * HEAD_DIM)
    got, mixed_all = lax.optimization_barrier((got, mixed_all))
    stripes = call(
        slope_kernel,
        sds((2 * N_DP, OWN, 256), BF),
        scratch=(pltpu.VMEM((OWN, width), F32),),
        name="slope",
    )(keep, got, tokens_own, seeds, count)
    arrived = lax.all_to_all(stripes, (*DP, "grp"), split_axis=0, concat_axis=0, tiled=True)
    grad = lax.dot_general(
        arrived.reshape(N_DP * TGT, 256),
        mixed_all,
        (((0,), (0,)), ((), ())),
        preferred_element_type=F32,
    )
    lower, upper = (grad[: 16 * N_Z], grad[16 * N_Z :])
    grad_keep = jnp.where(core == 0, lower, upper)
    grad_send = jnp.where(core == 0, upper, lower)
    grad = grad_keep + lax.ppermute(grad_send, "core", SWAP)
    grad = grad.astype(BF).reshape(N_Z, 16, N_Z * HEAD_DIM)
    grad = lax.all_to_all(grad, "z", split_axis=0, concat_axis=0, tiled=True)
    grad = jnp.sum(grad.astype(F32), axis=0).astype(BF)
    grad = to_all(grad, "z", N_Z).reshape(16 * N_Z, N_Z * HEAD_DIM)
    other = lax.ppermute(grad, "core", SWAP)
    out_grad = call(
        finish_kernel,
        sds((student_out.shape[1], student_out.shape[0]), F32),
        in_specs=[SMEM] + [pl.BlockSpec()] * 2,
        name="finish",
    )(core_at, grad, other).T

    target_blend = pl.pallas_call(
        blend_kernel,
        grid=(width // LANES,),
        in_specs=[
            pl.BlockSpec((half, LANES), lambda i: (0, i)),
            pl.BlockSpec((LANES, half), lambda i: (i, 0)),
        ],
        out_specs=pl.BlockSpec((half, LANES), lambda i: (0, i)),
        out_shape=sds((half, width), F32),
        cost_estimate=pl.CostEstimate(flops=4 * 10**9, bytes_accessed=10**7, transcendentals=0),
        name="blend",
    )(target_out, relaid_t)
    return (out_grad, target_blend)


def solution(mesh):
    fine = Mesh(mesh.devices.reshape(8, 2, 2, 2, 4), ("z", "core", "grp", "ylo", "x"))
    seq = ("z", "core")
    in_specs = (
        P(DP, seq, None),
        P(DP, seq),
        P(DP, seq),
        P(None, DP, "grp"),
        P("grp", None),
        P(None, DP, "grp"),
        P("grp", DP),
        P(),
    )
    out_specs = (P("grp", DP), P("grp", None))
    return jax.shard_map(body, mesh=fine, in_specs=in_specs, out_specs=out_specs, check_vma=False)
```

profile of v0, /device:TPU:1, one launch (start us, length us, event | category | flops | bytes accessed | tf_op | source)
XLA Modules:
  0.0 227.6 jit_solution(8393788669769725715)
XLA Ops:
  0.6 0.0 copy-start.9
  0.7 1.3 fusion.1
  2.0 1.2 fusion.3
  3.2 1.2 fusion.5
  4.4 1.2 fusion.7
  5.7 0.3 fusion.9
  6.0 0.3 fusion.11
  6.2 1.5 broadcast_in_dim.8
  7.7 6.0 %all-to-all-start = ((bf16[8,176,768]{2,1,0:T(8,128)(2,1)}), bf16[8,176,768]{2,1,0:T(8,128)(2,1)S(1)}, u32[]{:S(2)}, u32[]{:S(2)}) async-start(bf16[8,176,768]{2,1,0:T(8,128)(2,1)} %broadcast_in_dim.8), calls=%async_computation | async-start | bytes 4325376 | tf_op jit(solution)/shard_map/all_to_all | solution.py:60
  13.7 2.3 sorted_norm.1
  16.0 5.6 %collective-permute-start.7 = (bf16[64,1408]{1,0:T(8,128)(2,1)}, bf16[64,1408]{1,0:T(8,128)(2,1)S(1)}, u32[]{:S(2)}, u32[]{:S(2)}) collective-permute-start(bf16[64,1408]{1,0:T(8,128)(2,1)} %get-tuple-element.17.refs_1_), channel_id=1, source_target_pairs={{0,224},{32,0},{64,32},{96,64},{128,96},{160,128},{192,160},{224,1... | collective-permute-start | bytes 540680 | tf_op jit(solution)/shard_map/ppermute | solution.py:238
  21.5 2.7 %collective-permute-start.11 = (bf16[64,1408]{1,0:T(8,128)(2,1)}, bf16[64,1408]{1,0:T(8,128)(2,1)S(1)}, u32[]{:S(2)}, u32[]{:S(2)}) collective-permute-start(bf16[64,1408]{1,0:T(8,128)(2,1)} %get-tuple-element.16.refs_0_), channel_id=1, source_target_pairs={{0,224},{32,0},{64,32},{96,64},{128,96},{160,128},{192,160},{224,1... | collective-permute-start | bytes 540680 | tf_op jit(solution)/shard_map/ppermute | solution.py:238
  24.2 0.6 collective-permute-done.7.refs_15_
  24.8 3.3 %collective-permute-start.8 = (bf16[64,1408]{1,0:T(8,128)(2,1)S(1)}, bf16[64,1408]{1,0:T(8,128)(2,1)S(1)}, u32[]{:S(2)}, u32[]{:S(2)}) collective-permute-start(bf16[64,1408]{1,0:T(8,128)(2,1)S(1)} %collective-permute-done.7.refs_15_), channel_id=1, source_target_pairs={{0,224},{32,0},{64,32},{96,64},{128,96},{160,128},{192,160},{224,1... | collective-permute-start | bytes 540680 | tf_op jit(solution)/shard_map/ppermute | solution.py:238
  28.1 3.4 %collective-permute-start.16 = (s32[1,192]{1,0:T(1,128)S(1)}, s32[1,192]{1,0:T(1,128)S(1)}, u32[]{:S(2)}, u32[]{:S(2)}) collective-permute-start(s32[1,192]{1,0:T(1,128)S(1)} %copy-done.8), channel_id=1, source_target_pairs={{0,16},{16,0},{1,17},{17,1},{2,18},{18,2},{3,19},{19,3},{4,20},{20... | collective-permute-start | bytes 2312 | tf_op jit(solution)/shard_map/ppermute | solution.py:277
  31.5 2.9 %collective-permute-start.12 = (bf16[64,1408]{1,0:T(8,128)(2,1)S(1)}, bf16[64,1408]{1,0:T(8,128)(2,1)S(1)}, u32[]{:S(2)}, u32[]{:S(2)}) collective-permute-start(bf16[64,1408]{1,0:T(8,128)(2,1)S(1)} %collective-permute-done.11.refs_14_), channel_id=1, source_target_pairs={{0,224},{32,0},{64,32},{96,64},{128,96},{160,128},{192,160},{224,1... | collective-permute-start | bytes 540680 | tf_op jit(solution)/shard_map/ppermute | solution.py:238
  34.4 2.7 %collective-permute-start.9 = (bf16[64,1408]{1,0:T(8,128)(2,1)S(1)}, bf16[64,1408]{1,0:T(8,128)(2,1)}, u32[]{:S(2)}, u32[]{:S(2)}) collective-permute-start(bf16[64,1408]{1,0:T(8,128)(2,1)S(1)} %collective-permute-done.8.refs_13_), channel_id=1, source_target_pairs={{0,224},{32,0},{64,32},{96,64},{128,96},{160,128},{192,160},{224,1... | collective-permute-start | bytes 540680 | tf_op jit(solution)/shard_map/ppermute | solution.py:238
  37.1 0.6 collective-permute-done.12.refs_12_
  37.7 3.4 %collective-permute-start.13 = (bf16[64,1408]{1,0:T(8,128)(2,1)S(1)}, bf16[64,1408]{1,0:T(8,128)(2,1)}, u32[]{:S(2)}, u32[]{:S(2)}) collective-permute-start(bf16[64,1408]{1,0:T(8,128)(2,1)S(1)} %collective-permute-done.12.refs_12_), channel_id=1, source_target_pairs={{0,224},{32,0},{64,32},{96,64},{128,96},{160,128},{192,160},{224,1... | collective-permute-start | bytes 540680 | tf_op jit(solution)/shard_map/ppermute | solution.py:238
  41.1 0.4 collective-permute-done.9.refs_11_
  41.5 3.5 %collective-permute-start.10 = (bf16[64,1408]{1,0:T(8,128)(2,1)}, bf16[64,1408]{1,0:T(8,128)(2,1)}, u32[]{:S(2)}, u32[]{:S(2)}) collective-permute-start(bf16[64,1408]{1,0:T(8,128)(2,1)} %collective-permute-done.9.refs_11_), channel_id=1, source_target_pairs={{0,224},{32,0},{64,32},{96,64},{128,96},{160,128},{192,160},{224,1... | collective-permute-start | bytes 540680 | tf_op jit(solution)/shard_map/ppermute | solution.py:238
  45.0 2.3 fusion.12
  47.3 0.4 collective-permute-done.5.refs_7_
  47.7 0.8 collective-permute-done.10.refs_9_
  48.5 3.6 %collective-permute-done.6.refs_8_ = bf16[64,1408]{1,0:T(8,128)(2,1)} collective-permute-done((bf16[64,1408]{1,0:T(8,128)(2,1)}, bf16[64,1408]{1,0:T(8,128)(2,1)}, u32[]{:S(2)}, u32[]{:S(2)}) %collective-permute-start.6) | collective-permute-done | bytes 180256 | tf_op jit(solution)/shard_map/ppermute | solution.py:235
  52.2 5.4 %project.1 = (bf16[8,96,128]{2,1,0:T(8,128)(2,1)}, bf16[1024,256]{1,0:T(8,128)(2,1)}, bf16[256,256]{1,0:T(8,128)(2,1)}) custom-call(s32[1]{0:T(128)} %bitcast.2.z_ref, bf16[64,1408]{1,0:T(8,128)(2,1)} %get-tuple-element.16.refs_0_, bf16[64,1408]{1,0:T(8,128)(2,1)} %get-tuple-element.17.refs_1_, bf16[64,1408]{1,0:T(8,128)(2,1)} %copy-done.13, ...), custom_call_target="tpu_custom_call" | custom-call | flops 2000000000 | bytes 1000000 | tf_op jit(solution)/shard_map/project/pallas_call | solution.py:297
  57.6 2.7 %collective-permute-start.14 = (bf16[1024,256]{1,0:T(8,128)(2,1)}, bf16[1024,256]{1,0:T(8,128)(2,1)S(1)}, u32[]{:S(2)}, u32[]{:S(2)}) collective-permute-start(bf16[1024,256]{1,0:T(8,128)(2,1)} %get-tuple-element.20.kv_ref), channel_id=1, source_target_pairs={{0,16},{16,0},{1,17},{17,1},{2,18},{18,2},{3,19},{19,3},{4,20},{20... | collective-permute-start | bytes 1572872 | tf_op jit(solution)/shard_map/ppermute | solution.py:309
  60.3 0.8 multiply_cosine_fusion.1
  61.1 0.7 reshape.68.mask_ref
  61.7 0.7 pad_add_fusion.listed_ref
  62.4 0.0 collective-permute-start.15
  62.4 7.0 %seed_query.1.query_s_ref = bf16[1024,128]{1,0:T(8,128)(2,1)} custom-call(f32[128,704]{1,0:T(8,128)} %get-tuple-element.35.sin_ref, f32[128,704]{1,0:T(8,128)} %get-tuple-element.34.cos_ref, f32[8,704]{1,0:T(8,128)} %get-tuple-element.33.bsin_ref, f32[8,704]{1,0:T(8,128)} %get-tuple-element.32.bcos_ref, f32[2,704]{1,0:T(2,128)} %reshape.68.mask_ref, ...), custom_call_target="tpu_custom_call" | custom-call | flops 4000000000 | bytes 1000000 | tf_op jit(solution)/shard_map/seed_query/pallas_call | solution.py:285
  69.4 0.6 copy-done.19
  70.0 0.2 copy-done.10
  70.2 9.5 %attention.1 = bf16[8,224,128]{2,1,0:T(8,128)(2,1)} custom-call(s32[1]{0:T(128)} %bitcast.core_ref, bf16[8,96,128]{2,1,0:T(8,128)(2,1)} %get-tuple-element.19.query_ref, bf16[1024,256]{1,0:T(8,128)(2,1)} %get-tuple-element.20.kv_ref, bf16[1024,256]{1,0:T(8,128)(2,1)} %copy-done.10, bf16[1024,128]{1,0:T(8,128)(2,1)} %seed_query.1.query_s_ref, ...), custom_call_target="tpu_custom_call" | custom-call | flops 4000000000 | bytes 1000000 | tf_op jit(solution)/shard_map/attention/pallas_call | solution.py:311
  79.7 20.2 %all_to_all.35.got_ref = bf16[8,224,128]{2,1,0:T(8,128)(2,1)} all-to-all(bf16[8,224,128]{2,1,0:T(8,128)(2,1)} %attention.1), channel_id=1, replica_groups=mesh['z'=8,'core'=2,'grp'=2,'ylo'=2,'x'=4] {'z'}, dimensions={0} | all-to-all | bytes 917504 | tf_op jit(solution)/shard_map/all_to_all | solution.py:318
  99.9 1.5 broadcast_in_dim.9
  101.4 5.1 %all-to-all-start.2 = ((bf16[8,176,704]{2,1,0:T(8,128)(2,1)}), bf16[8,176,704]{2,1,0:T(8,128)(2,1)S(1)}, u32[]{:S(2)}, u32[]{:S(2)}) async-start(bf16[8,176,704]{2,1,0:T(8,128)(2,1)} %broadcast_in_dim.9), calls=%async_computation.2 | async-start | bytes 4325376 | tf_op jit(solution)/shard_map/all_to_all | solution.py:60
  106.6 0.8 multiply_reduce_fusion
  107.4 27.0 %all-to-all-done.2 = bf16[8,176,704]{2,1,0:T(8,128)(2,1)S(1)} async-done(((bf16[8,176,704]{2,1,0:T(8,128)(2,1)}), bf16[8,176,704]{2,1,0:T(8,128)(2,1)S(1)}, u32[]{:S(2)}, u32[]{:S(2)}) %all-to-all-start.2) | async-done | bytes 1982496 | tf_op jit(solution)/shard_map/all_to_all | solution.py:60
  134.4 1.4 copy-done
  135.7 4.4 %output.1 = (bf16[96,1408]{1,0:T(8,128)(2,1)}, bf16[96,1408]{1,0:T(8,128)(2,1)}, bf16[96,704]{1,0:T(8,128)(2,1)}, f32[48,128]{1,0:T(8,128)}) custom-call(s32[1]{0:T(128)} %bitcast.1.grp_ref, bf16[8,224,128]{2,1,0:T(8,128)(2,1)} %all_to_all.35.got_ref, bf16[128,128]{1,0:T(8,128)(2,1)} %get-tuple-element.22.perm_ref, bf16[704,1408]{1,0:T(8,128)(2,1)} %target_ref.1, ...), custom_call_target="tpu_custom_call" | custom-call | flops 1000000000 | bytes 1000000 | tf_op jit(solution)/shard_map/output/pallas_call | solution.py:320
  140.1 2.1 broadcast_in_dim.10
  142.2 4.0 %all-to-all-start.3 = ((bf16[8,96,704]{2,1,0:T(8,128)(2,1)}), bf16[8,96,704]{2,1,0:T(8,128)(2,1)S(1)}, u32[]{:S(2)}, u32[]{:S(2)}) async-start(bf16[8,96,704]{2,1,0:T(8,128)(2,1)} %broadcast_in_dim.10), calls=%async_computation.3 | async-start | bytes 2359296 | tf_op jit(solution)/shard_map/all_to_all | solution.py:60
  146.2 0.6 multiply_sine_fusion
  146.8 2.7 %collective-permute-start.17 = (bf16[96,1408]{1,0:T(8,128)(2,1)S(1)}, bf16[96,1408]{1,0:T(8,128)(2,1)S(1)}, u32[]{:S(2)}, u32[]{:S(2)}) collective-permute-start(bf16[96,1408]{1,0:T(8,128)(2,1)S(1)} %copy-done.11), channel_id=1, source_target_pairs={{0,8},{8,0},{1,9},{9,1},{2,10},{10,2},{3,11},{11,3},{4,12},{12,4},... | collective-permute-start | bytes 811016 | tf_op jit(solution)/shard_map/ppermute | solution.py:338
  149.5 0.8 maximum_add_fusion.seeds_ref
  150.3 1.6 fusion.45.tokens_ref
  151.9 14.2 %collective-permute-done.17.got_ref = bf16[96,1408]{1,0:T(8,128)(2,1)S(1)} collective-permute-done((bf16[96,1408]{1,0:T(8,128)(2,1)S(1)}, bf16[96,1408]{1,0:T(8,128)(2,1)S(1)}, u32[]{:S(2)}, u32[]{:S(2)}) %collective-permute-start.17) | collective-permute-done | bytes 270368 | tf_op jit(solution)/shard_map/ppermute | solution.py:338
  166.2 0.7 copy-done.5
  166.9 2.6 %slope.1 = bf16[16,48,256]{2,1,0:T(8,128)(2,1)} custom-call(bf16[96,1408]{1,0:T(8,128)(2,1)} %get-tuple-element.24.keep_ref, bf16[96,1408]{1,0:T(8,128)(2,1)} %copy-done.5, f32[48,1408]{1,0:T(8,128)} %fusion.45.tokens_ref, f32[48,1408]{1,0:T(8,128)} %maximum_add_fusion.seeds_ref, f32[48,128]{1,0:T(8,128)} %get-tuple-element.28.count_ref), custom_call_target="tpu_custom_call" | custom-call | flops 100000000 | bytes 1000000 | tf_op jit(solution)/shard_map/slope/pallas_call | solution.py:341
  169.5 7.1 %all-to-all-start.4 = ((bf16[16,48,256]{2,1,0:T(8,128)(2,1)}), bf16[16,48,256]{2,1,0:T(8,128)(2,1)S(1)}, u32[]{:S(2)}, u32[]{:S(2)}) async-start(bf16[16,48,256]{2,1,0:T(8,128)(2,1)} %slope.1), calls=%async_computation.4 | async-start | bytes 786432 | tf_op jit(solution)/shard_map/all_to_all | solution.py:347
  176.6 8.5 %all-to-all-done.4 = bf16[16,48,256]{2,1,0:T(8,128)(2,1)S(1)} async-done(((bf16[16,48,256]{2,1,0:T(8,128)(2,1)}), bf16[16,48,256]{2,1,0:T(8,128)(2,1)S(1)}, u32[]{:S(2)}, u32[]{:S(2)}) %all-to-all-start.4) | async-done | bytes 393248 | tf_op jit(solution)/shard_map/all_to_all | solution.py:347
  185.1 0.6 fusion.49
  185.7 2.6 %collective-permute-start.18 = (f32[128,704]{0,1:T(8,128)S(1)}, f32[128,704]{0,1:T(8,128)S(1)}, u32[]{:S(2)}, u32[]{:S(2)}) collective-permute-start(f32[128,704]{0,1:T(8,128)S(1)} %slice_select_fusion), channel_id=1, source_target_pairs={{0,16},{16,0},{1,17},{17,1},{2,18},{18,2},{3,19},{19,3},{4,20},{20... | collective-permute-start | bytes 1081352 | tf_op jit(solution)/shard_map/ppermute | solution.py:357
  188.3 1.3 collective-permute-done.18
  189.6 0.1 add_convert_fusion
  189.7 0.1 copy.10
  189.9 12.4 %all_to_all.36 = bf16[8,16,704]{2,1,0:T(8,128)(2,1)S(1)} all-to-all(bf16[8,16,704]{2,1,0:T(8,128)(2,1)S(1)} %bitcast.64), channel_id=1, replica_groups=mesh['z'=8,'core'=2,'grp'=2,'ylo'=2,'x'=4] {'z'}, dimensions={0} | all-to-all | bytes 360448 | tf_op jit(solution)/shard_map/all_to_all | solution.py:359
  202.3 10.8 %all_to_all.37 = bf16[8,16,704]{2,1,0:T(8,128)(2,1)S(1)} all-to-all(bf16[8,16,704]{2,1,0:T(8,128)(2,1)S(1)} %broadcast_in_dim.11), channel_id=1, replica_groups=mesh['z'=8,'core'=2,'grp'=2,'ylo'=2,'x'=4] {'z'}, dimensions={0} | all-to-all | bytes 360448 | tf_op jit(solution)/shard_map/all_to_all | solution.py:60
  213.1 3.1 %collective-permute-start.19 = (bf16[128,704]{1,0:T(8,128)(2,1)S(1)}, bf16[128,704]{1,0:T(8,128)(2,1)S(1)}, u32[]{:S(2)}, u32[]{:S(2)}) collective-permute-start(bf16[128,704]{1,0:T(8,128)(2,1)S(1)} %bitcast.65), channel_id=1, source_target_pairs={{0,16},{16,0},{1,17},{17,1},{2,18},{18,2},{3,19},{19,3},{4,20},{20... | collective-permute-start | bytes 540680 | tf_op jit(solution)/shard_map/ppermute | solution.py:362
  216.2 8.6 %blend.1 = f32[704,1408]{1,0:T(8,128)} custom-call(bf16[704,1408]{1,0:T(8,128)(2,1)} %target_ref.1, bf16[1408,704]{1,0:T(8,128)(2,1)} %bitcast.59), custom_call_target="tpu_custom_call" | custom-call | flops 4000000000 | bytes 10000000 | tf_op jit(solution)/shard_map/blend/pallas_call | solution.py:370
  224.9 0.7 copy-done.6
  225.5 2.1 finish.1
  (63 shorter events, 0.2 us)
Async XLA Ops:
  0.6 5.0 %copy-start.9 = (bf16[3,176,704]{2,1,0:T(8,128)(2,1)S(1)}, bf16[3,176,704]{2,1,0:T(8,128)(2,1)}, u32[]{:S(2)}) copy-start(bf16[3,176,704]{2,1,0:T(8,128)(2,1)} %param.13) | copy-start | bytes 2230276
  7.7 20.4 %copy-start.8 = (s32[1,192]{1,0:T(1,128)S(1)}, s32[1,192]{1,0:T(1,128)}, u32[]{:S(2)}) copy-start(s32[1,192]{1,0:T(1,128)} %param.10) | copy-start | bytes 2308
  7.7 39.6 %all-to-all-start = ((bf16[8,176,768]{2,1,0:T(8,128)(2,1)}), bf16[8,176,768]{2,1,0:T(8,128)(2,1)S(1)}, u32[]{:S(2)}, u32[]{:S(2)}) async-start(bf16[8,176,768]{2,1,0:T(8,128)(2,1)} %broadcast_in_dim.8), calls=%async_computation | async-start | bytes 4325376 | tf_op jit(solution)/shard_map/all_to_all | solution.py:60
  16.0 8.8 %collective-permute-start.7 = (bf16[64,1408]{1,0:T(8,128)(2,1)}, bf16[64,1408]{1,0:T(8,128)(2,1)S(1)}, u32[]{:S(2)}, u32[]{:S(2)}) collective-permute-start(bf16[64,1408]{1,0:T(8,128)(2,1)} %get-tuple-element.17.refs_1_), channel_id=1, source_target_pairs={{0,224},{32,0},{64,32},{96,64},{128,96},{160,128},{192,160},{224,1... | collective-permute-start | bytes 540680 | tf_op jit(solution)/shard_map/ppermute | solution.py:238
  21.5 6.6 %collective-permute-start = (bf16[64,1408]{1,0:T(8,128)(2,1)}, bf16[64,1408]{1,0:T(8,128)(2,1)S(1)}, u32[]{:S(2)}, u32[]{:S(2)}) collective-permute-start(bf16[64,1408]{1,0:T(8,128)(2,1)} %get-tuple-element.16.refs_0_), channel_id=1, source_target_pairs={{0,32},{32,64},{64,96},{96,128},{128,160},{160,192},{192,224},{224... | collective-permute-start | bytes 540680 | tf_op jit(solution)/shard_map/ppermute | solution.py:235
  21.5 10.0 %collective-permute-start.11 = (bf16[64,1408]{1,0:T(8,128)(2,1)}, bf16[64,1408]{1,0:T(8,128)(2,1)S(1)}, u32[]{:S(2)}, u32[]{:S(2)}) collective-permute-start(bf16[64,1408]{1,0:T(8,128)(2,1)} %get-tuple-element.16.refs_0_), channel_id=1, source_target_pairs={{0,224},{32,0},{64,32},{96,64},{128,96},{160,128},{192,160},{224,1... | collective-permute-start | bytes 540680 | tf_op jit(solution)/shard_map/ppermute | solution.py:238
  24.2 10.1 %collective-permute-start.1 = (bf16[64,1408]{1,0:T(8,128)(2,1)}, bf16[64,1408]{1,0:T(8,128)(2,1)S(1)}, u32[]{:S(2)}, u32[]{:S(2)}) collective-permute-start(bf16[64,1408]{1,0:T(8,128)(2,1)} %get-tuple-element.17.refs_1_), channel_id=1, source_target_pairs={{0,32},{32,64},{64,96},{96,128},{128,160},{160,192},{192,224},{224... | collective-permute-start | bytes 540680 | tf_op jit(solution)/shard_map/ppermute | solution.py:235
  24.8 27.4 %copy-start.12 = (bf16[64,1408]{1,0:T(8,128)(2,1)}, bf16[64,1408]{1,0:T(8,128)(2,1)S(1)}, u32[]{:S(2)}) copy-start(bf16[64,1408]{1,0:T(8,128)(2,1)S(1)} %collective-permute-done.7.refs_15_) | copy-start | bytes 540676
  24.8 9.6 %collective-permute-start.8 = (bf16[64,1408]{1,0:T(8,128)(2,1)S(1)}, bf16[64,1408]{1,0:T(8,128)(2,1)S(1)}, u32[]{:S(2)}, u32[]{:S(2)}) collective-permute-start(bf16[64,1408]{1,0:T(8,128)(2,1)S(1)} %collective-permute-done.7.refs_15_), channel_id=1, source_target_pairs={{0,224},{32,0},{64,32},{96,64},{128,96},{160,128},{192,160},{224,1... | collective-permute-start | bytes 540680 | tf_op jit(solution)/shard_map/ppermute | solution.py:238
  28.1 24.0 %copy-start.13 = (bf16[64,1408]{1,0:T(8,128)(2,1)}, bf16[64,1408]{1,0:T(8,128)(2,1)S(1)}, u32[]{:S(2)}) copy-start(bf16[64,1408]{1,0:T(8,128)(2,1)S(1)} %collective-permute-done.refs_2_) | copy-start | bytes 540676
  28.1 8.9 %collective-permute-start.2 = (bf16[64,1408]{1,0:T(8,128)(2,1)S(1)}, bf16[64,1408]{1,0:T(8,128)(2,1)S(1)}, u32[]{:S(2)}, u32[]{:S(2)}) collective-permute-start(bf16[64,1408]{1,0:T(8,128)(2,1)S(1)} %collective-permute-done.refs_2_), channel_id=1, source_target_pairs={{0,32},{32,64},{64,96},{96,128},{128,160},{160,192},{192,224},{224... | collective-permute-start | bytes 540680 | tf_op jit(solution)/shard_map/ppermute | solution.py:235
  28.1 33.6 %collective-permute-start.16 = (s32[1,192]{1,0:T(1,128)S(1)}, s32[1,192]{1,0:T(1,128)S(1)}, u32[]{:S(2)}, u32[]{:S(2)}) collective-permute-start(s32[1,192]{1,0:T(1,128)S(1)} %copy-done.8), channel_id=1, source_target_pairs={{0,16},{16,0},{1,17},{17,1},{2,18},{18,2},{3,19},{19,3},{4,20},{20... | collective-permute-start | bytes 2312 | tf_op jit(solution)/shard_map/ppermute | solution.py:277
  31.5 20.7 %copy-start.14 = (bf16[64,1408]{1,0:T(8,128)(2,1)}, bf16[64,1408]{1,0:T(8,128)(2,1)S(1)}, u32[]{:S(2)}) copy-start(bf16[64,1408]{1,0:T(8,128)(2,1)S(1)} %collective-permute-done.11.refs_14_) | copy-start | bytes 540676
  31.5 6.2 %collective-permute-start.12 = (bf16[64,1408]{1,0:T(8,128)(2,1)S(1)}, bf16[64,1408]{1,0:T(8,128)(2,1)S(1)}, u32[]{:S(2)}, u32[]{:S(2)}) collective-permute-start(bf16[64,1408]{1,0:T(8,128)(2,1)S(1)} %collective-permute-done.11.refs_14_), channel_id=1, source_target_pairs={{0,224},{32,0},{64,32},{96,64},{128,96},{160,128},{192,160},{224,1... | collective-permute-start | bytes 540680 | tf_op jit(solution)/shard_map/ppermute | solution.py:238
  34.4 17.8 %copy-start.15 = (bf16[64,1408]{1,0:T(8,128)(2,1)}, bf16[64,1408]{1,0:T(8,128)(2,1)S(1)}, u32[]{:S(2)}) copy-start(bf16[64,1408]{1,0:T(8,128)(2,1)S(1)} %collective-permute-done.1.refs_3_) | copy-start | bytes 540676
  34.4 6.7 %collective-permute-start.3 = (bf16[64,1408]{1,0:T(8,128)(2,1)S(1)}, bf16[64,1408]{1,0:T(8,128)(2,1)}, u32[]{:S(2)}, u32[]{:S(2)}) collective-permute-start(bf16[64,1408]{1,0:T(8,128)(2,1)S(1)} %collective-permute-done.1.refs_3_), channel_id=1, source_target_pairs={{0,32},{32,64},{64,96},{96,128},{128,160},{160,192},{192,224},{224... | collective-permute-start | bytes 540680 | tf_op jit(solution)/shard_map/ppermute | solution.py:235
  34.4 17.8 %copy-start.16 = (bf16[64,1408]{1,0:T(8,128)(2,1)}, bf16[64,1408]{1,0:T(8,128)(2,1)S(1)}, u32[]{:S(2)}) copy-start(bf16[64,1408]{1,0:T(8,128)(2,1)S(1)} %collective-permute-done.8.refs_13_) | copy-start | bytes 540676
  34.4 7.1 %collective-permute-start.9 = (bf16[64,1408]{1,0:T(8,128)(2,1)S(1)}, bf16[64,1408]{1,0:T(8,128)(2,1)}, u32[]{:S(2)}, u32[]{:S(2)}) collective-permute-start(bf16[64,1408]{1,0:T(8,128)(2,1)S(1)} %collective-permute-done.8.refs_13_), channel_id=1, source_target_pairs={{0,224},{32,0},{64,32},{96,64},{128,96},{160,128},{192,160},{224,1... | collective-permute-start | bytes 540680 | tf_op jit(solution)/shard_map/ppermute | solution.py:238
  37.0 15.1 %copy-start.17 = (bf16[64,1408]{1,0:T(8,128)(2,1)}, bf16[64,1408]{1,0:T(8,128)(2,1)S(1)}, u32[]{:S(2)}) copy-start(bf16[64,1408]{1,0:T(8,128)(2,1)S(1)} %collective-permute-done.2.refs_4_) | copy-start | bytes 540676
  37.0 8.0 %collective-permute-start.4 = (bf16[64,1408]{1,0:T(8,128)(2,1)S(1)}, bf16[64,1408]{1,0:T(8,128)(2,1)}, u32[]{:S(2)}, u32[]{:S(2)}) collective-permute-start(bf16[64,1408]{1,0:T(8,128)(2,1)S(1)} %collective-permute-done.2.refs_4_), channel_id=1, source_target_pairs={{0,32},{32,64},{64,96},{96,128},{128,160},{160,192},{192,224},{224... | collective-permute-start | bytes 540680 | tf_op jit(solution)/shard_map/ppermute | solution.py:235
  37.7 14.5 %copy-start.18 = (bf16[64,1408]{1,0:T(8,128)(2,1)}, bf16[64,1408]{1,0:T(8,128)(2,1)S(1)}, u32[]{:S(2)}) copy-start(bf16[64,1408]{1,0:T(8,128)(2,1)S(1)} %collective-permute-done.12.refs_12_) | copy-start | bytes 540676
  37.7 9.6 %collective-permute-start.13 = (bf16[64,1408]{1,0:T(8,128)(2,1)S(1)}, bf16[64,1408]{1,0:T(8,128)(2,1)}, u32[]{:S(2)}, u32[]{:S(2)}) collective-permute-start(bf16[64,1408]{1,0:T(8,128)(2,1)S(1)} %collective-permute-done.12.refs_12_), channel_id=1, source_target_pairs={{0,224},{32,0},{64,32},{96,64},{128,96},{160,128},{192,160},{224,1... | collective-permute-start | bytes 540680 | tf_op jit(solution)/shard_map/ppermute | solution.py:238
  41.1 6.7 %collective-permute-start.5 = (bf16[64,1408]{1,0:T(8,128)(2,1)}, bf16[64,1408]{1,0:T(8,128)(2,1)}, u32[]{:S(2)}, u32[]{:S(2)}) collective-permute-start(bf16[64,1408]{1,0:T(8,128)(2,1)} %collective-permute-done.3.refs_5_), channel_id=1, source_target_pairs={{0,32},{32,64},{64,96},{96,128},{128,160},{160,192},{192,224},{224... | collective-permute-start | bytes 540680 | tf_op jit(solution)/shard_map/ppermute | solution.py:235
  41.5 7.0 %collective-permute-start.10 = (bf16[64,1408]{1,0:T(8,128)(2,1)}, bf16[64,1408]{1,0:T(8,128)(2,1)}, u32[]{:S(2)}, u32[]{:S(2)}) collective-permute-start(bf16[64,1408]{1,0:T(8,128)(2,1)} %collective-permute-done.9.refs_11_), channel_id=1, source_target_pairs={{0,224},{32,0},{64,32},{96,64},{128,96},{160,128},{192,160},{224,1... | collective-permute-start | bytes 540680 | tf_op jit(solution)/shard_map/ppermute | solution.py:238
  45.0 7.1 %collective-permute-start.6 = (bf16[64,1408]{1,0:T(8,128)(2,1)}, bf16[64,1408]{1,0:T(8,128)(2,1)}, u32[]{:S(2)}, u32[]{:S(2)}) collective-permute-start(bf16[64,1408]{1,0:T(8,128)(2,1)} %collective-permute-done.4.refs_6_), channel_id=1, source_target_pairs={{0,32},{32,64},{64,96},{96,128},{128,160},{160,192},{192,224},{224... | collective-permute-start | bytes 540680 | tf_op jit(solution)/shard_map/ppermute | solution.py:235
  47.3 4.9 %copy-start.1 = (bf16[8,176,768]{2,1,0:T(8,128)(2,1)}, bf16[8,176,768]{2,1,0:T(8,128)(2,1)S(1)}, u32[]{:S(2)}) copy-start(bf16[8,176,768]{2,1,0:T(8,128)(2,1)S(1)} %all-to-all-done) | copy-start | bytes 6488068
  52.2 8.9 %copy-start.7 = (f32[1408]{0:T(1024)S(1)}, f32[1408]{0:T(1024)}, u32[]{:S(2)}) copy-start(f32[1408]{0:T(1024)} %param.15) | copy-start | bytes 16900
  57.6 11.8 %collective-permute-start.14 = (bf16[1024,256]{1,0:T(8,128)(2,1)}, bf16[1024,256]{1,0:T(8,128)(2,1)S(1)}, u32[]{:S(2)}, u32[]{:S(2)}) collective-permute-start(bf16[1024,256]{1,0:T(8,128)(2,1)} %get-tuple-element.20.kv_ref), channel_id=1, source_target_pairs={{0,16},{16,0},{1,17},{17,1},{2,18},{18,2},{3,19},{19,3},{4,20},{20... | collective-permute-start | bytes 1572872 | tf_op jit(solution)/shard_map/ppermute | solution.py:309
  62.4 7.0 %collective-permute-start.15 = (bf16[256,256]{1,0:T(8,128)(2,1)}, bf16[256,256]{1,0:T(8,128)(2,1)S(1)}, u32[]{:S(2)}, u32[]{:S(2)}) collective-permute-start(bf16[256,256]{1,0:T(8,128)(2,1)} %get-tuple-element.21.kvs_ref), channel_id=1, source_target_pairs={{0,16},{16,0},{1,17},{17,1},{2,18},{18,2},{3,19},{19,3},{4,20},{20... | collective-permute-start | bytes 393224 | tf_op jit(solution)/shard_map/ppermute | solution.py:310
  69.4 0.7 copy-start.19
  69.4 0.8 copy-start.10
  70.2 29.7 %copy-start.4 = (bf16[704,176]{0,1:T(8,128)(2,1)S(1)}, bf16[704,176]{0,1:T(8,128)(2,1)}, u32[]{:S(2)}) copy-start(bf16[704,176]{0,1:T(8,128)(2,1)} %param.14) | copy-start | bytes 743428
  101.4 32.9 %all-to-all-start.2 = ((bf16[8,176,704]{2,1,0:T(8,128)(2,1)}), bf16[8,176,704]{2,1,0:T(8,128)(2,1)S(1)}, u32[]{:S(2)}, u32[]{:S(2)}) async-start(bf16[8,176,704]{2,1,0:T(8,128)(2,1)} %broadcast_in_dim.9), calls=%async_computation.2 | async-start | bytes 4325376 | tf_op jit(solution)/shard_map/all_to_all | solution.py:60
  134.4 1.4 copy-start
  140.1 6.7 %copy-start.11 = (bf16[96,1408]{1,0:T(8,128)(2,1)S(1)}, bf16[96,1408]{1,0:T(8,128)(2,1)}, u32[]{:S(2)}) copy-start(bf16[96,1408]{1,0:T(8,128)(2,1)} %get-tuple-element.25) | copy-start | bytes 811012
  140.1 10.2 %copy-start.3 = (bf16[1,128,1408]{2,1,0:T(8,128)(2,1)S(1)}, bf16[1,128,1408]{2,1,0:T(8,128)(2,1)}, u32[]{:S(2)}) copy-start(bf16[1,128,1408]{2,1,0:T(8,128)(2,1)} %param.8) | copy-start | bytes 1081348
  142.2 23.9 %all-to-all-start.3 = ((bf16[8,96,704]{2,1,0:T(8,128)(2,1)}), bf16[8,96,704]{2,1,0:T(8,128)(2,1)S(1)}, u32[]{:S(2)}, u32[]{:S(2)}) async-start(bf16[8,96,704]{2,1,0:T(8,128)(2,1)} %broadcast_in_dim.10), calls=%async_computation.3 | async-start | bytes 2359296 | tf_op jit(solution)/shard_map/all_to_all | solution.py:60
  146.8 19.3 %collective-permute-start.17 = (bf16[96,1408]{1,0:T(8,128)(2,1)S(1)}, bf16[96,1408]{1,0:T(8,128)(2,1)S(1)}, u32[]{:S(2)}, u32[]{:S(2)}) collective-permute-start(bf16[96,1408]{1,0:T(8,128)(2,1)S(1)} %copy-done.11), channel_id=1, source_target_pairs={{0,8},{8,0},{1,9},{9,1},{2,10},{10,2},{3,11},{11,3},{4,12},{12,4},... | collective-permute-start | bytes 811016 | tf_op jit(solution)/shard_map/ppermute | solution.py:338
  166.2 0.7 copy-start.5
  169.5 15.6 %all-to-all-start.4 = ((bf16[16,48,256]{2,1,0:T(8,128)(2,1)}), bf16[16,48,256]{2,1,0:T(8,128)(2,1)S(1)}, u32[]{:S(2)}, u32[]{:S(2)}) async-start(bf16[16,48,256]{2,1,0:T(8,128)(2,1)} %slope.1), calls=%async_computation.4 | async-start | bytes 786432 | tf_op jit(solution)/shard_map/all_to_all | solution.py:347
  185.7 3.9 %collective-permute-start.18 = (f32[128,704]{0,1:T(8,128)S(1)}, f32[128,704]{0,1:T(8,128)S(1)}, u32[]{:S(2)}, u32[]{:S(2)}) collective-permute-start(f32[128,704]{0,1:T(8,128)S(1)} %slice_select_fusion), channel_id=1, source_target_pairs={{0,16},{16,0},{1,17},{17,1},{2,18},{18,2},{3,19},{19,3},{4,20},{20... | collective-permute-start | bytes 1081352 | tf_op jit(solution)/shard_map/ppermute | solution.py:357
  213.1 11.7 %copy-start.2 = (bf16[8,16,704]{2,1,0:T(8,128)(2,1)}, bf16[8,16,704]{2,1,0:T(8,128)(2,1)S(1)}, u32[]{:S(2)}) copy-start(bf16[8,16,704]{2,1,0:T(8,128)(2,1)S(1)} %all_to_all.37) | copy-start | bytes 540676
  213.1 11.7 %collective-permute-start.19 = (bf16[128,704]{1,0:T(8,128)(2,1)S(1)}, bf16[128,704]{1,0:T(8,128)(2,1)S(1)}, u32[]{:S(2)}, u32[]{:S(2)}) collective-permute-start(bf16[128,704]{1,0:T(8,128)(2,1)S(1)} %bitcast.65), channel_id=1, source_target_pairs={{0,16},{16,0},{1,17},{17,1},{2,18},{18,2},{3,19},{19,3},{4,20},{20... | collective-permute-start | bytes 540680 | tf_op jit(solution)/shard_map/ppermute | solution.py:362
  224.8 0.7 copy-start.6
where the time goes:
time: 229 us; the launch traced here: 228 us
  starting transfers between devices  60.6 us (26%)
  waiting for transfers between devices  57.5 us (25%)
  blocking collectives  43.4 us (19%)
  Pallas kernels  41.9 us (18%)
  local copies, waits for them, and re-layouts  9.5 us (4%)
  matrix products  7.68 us (3%)
  other arithmetic  6.1 us (3%)
    all_to_all x3, waiting for transfers between devices, to_all(): return lax.all_to_all(copies, axes, split_axis=0, concat_axis=0, tiled=True)  27 us
    ppermute x7, starting transfers between devices, ring(): downs[c] = lax.ppermute(downs[c], 'z', down)  24 us
    all_to_all x1, blocking collectives, body(): mixed = lax.all_to_all(mixed, 'z', split_axis=0, concat_axis=0, tiled=True)  20.2 us
    all_to_all x3, starting transfers between devices, to_all(): return lax.all_to_all(copies, axes, split_axis=0, concat_axis=0, tiled=True)  15.1 us
    ppermute x1, waiting for transfers between devices, body(): got = lax.ppermute(send, 'grp', SWAP)  14.2 us
    all_to_all x1, blocking collectives, body(): grad = lax.all_to_all(grad, 'z', split_axis=0, concat_axis=0, tiled=True)  12.4 us
    all_to_all x1, blocking collectives, to_all(): return lax.all_to_all(copies, axes, split_axis=0, concat_axis=0, tiled=True)  10.8 us
    pallas_call x1, Pallas kernels, body(): call(attention_kernel, sds((N_Z, TGT + BLOCK, LANES), BF), in_specs=[SMEM...  9.49 us
  transfers between devices with their start and end apart: 24, of which 10 were waited for; matrix products, arithmetic and copies ran while one was open for 4% of the time, Pallas kernels for 10%

commit v1 on v0

v1 whole, which is shorter than its diff:
```python
import functools
import math

import jax
import jax.numpy as jnp
from jax import lax
from jax.experimental import pallas as pl
from jax.experimental.pallas import tpu as pltpu
from jax.sharding import Mesh, PartitionSpec as P


HEAD_DIM = 88
LANES = 128
CTX = 32
BLOCK = 128
TGT = 96
OWN = 48
N_Z = 8
N_DP = 8
STRIPE = 11
EPSILON = 1e-06
MOMENTUM = 0.99
SCALE = HEAD_DIM ** (-0.5)
BF = jnp.bfloat16
F32 = jnp.float32
I32 = jnp.int32
SWAP = [(0, 1), (1, 0)]
FLOPS = 10**6
DP = ("ylo", "x")
SMEM = pl.BlockSpec(memory_space=pltpu.SMEM)


def iota(shape, dim):
    return lax.broadcasted_iota(I32, shape, dim)


def mm(a, b):
    return jnp.dot(a, b, preferred_element_type=F32)


def mm_nt(a, b):
    return lax.dot_general(a, b, (((1,), (1,)), ((), ())), preferred_element_type=F32)


def sds(shape, dtype):
    return jax.ShapeDtypeStruct(shape, dtype)


def call(kernel, outs, scratch=(), flops=FLOPS, **specs):
    return pl.pallas_call(
        kernel,
        out_shape=outs,
        scratch_shapes=list(scratch),
        **specs,
        cost_estimate=pl.CostEstimate(flops=flops, bytes_accessed=10**6, transcendentals=0),
    )


def to_all(shard, axes, count):
    copies = jnp.broadcast_to(shard[None], (count, *shard.shape))
    return lax.all_to_all(copies, axes, split_axis=0, concat_axis=0, tiled=True)


def exchange(pieces, axes):
    return lax.all_to_all(pieces, axes, split_axis=0, concat_axis=0, tiled=True)


def after(value, others):
    return lax.optimization_barrier((value, others))[0]


def normalized(values):
    center = values - jnp.mean(values, axis=-1, keepdims=True)
    factor = lax.rsqrt(jnp.mean(center * center, axis=-1, keepdims=True) + EPSILON)
    return (center * factor, factor)


def sorted_norm_kernel(tokens_ref, context_ref, moved_ref, perm_ref):
    normed = normalized(tokens_ref[...].astype(F32))[0].astype(BF)
    flag = jnp.where(context_ref[...] == 1, 1.0, 0.0)
    upto = jnp.where(iota((BLOCK, BLOCK), 0) <= iota((BLOCK, BLOCK), 1), 1.0, 0.0).astype(BF)
    before = mm(jnp.broadcast_to(flag, (16, BLOCK)).astype(BF), upto)[:1]
    spot = iota((1, BLOCK), 1).astype(F32)
    rank = jnp.where(flag == 1.0, before - 1.0, CTX + spot - before).astype(I32)
    perm = jnp.where(rank == iota((BLOCK, BLOCK), 0), 1.0, 0.0).astype(BF)
    moved_ref[...] = mm(perm, normed).astype(BF)
    perm_ref[...] = perm


def head_kernel(z_ref, core_ref, target_ref, student_ref, out_ref):
    rows = target_ref.shape[2]
    col = z_ref[0] * HEAD_DIM + iota((rows, LANES), 1)
    same = (iota((rows, LANES), 0) == col) & (iota((rows, LANES), 1) < HEAD_DIM)
    picked = jnp.where(same, 1.0, 0.0).astype(BF)

    def fill(ref):
        for k in range(3):
            got = mm(ref[k], picked).astype(BF)
            for d in range(N_DP):
                out_ref[d, :, k * LANES : (k + 1) * LANES] = got

    pl.when(core_ref[0] == 0)(lambda: fill(target_ref))
    pl.when(core_ref[0] == 1)(lambda: fill(student_ref))


def seed_norm_kernel(sin_ref, cos_ref, bsin_ref, bcos_ref, mask_ref, lower_ref, upper_ref):
    half = sin_ref.shape[1]
    rows = 32
    bsin = bsin_ref[0]
    bcos = bcos_ref[0]

    def one(i, carry):
        at = pl.multiple_of(i * rows, rows)
        t_sin = sin_ref[pl.ds(at, rows), :]
        t_cos = cos_ref[pl.ds(at, rows), :]
        a = bsin * t_cos + bcos * t_sin + mask_ref[0:1, :]
        b = bcos * t_cos - bsin * t_sin + mask_ref[1:2, :]
        mean = (jnp.sum(a, -1, keepdims=True) + jnp.sum(b, -1, keepdims=True)) / (2 * half)
        a = a - mean
        b = b - mean
        var = (jnp.sum(a * a, -1, keepdims=True) + jnp.sum(b * b, -1, keepdims=True)) / (2 * half)
        inv = lax.rsqrt(var + EPSILON)
        lower_ref[pl.ds(at, rows), :] = (a * inv).astype(BF)
        upper_ref[pl.ds(at, rows), :] = (b * inv).astype(BF)
        return carry

    lax.fori_loop(0, BLOCK // rows, one, 0, unroll=2)


def project_kernel(z_ref, *refs):
    pieces = refs[: N_Z - 1]
    target_ref, student_ref, query_ref, kv_ref, kvs_ref, rows_ref, ctx_ref = refs[N_Z - 1 :]
    slots = [d for d in range(N_Z) if d != N_Z // 2]
    for i in range(N_Z - 1):
        rows_ref[i * BLOCK : (i + 1) * BLOCK, :] = pieces[i][...]
        ctx_ref[i * CTX : (i + 1) * CTX, :] = pieces[i][:CTX, :]
    for at, count in ((0, 2), (2, 2), (4, 2), (6, 1)):
        rows = slice(at * BLOCK, (at + count) * BLOCK)
        got = mm(rows_ref[rows, :], target_ref[...]).astype(BF)
        kv_ref[rows, :] = got[:, LANES:]
        for k in range(count):
            dest = lax.rem(z_ref[0] - slots[at + k] + N_Z, N_Z)
            query_ref[dest] = got[k * BLOCK + CTX : (k + 1) * BLOCK, :LANES]
    kvs_ref[...] = mm(ctx_ref[...], student_ref[:, LANES:]).astype(BF)


def project_last_kernel(
    first_ref, second_ref, kvs_early_ref, target_ref, student_ref, query_ref, kv_ref, kvs_ref, rows_ref
):
    early = (N_Z - 1) * CTX
    kvs_ref[:early, :] = kvs_early_ref[...]
    kvs_ref[early:, :] = mm(first_ref[:CTX, :], student_ref[:, LANES:]).astype(BF)
    rows_ref[: BLOCK // 2, :] = first_ref[...]
    rows_ref[BLOCK // 2 :, :] = second_ref[...]
    got = mm(rows_ref[...], target_ref[...]).astype(BF)
    kv_ref[...] = got[:, LANES:]
    query_ref[...] = got[CTX:, :LANES]


def softmax_rows(query, pairs):
    scores = [mm_nt(query, pair[:, :LANES]) * SCALE for pair in pairs]
    peak = functools.reduce(jnp.maximum, [jnp.max(s, axis=1, keepdims=True) for s in scores])
    total, mixed = (0.0, 0.0)
    for s, pair in zip(scores, pairs):
        raised = jnp.exp(s - peak)
        total = total + jnp.sum(raised, axis=1, keepdims=True)
        mixed = mixed + mm(raised.astype(BF), pair[:, LANES:])
    return mixed / total


def attend_target_kernel(
    z_ref, query_ref, query_last_ref, kv_ref, kv_other_ref, last_ref, last_other_ref, out_ref
):
    last = lax.rem(z_ref[0] + N_Z // 2, N_Z)

    def one(j, carry):
        query = jnp.where(j == last, query_last_ref[...], query_ref[j])
        pairs = (kv_ref, kv_other_ref, last_ref, last_other_ref)
        out_ref[j] = softmax_rows(query, [pair[...] for pair in pairs]).astype(BF)
        return carry

    lax.fori_loop(0, N_Z, one, 0)


def attend_student_kernel(core_ref, query_ref, kvs_ref, kvs_other_ref, listed_ref, out_ref):
    lane = iota((BLOCK, LANES), 1)

    def one(j, carry):
        at = pl.multiple_of(j * BLOCK, BLOCK)
        pairs = (kvs_ref[...], kvs_other_ref[...])
        mixed = softmax_rows(query_ref[pl.ds(at, BLOCK), :], pairs)
        place = (2 * j + core_ref[0]) * BLOCK + iota((BLOCK, listed_ref.shape[1]), 0)
        same = jnp.where(place == listed_ref[...], 1.0, 0.0)
        count = jnp.sum(same, axis=1, keepdims=True)
        out_ref[j] = jnp.where(lane == HEAD_DIM, count, mixed).astype(BF)
        return carry

    lax.fori_loop(0, N_Z, one, 0)


def divide(grp_ref, part_ref, keep_ref, send_ref):
    mine = pl.multiple_of(grp_ref[0] * OWN, OWN)
    other = pl.multiple_of((1 - grp_ref[0]) * OWN, OWN)
    keep_ref[...] = part_ref[pl.ds(mine, OWN), :].astype(BF)
    send_ref[...] = part_ref[pl.ds(other, OWN), :].astype(BF)


def output_student_kernel(
    grp_ref, got_ref, perm_ref, student_ref, keep_ref, send_ref, mixed_ref, count_ref,
    wide_ref, thin_ref, part_ref, all_count_ref,
):
    for h in range(N_Z):
        wide_ref[:, h * LANES : (h + 1) * LANES] = got_ref[h]
    chosen = mm(perm_ref[CTX:, :], wide_ref[...])
    lane = lax.rem(iota(chosen.shape, 1), LANES)
    all_count_ref[...] = jnp.broadcast_to(
        jnp.sum(jnp.where(lane == HEAD_DIM, chosen, 0.0), axis=1, keepdims=True), (TGT, LANES)
    )
    for h in range(N_Z):
        thin_ref[:, h * HEAD_DIM : (h + 1) * HEAD_DIM] = chosen[:, h * LANES : h * LANES + HEAD_DIM]
    mixed = thin_ref[...].astype(BF)
    for d in range(N_DP):
        mixed_ref[d] = mixed
    part_ref[...] = mm_nt(mixed, student_ref[...])
    divide(grp_ref, part_ref, keep_ref, send_ref)
    count_ref[...] = all_count_ref[pl.ds(pl.multiple_of(grp_ref[0] * OWN, OWN), OWN), :]


def output_target_kernel(grp_ref, got_ref, out_ref, keep_ref, send_ref, thin_ref, part_ref):
    for h in range(N_Z):
        thin_ref[:, h * HEAD_DIM : (h + 1) * HEAD_DIM] = got_ref[h, :, :HEAD_DIM].astype(F32)
    part_ref[...] = mm(thin_ref[...].astype(BF), out_ref[...])
    divide(grp_ref, part_ref, keep_ref, send_ref)


def slope_kernel(
    keep_ref, got_ref, keep_s_ref, got_s_ref, tokens_ref, seeds_ref, count_ref, out_ref, back_ref
):
    target_sum = keep_ref[...].astype(F32) + got_ref[...].astype(F32)
    student_sum = keep_s_ref[...].astype(F32) + got_s_ref[...].astype(F32)
    wanted = normalized(tokens_ref[...] + target_sum)[0].astype(BF).astype(F32)
    predicted, factor = normalized(seeds_ref[...] + student_sum)
    slope = jnp.clip(predicted - wanted, -1.0, 1.0) * count_ref[:, :1]
    back_ref[...] = (
        slope
        - jnp.mean(slope, axis=1, keepdims=True)
        - predicted * jnp.mean(slope * predicted, axis=1, keepdims=True)
    ) * factor
    columns = STRIPE * 2 * N_Z
    row = iota((columns, 2 * LANES), 0)
    col = iota((columns, 2 * LANES), 1)
    stripe = lax.div(col, 16)
    inner = lax.rem(col, 16)
    spread = jnp.where((inner < STRIPE) & (row == stripe * STRIPE + inner), 1.0, 0.0).astype(BF)
    for d in range(N_DP):
        part = back_ref[:, d * columns : (d + 1) * columns].astype(BF)
        part = mm(part, spread).astype(BF)
        out_ref[2 * d] = part
        out_ref[2 * d + 1] = part


def finish_kernel(core_ref, mine_ref, other_ref, out_ref):
    total = jnp.zeros(out_ref.shape, F32)
    for ref, flip in ((mine_ref, 0), (other_ref, 1)):
        side = core_ref[0] * (1 - 2 * flip) + flip
        row = iota((out_ref.shape[0], 16 * N_Z), 0)
        col = iota((out_ref.shape[0], 16 * N_Z), 1)
        stripe = side * N_Z + lax.div(col, 16)
        inner = lax.rem(col, 16)
        gather = jnp.where((inner < STRIPE) & (row == stripe * STRIPE + inner), 1.0, 0.0)
        total = total + mm(gather.astype(BF), ref[...])
    out_ref[...] = total


def blend_kernel(target_ref, student_ref, out_ref):
    turned = jnp.transpose(student_ref[...].astype(F32))
    out_ref[...] = MOMENTUM * target_ref[...].astype(F32) + (1.0 - MOMENTUM) * turned


def ring(rows, gates):
    up = [(i, (i + 1) % N_Z) for i in range(N_Z)]
    down = [(i, (i - 1) % N_Z) for i in range(N_Z)]
    below = above = rows
    lower, upper = ([], [])
    for step in range(1, N_Z // 2):
        if step in gates:
            below, above, _ = lax.optimization_barrier((below, above, gates[step]))
        below = lax.ppermute(below, "z", up)
        above = lax.ppermute(above, "z", down)
        lower.append(below)
        upper.append(above)
    first = lax.ppermute(below[: BLOCK // 2], "z", up)
    second = lax.ppermute(above[BLOCK // 2 :], "z", down)
    return [rows] + lower + upper[::-1], (first, second)


def body(
    clips, context, predict_index, target_qkv, target_out, student_qkv, student_out, mask_token
):
    tokens = clips[0]
    width = tokens.shape[1]
    half = width // 2
    z = lax.axis_index("z")
    core = lax.axis_index("core")
    grp = lax.axis_index("grp")
    z_at, core_at, grp_at = (v.astype(I32).reshape(1) for v in (z, core, grp))

    moved, perm = call(
        sorted_norm_kernel, (sds((BLOCK, width), BF), sds((BLOCK, BLOCK), BF))
    )(tokens, context)
    spacing = jnp.exp(jnp.arange(half, dtype=F32) * (-math.log(10000.0) / half))
    spot = jnp.arange(BLOCK, dtype=F32)
    t_angle = spot[:, None] * spacing[None, :]
    base = ((2 * jnp.arange(N_Z, dtype=I32) + core) * BLOCK).astype(F32)
    b_angle = base[:, None] * spacing[None, :]
    tables = (
        jnp.sin(t_angle),
        jnp.cos(t_angle),
        jnp.sin(b_angle)[:, None],
        jnp.cos(b_angle)[:, None],
    )
    table = pl.BlockSpec((BLOCK, half), lambda j: (0, 0))
    row = pl.BlockSpec((1, 1, half), lambda j: (j, 0, 0))
    block = pl.BlockSpec((BLOCK, half), lambda j: (j, 0))
    seed_a, seed_b = call(
        seed_norm_kernel,
        (sds((N_Z * BLOCK, half), BF), sds((N_Z * BLOCK, half), BF)),
        grid=(N_Z,),
        in_specs=[table, table, row, row, pl.BlockSpec((2, half), lambda j: (0, 0))],
        out_specs=(block, block),
    )(
        *tables,
        mask_token.reshape(2, half),
    )
    pieces, last = ring(moved, {2: tables, 3: (seed_a, seed_b)})

    head = call(
        head_kernel,
        sds((N_DP, width // N_DP, 3 * LANES), BF),
        in_specs=[SMEM, SMEM, pl.BlockSpec(), pl.BlockSpec()],
    )(z_at, core_at, after(target_qkv, moved), student_qkv)
    weights = after(exchange(head, DP), seed_a).reshape(width, 3 * LANES)
    swapped = lax.ppermute(weights, "core", SWAP)
    target_w = jnp.where(core == 0, weights, swapped)
    student_w = jnp.where(core == 0, swapped, weights)

    cols = student_out.shape[1] // 2
    turned = lax.dynamic_slice_in_dim(student_out.T, core * cols, cols, axis=0)
    fetched = to_all(after(turned, weights), DP, N_DP)
    fetched_other = lax.ppermute(fetched, "core", SWAP)
    relaid_t = jnp.where(
        core == 0,
        jnp.stack([fetched, fetched_other], axis=1),
        jnp.stack([fetched_other, fetched], axis=1),
    ).reshape(width, student_out.shape[0])

    listed = predict_index
    listed = jnp.concatenate([listed, lax.ppermute(listed, "core", SWAP)], axis=1)
    rows_own = lax.dynamic_slice_in_dim(perm, CTX + grp * OWN, OWN, axis=0)
    tokens_own = mm(rows_own, tokens)
    places_own = jnp.sum(rows_own.astype(F32) * spot[None, :], axis=1)
    places_own = places_own + ((2 * z + core) * BLOCK).astype(F32)
    angle = places_own[:, None] * spacing[None, :]
    seeds = mask_token[None, :] + jnp.concatenate([jnp.sin(angle), jnp.cos(angle)], axis=1)

    query_s = mm(seed_a, student_w[:half, :LANES]) + mm(seed_b, student_w[half:, :LANES])
    query_s = query_s.astype(BF)

    query_t, kv, kvs = call(
        project_kernel,
        (
            sds((N_Z, TGT, LANES), BF),
            sds(((N_Z - 1) * BLOCK, 2 * LANES), BF),
            sds(((N_Z - 1) * CTX, 2 * LANES), BF),
        ),
        scratch=(
            pltpu.VMEM(((N_Z - 1) * BLOCK, width), BF),
            pltpu.VMEM(((N_Z - 1) * CTX, width), BF),
        ),
        in_specs=[SMEM] + [pl.BlockSpec()] * (N_Z + 1),
    )(z_at, *pieces, target_w, student_w)
    kv_other = lax.ppermute(kv, "core", SWAP)
    query_last, kv_last, kvs = call(
        project_last_kernel,
        (
            sds((TGT, LANES), BF),
            sds((BLOCK, 2 * LANES), BF),
            sds((N_Z * CTX, 2 * LANES), BF),
        ),
        scratch=(pltpu.VMEM((BLOCK, width), BF),),
    )(*last, kvs, target_w, student_w)
    kvs_other = lax.ppermute(kvs, "core", SWAP)
    kv_last_other = lax.ppermute(kv_last, "core", SWAP)

    mixed_s = call(
        attend_student_kernel, sds((N_Z, BLOCK, LANES), BF), in_specs=[SMEM] + [pl.BlockSpec()] * 4
    )(core_at, query_s, kvs, kvs_other, listed)
    mixed_s = exchange(after(mixed_s, relaid_t), "z")
    mixed_t = call(
        attend_target_kernel, sds((N_Z, TGT, LANES), BF), in_specs=[SMEM] + [pl.BlockSpec()] * 6
    )(z_at, query_t, query_last, kv, kv_other, kv_last, kv_last_other)
    mixed_t = exchange(after(mixed_t, mixed_s), "z")
    keep_s, send_s, mixed_c, count = call(
        output_student_kernel,
        (
            sds((OWN, width), BF),
            sds((OWN, width), BF),
            sds((N_DP, TGT, N_Z * HEAD_DIM), BF),
            sds((OWN, LANES), F32),
        ),
        scratch=(
            pltpu.VMEM((BLOCK, N_Z * LANES), BF),
            pltpu.VMEM((TGT, N_Z * HEAD_DIM), F32),
            pltpu.VMEM((TGT, width), F32),
            pltpu.VMEM((TGT, LANES), F32),
        ),
        in_specs=[SMEM] + [pl.BlockSpec()] * 3,
    )(grp_at, mixed_s, perm, relaid_t)
    got_s = lax.ppermute(send_s, "grp", SWAP)
    target_blend = call(
        blend_kernel,
        sds((half, width), F32),
        grid=(width // LANES,),
        in_specs=[
            pl.BlockSpec((half, LANES), lambda i: (0, i)),
            pl.BlockSpec((LANES, half), lambda i: (i, 0)),
        ],
        out_specs=pl.BlockSpec((half, LANES), lambda i: (0, i)),
    )(target_out, after(relaid_t, mixed_c))
    keep, send = call(
        output_target_kernel,
        (sds((OWN, width), BF), sds((OWN, width), BF)),
        scratch=(pltpu.VMEM((TGT, N_Z * HEAD_DIM), F32), pltpu.VMEM((TGT, width), F32)),
        in_specs=[SMEM] + [pl.BlockSpec()] * 2,
    )(grp_at, after(mixed_t, got_s), target_out)
    got = lax.ppermute(send, "grp", SWAP)
    mixed_all = exchange(after(mixed_c, (mixed_t, target_blend)), DP).reshape(N_DP * TGT, N_Z * HEAD_DIM)
    stripes = call(
        slope_kernel, sds((2 * N_DP, OWN, 256), BF), scratch=(pltpu.VMEM((OWN, width), F32),)
    )(keep, got, keep_s, got_s, tokens_own, seeds, count)
    stripes = after(stripes, mixed_all)
    arrived = lax.all_to_all(stripes, (*DP, "grp"), split_axis=0, concat_axis=0, tiled=True)
    grad = lax.dot_general(
        arrived.reshape(N_DP * TGT, 256),
        mixed_all,
        (((0,), (0,)), ((), ())),
        preferred_element_type=F32,
    )
    lower, upper = (grad[: 16 * N_Z], grad[16 * N_Z :])
    grad_keep = jnp.where(core == 0, lower, upper)
    grad_send = jnp.where(core == 0, upper, lower)
    grad = grad_keep + lax.ppermute(grad_send, "core", SWAP)
    grad = grad.astype(BF).reshape(N_Z, 16, N_Z * HEAD_DIM)
    grad = lax.all_to_all(grad, "z", split_axis=0, concat_axis=0, tiled=True)
    grad = jnp.sum(grad.astype(F32), axis=0).astype(BF)
    grad = to_all(grad, "z", N_Z).reshape(16 * N_Z, N_Z * HEAD_DIM)
    other = lax.ppermute(grad, "core", SWAP)
    out_grad = call(
        finish_kernel,
        sds((student_out.shape[1], student_out.shape[0]), F32),
        in_specs=[SMEM] + [pl.BlockSpec()] * 2,
    )(core_at, grad, other).T
    return (out_grad, target_blend)


def solution(mesh):
    fine = Mesh(mesh.devices.reshape(8, 2, 2, 2, 4), ("z", "core", "grp", "ylo", "x"))
    seq = ("z", "core")
    in_specs = (
        P(DP, seq, None),
        P(DP, seq),
        P(DP, seq),
        P(None, DP, "grp"),
        P("grp", None),
        P(None, DP, "grp"),
        P("grp", DP),
        P(),
    )
    out_specs = (P("grp", DP), P("grp", None))
    return jax.shard_map(body, mesh=fine, in_specs=in_specs, out_specs=out_specs, check_vma=False)
```

time: 229 us -> 217 us (0.948)
  waiting for transfers between devices: 57.5 us -> 32.9 us
  Pallas kernels: 41.9 us -> 53.5 us
  other arithmetic: 6.1 us -> 11.8 us
  starting transfers between devices: 60.6 us -> 56.6 us
    all_to_all x3 -> x1, waiting for transfers between devices: 27 us -> 0.01 us  [to_all(): return lax.all_to_all(copies, axes, split_axis=0, concat_axis=0, tiled=True)]
    ppermute x14 -> x12, waiting for transfers between devices: 6.46 us -> 25 us  [the longest x3 12.9 us: ring(): below = lax.ppermute(below, 'z', up)]
    all_to_all x1 -> x4, starting transfers between devices: 7.06 us -> 21.3 us  [exchange(): return lax.all_to_all(pieces, axes, split_axis=0, concat_axis=0, tiled=True)]
    pallas_call x6 -> x10, Pallas kernels: 37.2 us -> 48.7 us  [the longest x1 8.65 us: body(): call(blend_kernel, sds((half, width), F32), grid=(width // LANES,), in_sp...]
    ppermute x1, waiting for transfers between devices: 14.2 us -> 2.74 us  [body(): got = lax.ppermute(send, 'grp', SWAP)]
    all_to_all x3 -> x1, starting transfers between devices: 15.1 us -> 5.47 us  [to_all(): return lax.all_to_all(copies, axes, split_axis=0, concat_axis=0, tiled=True)]
    all_to_all x1 -> x4, waiting for transfers between devices: 8.53 us -> 1.92 us  [exchange(): return lax.all_to_all(pieces, axes, split_axis=0, concat_axis=0, tiled=True)]
    select_n x0 -> x2, other arithmetic: none -> 5.2 us  [the longest x1 3.45 us: body(): jnp.where(core == 0, jnp.stack([fetched, fetched_other], axis=1), jnp.sta...]
  transfers between devices with their start and end apart: 24 -> 23, of which waited for: 10 -> 9; matrix products, arithmetic and copies ran while one was open for 4% -> 10% of each run, Pallas kernels for 10% -> 21%
where the time goes in v1:
time: 217 us; the launch traced here: 216 us
  starting transfers between devices  56.6 us (26%)
  Pallas kernels  53.5 us (25%)
  blocking collectives  45.6 us (21%)
  waiting for transfers between devices  32.9 us (15%)
  other arithmetic  11.8 us (5%)
  local copies, waits for them, and re-layouts  8.62 us (4%)
  matrix products  6.08 us (3%)
    all_to_all x4, starting transfers between devices, exchange(): return lax.all_to_all(pieces, axes, split_axis=0, concat_axis=0, tiled=True)  21.3 us
    all_to_all x1, blocking collectives, body(): lax.all_to_all(stripes, (*DP, 'grp'), split_axis=0, concat_axis=0, tiled=...  18.4 us
    all_to_all x1, blocking collectives, body(): grad = lax.all_to_all(grad, 'z', split_axis=0, concat_axis=0, tiled=True)  15.9 us
    ppermute x3, waiting for transfers between devices, ring(): below = lax.ppermute(below, 'z', up)  12.9 us
    all_to_all x1, blocking collectives, to_all(): return lax.all_to_all(copies, axes, split_axis=0, concat_axis=0, tiled=True)  11.3 us
    ppermute x1, waiting for transfers between devices, body(): got_s = lax.ppermute(send_s, 'grp', SWAP)  11.2 us
    ppermute x3, starting transfers between devices, ring(): above = lax.ppermute(above, 'z', down)  9.39 us
    pallas_call x1, Pallas kernels, body(): call(blend_kernel, sds((half, width), F32), grid=(width // LANES,), in_sp...  8.65 us
  transfers between devices with their start and end apart: 23, of which 9 were waited for; matrix products, arithmetic and copies ran while one was open for 10% of the time, Pallas kernels for 21%

profile of v1, /device:TPU:1, one launch (start us, length us, event | category | flops | bytes accessed | tf_op | source)
XLA Modules:
  0.0 216.0 jit_solution(8930078218209851708)
XLA Ops:
  0.7 2.3 %shard_map.95 = (bf16[128,1408]{1,0:T(8,128)(2,1)}, bf16[128,128]{1,0:T(8,128)(2,1)}) custom-call(bf16[128,1408]{1,0:T(8,128)(2,1)} %bitcast.29, s32[1,128]{1,0:T(1,128)} %context_ref.1), custom_call_target="tpu_custom_call" | custom-call | flops 1000000 | bytes 1000000 | tf_op jit(solution)/shard_map/pallas_call | solution.py:308
  2.9 2.8 %shard_map.97 = bf16[8,176,384]{2,1,0:T(8,128)(2,1)} custom-call(s32[1]{0:T(128)} %bitcast.2.z_ref, s32[1]{0:T(128)} %bitcast.core_ref, bf16[3,176,704]{2,1,0:T(8,128)(2,1)} %target_ref.1, bf16[3,176,704]{2,1,0:T(8,128)(2,1)} %student_ref.1), custom_call_target="tpu_custom_call" | custom-call | flops 1000000 | bytes 1000000 | tf_op jit(solution)/shard_map/pallas_call | solution.py:337
  5.8 6.0 %all-to-all-start = ((bf16[8,176,384]{2,1,0:T(8,128)(2,1)}), bf16[8,176,384]{2,1,0:T(8,128)(2,1)S(1)}, u32[]{:S(2)}, u32[]{:S(2)}) async-start(bf16[8,176,384]{2,1,0:T(8,128)(2,1)} %shard_map.97), calls=%async_computation | async-start | bytes 2162688 | tf_op jit(solution)/shard_map/all_to_all | solution.py:65
  11.7 1.6 collective-permute-start
  13.4 4.0 %collective-permute-start.1 = (bf16[128,1408]{1,0:T(8,128)(2,1)}, bf16[128,1408]{1,0:T(8,128)(2,1)}, u32[]{:S(2)}, u32[]{:S(2)}) collective-permute-start(bf16[128,1408]{1,0:T(8,128)(2,1)} %get-tuple-element.31.refs_0_), channel_id=1, source_target_pairs={{0,224},{32,0},{64,32},{96,64},{128,96},{160,128},{192,160},{224,1... | collective-permute-start | bytes 1081352 | tf_op jit(solution)/shard_map/ppermute | solution.py:289
  17.4 2.2 %fusion.1 = (f32[128,704]{1,0:T(8,128)}, f32[128,704]{1,0:T(8,128)}) fusion(f32[704]{0:T(1024)S(1)} %multiply_exponential_fusion), kind=kLoop, calls=%fused_computation.6 | loop fusion | flops 90112 | bytes 723712 | tf_op jit(solution)/shard_map/cos | solution.py:318
  19.6 1.4 multiply_cosine_fusion.1
  21.0 0.7 reshape.138.mask_ref
  21.7 6.9 %shard_map.96 = (bf16[1024,704]{1,0:T(8,128)(2,1)}, bf16[1024,704]{1,0:T(8,128)(2,1)}) custom-call(f32[128,704]{1,0:T(8,128)} %get-tuple-element.67.sin_ref, f32[128,704]{1,0:T(8,128)} %get-tuple-element.66.cos_ref, f32[8,1,704]{2,1,0:T(1,128)} %get-tuple-element.65.bsin_ref, f32[8,1,704]{2,1,0:T(1,128)} %get-tuple-element.64.bcos_ref, ...), custom_call_target="tpu_custom_call" | custom-call | flops 1000000 | bytes 1000000 | tf_op jit(solution)/shard_map/pallas_call | solution.py:325
  28.6 1.3 collective-permute-start.6
  29.9 1.1 broadcast_in_dim.4
  31.0 5.5 %all-to-all-start.1 = ((bf16[8,88,704]{2,1,0:T(8,128)(2,1)}), bf16[8,88,704]{2,1,0:T(8,128)(2,1)S(1)}, u32[]{:S(2)}, u32[]{:S(2)}) async-start(bf16[8,88,704]{2,1,0:T(8,128)(2,1)} %broadcast_in_dim.4), calls=%async_computation.1 | async-start | bytes 2162688 | tf_op jit(solution)/shard_map/all_to_all | solution.py:61
  36.6 2.7 %collective-permute-start.3 = (bf16[128,1408]{1,0:T(8,128)(2,1)}, bf16[128,1408]{1,0:T(8,128)(2,1)}, u32[]{:S(2)}, u32[]{:S(2)}) collective-permute-start(bf16[128,1408]{1,0:T(8,128)(2,1)} %collective-permute-done.1.refs_6_), channel_id=1, source_target_pairs={{0,224},{32,0},{64,32},{96,64},{128,96},{160,128},{192,160},{224,1... | collective-permute-start | bytes 1081352 | tf_op jit(solution)/shard_map/ppermute | solution.py:289
  39.3 8.5 %collective-permute-done.2.refs_2_ = bf16[128,1408]{1,0:T(8,128)(2,1)} collective-permute-done((bf16[128,1408]{1,0:T(8,128)(2,1)}, bf16[128,1408]{1,0:T(8,128)(2,1)}, u32[]{:S(2)}, u32[]{:S(2)}) %collective-permute-start.2) | collective-permute-done | bytes 360480 | tf_op jit(solution)/shard_map/ppermute | solution.py:288
  47.8 2.7 %collective-permute-start.5 = (bf16[128,1408]{1,0:T(8,128)(2,1)}, bf16[128,1408]{1,0:T(8,128)(2,1)}, u32[]{:S(2)}, u32[]{:S(2)}) collective-permute-start(bf16[128,1408]{1,0:T(8,128)(2,1)} %collective-permute-done.3.refs_5_), channel_id=1, source_target_pairs={{0,224},{32,0},{64,32},{96,64},{128,96},{160,128},{192,160},{224,1... | collective-permute-start | bytes 1081352 | tf_op jit(solution)/shard_map/ppermute | solution.py:289
  50.4 1.7 collective-permute-start.12
  52.2 0.8 collective-permute-done.12
  53.0 0.7 pad_add_fusion.listed_ref
  53.6 4.4 %collective-permute-done.4.refs_3_ = bf16[128,1408]{1,0:T(8,128)(2,1)} collective-permute-done((bf16[128,1408]{1,0:T(8,128)(2,1)}, bf16[128,1408]{1,0:T(8,128)(2,1)}, u32[]{:S(2)}, u32[]{:S(2)}) %collective-permute-start.4) | collective-permute-done | bytes 360480 | tf_op jit(solution)/shard_map/ppermute | solution.py:288
  58.1 1.6 slice.24
  59.7 1.6 slice.25
  61.3 2.7 %collective-permute-start.8 = (bf16[64,1408]{1,0:T(8,128)(2,1)}, bf16[64,1408]{1,0:T(8,128)(2,1)}, u32[]{:S(2)}, u32[]{:S(2)}) collective-permute-start(bf16[64,1408]{1,0:T(8,128)(2,1)} %slice.25), channel_id=1, source_target_pairs={{0,224},{32,0},{64,32},{96,64},{128,96},{160,128},{192,160},{224,1... | collective-permute-start | bytes 540680 | tf_op jit(solution)/shard_map/ppermute | solution.py:293
  64.0 2.6 %collective-permute-start.13 = (bf16[8,88,704]{2,1,0:T(8,128)(2,1)S(1)}, bf16[8,88,704]{2,1,0:T(8,128)(2,1)}, u32[]{:S(2)}, u32[]{:S(2)}) collective-permute-start(bf16[8,88,704]{2,1,0:T(8,128)(2,1)S(1)} %all-to-all-done.1), channel_id=1, source_target_pairs={{0,16},{16,0},{1,17},{17,1},{2,18},{18,2},{3,19},{19,3},{4,20},{20... | collective-permute-start | bytes 2973704 | tf_op jit(solution)/shard_map/ppermute | solution.py:350
  66.6 1.8 broadcast_select_fusion
  68.3 4.8 %shard_map.98 = (bf16[8,96,128]{2,1,0:T(8,128)(2,1)}, bf16[896,256]{1,0:T(8,128)(2,1)}, bf16[224,256]{1,0:T(8,128)(2,1)}) custom-call(s32[1]{0:T(128)} %bitcast.2.z_ref, bf16[128,1408]{1,0:T(8,128)(2,1)} %get-tuple-element.31.refs_0_, bf16[128,1408]{1,0:T(8,128)(2,1)} %collective-permute-done.refs_1_, bf16[128,1408]{1,0:T(8,128)(2,1)} %collective-permute-done.2.refs_2_, ...), custom_call_target="tpu_custom_call" | custom-call | flops 1000000 | bytes 1000000 | tf_op jit(solution)/shard_map/pallas_call | solution.py:369
  73.2 3.0 %shard_map.99 = (bf16[96,128]{1,0:T(8,128)(2,1)}, bf16[128,256]{1,0:T(8,128)(2,1)}, bf16[256,256]{1,0:T(8,128)(2,1)}) custom-call(bf16[64,1408]{1,0:T(8,128)(2,1)} %collective-permute-done.7.first_ref, bf16[64,1408]{1,0:T(8,128)(2,1)} %collective-permute-done.8.second_ref, bf16[224,256]{1,0:T(8,128)(2,1)} %get-tuple-element.41.kvs_early_ref, ...), custom_call_target="tpu_custom_call" | custom-call | flops 1000000 | bytes 1000000 | tf_op jit(solution)/shard_map/pallas_call | solution.py:383
  76.2 1.6 fusion.3
  77.8 2.3 %fusion.query_ref = bf16[1024,128]{1,0:T(8,128)(2,1)} fusion(f32[1024,128]{1,0:T(8,128)S(1)} %fusion.3, bf16[1024,704]{1,0:T(8,128)(2,1)S(1)} %copy-done.1, bf16[1408,384]{1,0:T(8,128)(2,1)} %get-tuple-element.60.refs_8_.student_ref), kind=kOutput, calls=%fused_computation.2 | convolution fusion | flops 184811520 | bytes 2408448 | tf_op jit(solution)/shard_map/dot_general | solution.py:38
  80.1 0.4 collective-permute-start.9
  80.5 0.7 copy-done.12
  81.1 5.2 %shard_map.101 = bf16[8,128,128]{2,1,0:T(8,128)(2,1)} custom-call(s32[1]{0:T(128)} %bitcast.core_ref, bf16[1024,128]{1,0:T(8,128)(2,1)} %fusion.query_ref, bf16[256,256]{1,0:T(8,128)(2,1)} %get-tuple-element.45.kvs_ref, bf16[256,256]{1,0:T(8,128)(2,1)} %copy-done.12, s32[1,384]{1,0:T(1,128)} %pad_add_fusion.listed_ref), custom_call_target="tpu_custom_call" | custom-call | flops 1000000 | bytes 1000000 | tf_op jit(solution)/shard_map/pallas_call | solution.py:395
  86.3 3.4 %maximum_select_fusion = bf16[8,2,88,704]{3,2,1,0:T(8,128)(2,1)} fusion(bf16[8,1,88,704]{3,2,1,0:T(8,128)(2,1)} %bitcast.7, bf16[8,1,88,704]{3,2,1,0:T(8,128)(2,1)S(1)} %bitcast.26, pred[]{:T(512)S(6)} %eq.2), kind=kLoop, calls=%fused_computation | loop fusion | flops 2973696 | bytes 3964929 | tf_op jit(solution)/shard_map/jit(_where)/select_n | solution.py:351
  89.8 5.6 %all-to-all-start.2 = ((bf16[8,128,128]{2,1,0:T(8,128)(2,1)}), bf16[8,128,128]{2,1,0:T(8,128)(2,1)S(1)}, u32[]{:S(2)}, u32[]{:S(2)}) async-start(bf16[8,128,128]{2,1,0:T(8,128)(2,1)} %shard_map.101), calls=%async_computation.2 | async-start | bytes 524288 | tf_op jit(solution)/shard_map/all_to_all | solution.py:65
  95.4 0.5 collective-permute-start.10
  95.8 0.9 collective-permute-done.10.last_other_ref
  96.8 0.6 copy-done.14
  97.5 8.2 %shard_map.100 = bf16[8,96,128]{2,1,0:T(8,128)(2,1)} custom-call(s32[1]{0:T(128)} %bitcast.2.z_ref, bf16[8,96,128]{2,1,0:T(8,128)(2,1)} %get-tuple-element.40.query_ref, bf16[96,128]{1,0:T(8,128)(2,1)} %get-tuple-element.42.query_last_ref, bf16[896,256]{1,0:T(8,128)(2,1)} %get-tuple-element.43.kv_ref, bf16[896,256]{1,0:T(8,128)(2,1)} %copy-done.8, ...), custom_call_target="tpu_custom_call" | custom-call | flops 1000000 | bytes 1000000 | tf_op jit(solution)/shard_map/pallas_call | solution.py:399
  105.7 1.9 all-to-all-done.2.got_ref
  107.6 4.9 %all-to-all-start.3 = ((bf16[8,96,128]{2,1,0:T(8,128)(2,1)}), bf16[8,96,128]{2,1,0:T(8,128)(2,1)S(1)}, u32[]{:S(2)}, u32[]{:S(2)}) async-start(bf16[8,96,128]{2,1,0:T(8,128)(2,1)} %shard_map.100), calls=%async_computation.3 | async-start | bytes 393216 | tf_op jit(solution)/shard_map/all_to_all | solution.py:65
  112.6 0.8 multiply_reduce_fusion
  113.4 3.9 %shard_map.102 = (bf16[48,1408]{1,0:T(8,128)(2,1)}, bf16[48,1408]{1,0:T(8,128)(2,1)}, bf16[8,96,704]{2,1,0:T(8,128)(2,1)}, f32[48,128]{1,0:T(8,128)}) custom-call(s32[1]{0:T(128)} %bitcast.1.grp_ref, bf16[8,128,128]{2,1,0:T(8,128)(2,1)} %copy-done.4, bf16[128,128]{1,0:T(8,128)(2,1)} %get-tuple-element.49.perm_ref, bf16[1408,704]{1,0:T(8,128)(2,1)} %bitcast.23), custom_call_target="tpu_custom_call" | custom-call | flops 1000000 | bytes 1000000 | tf_op jit(solution)/shard_map/pallas_call | solution.py:403
  117.3 8.7 %shard_map.105 = f32[704,1408]{1,0:T(8,128)} custom-call(bf16[704,1408]{1,0:T(8,128)(2,1)} %target_ref.2, bf16[1408,704]{1,0:T(8,128)(2,1)} %bitcast.24), custom_call_target="tpu_custom_call" | custom-call | flops 1000000 | bytes 1000000 | tf_op jit(solution)/shard_map/pallas_call | solution.py:420
  126.0 0.7 copy-done.5
  126.7 4.9 %all-to-all-start.4 = ((bf16[8,96,704]{2,1,0:T(8,128)(2,1)}), bf16[8,96,704]{2,1,0:T(8,128)(2,1)S(1)}, u32[]{:S(2)}, u32[]{:S(2)}) async-start(bf16[8,96,704]{2,1,0:T(8,128)(2,1)} %get-tuple-element.58), calls=%async_computation.4 | async-start | bytes 2359296 | tf_op jit(solution)/shard_map/all_to_all | solution.py:65
  131.5 0.6 multiply_sine_fusion
  132.1 2.7 %collective-permute-start.14 = (bf16[48,1408]{1,0:T(8,128)(2,1)S(1)}, bf16[48,1408]{1,0:T(8,128)(2,1)S(1)}, u32[]{:S(2)}, u32[]{:S(2)}) collective-permute-start(bf16[48,1408]{1,0:T(8,128)(2,1)S(1)} %copy-done.17), channel_id=1, source_target_pairs={{0,8},{8,0},{1,9},{9,1},{2,10},{10,2},{3,11},{11,3},{4,12},{12,4},... | collective-permute-start | bytes 405512 | tf_op jit(solution)/shard_map/ppermute | solution.py:419
  134.8 0.8 maximum_add_fusion.seeds_ref
  135.7 11.2 %collective-permute-done.14.got_s_ref = bf16[48,1408]{1,0:T(8,128)(2,1)S(1)} collective-permute-done((bf16[48,1408]{1,0:T(8,128)(2,1)S(1)}, bf16[48,1408]{1,0:T(8,128)(2,1)S(1)}, u32[]{:S(2)}, u32[]{:S(2)}) %collective-permute-start.14) | collective-permute-done | bytes 135200 | tf_op jit(solution)/shard_map/ppermute | solution.py:419
  146.9 3.0 %shard_map.103 = (bf16[48,1408]{1,0:T(8,128)(2,1)}, bf16[48,1408]{1,0:T(8,128)(2,1)}) custom-call(s32[1]{0:T(128)} %bitcast.1.grp_ref, bf16[8,96,128]{2,1,0:T(8,128)(2,1)} %copy-done.5, bf16[704,1408]{1,0:T(8,128)(2,1)} %target_ref.2), custom_call_target="tpu_custom_call" | custom-call | flops 1000000 | bytes 1000000 | tf_op jit(solution)/shard_map/pallas_call | solution.py:430
  149.8 1.2 collective-permute-start.15
  151.0 1.6 fusion.6.tokens_ref
  152.7 2.7 %collective-permute-done.15.got_ref = bf16[48,1408]{1,0:T(8,128)(2,1)S(1)} collective-permute-done((bf16[48,1408]{1,0:T(8,128)(2,1)}, bf16[48,1408]{1,0:T(8,128)(2,1)S(1)}, u32[]{:S(2)}, u32[]{:S(2)}) %collective-permute-start.15) | collective-permute-done | bytes 135200 | tf_op jit(solution)/shard_map/ppermute | solution.py:436
  155.4 0.6 copy-done.11
  156.1 2.7 %shard_map.104 = bf16[16,48,256]{2,1,0:T(8,128)(2,1)} custom-call(bf16[48,1408]{1,0:T(8,128)(2,1)} %get-tuple-element.52.keep_ref, bf16[48,1408]{1,0:T(8,128)(2,1)} %copy-done.11, bf16[48,1408]{1,0:T(8,128)(2,1)} %get-tuple-element.54.keep_s_ref, bf16[48,1408]{1,0:T(8,128)(2,1)} %copy-done.10, f32[48,1408]{1,0:T(8,128)} %fusion.6.tokens_ref, ...), custom_call_target="tpu_custom_call" | custom-call | flops 1000000 | bytes 1000000 | tf_op jit(solution)/shard_map/pallas_call | solution.py:438
  158.7 18.4 %all_to_all.40 = bf16[16,48,256]{2,1,0:T(8,128)(2,1)S(1)} all-to-all(bf16[16,48,256]{2,1,0:T(8,128)(2,1)} %shard_map.104), channel_id=1, replica_groups=mesh['z'=8,'core'=2,'grp'=2,'ylo'=2,'x'=4] {'ylo','x','grp'}, dimensions={0} | all-to-all | bytes 786432 | tf_op jit(solution)/shard_map/all_to_all | solution.py:442
  177.2 0.6 fusion.10
  177.8 2.7 %collective-permute-start.16 = (f32[128,704]{0,1:T(8,128)S(1)}, f32[128,704]{0,1:T(8,128)S(1)}, u32[]{:S(2)}, u32[]{:S(2)}) collective-permute-start(f32[128,704]{0,1:T(8,128)S(1)} %slice_select_fusion), channel_id=1, source_target_pairs={{0,16},{16,0},{1,17},{17,1},{2,18},{18,2},{3,19},{19,3},{4,20},{20... | collective-permute-start | bytes 1081352 | tf_op jit(solution)/shard_map/ppermute | solution.py:452
  180.5 1.3 collective-permute-done.16
  182.0 15.9 %all_to_all.41 = bf16[8,16,704]{2,1,0:T(8,128)(2,1)S(1)} all-to-all(bf16[8,16,704]{2,1,0:T(8,128)(2,1)S(1)} %bitcast.30), channel_id=1, replica_groups=mesh['z'=8,'core'=2,'grp'=2,'ylo'=2,'x'=4] {'z'}, dimensions={0} | all-to-all | bytes 360448 | tf_op jit(solution)/shard_map/all_to_all | solution.py:454
  197.9 11.3 %all_to_all.42 = bf16[8,16,704]{2,1,0:T(8,128)(2,1)S(1)} all-to-all(bf16[8,16,704]{2,1,0:T(8,128)(2,1)S(1)} %broadcast_in_dim.5), channel_id=1, replica_groups=mesh['z'=8,'core'=2,'grp'=2,'ylo'=2,'x'=4] {'z'}, dimensions={0} | all-to-all | bytes 360448 | tf_op jit(solution)/shard_map/all_to_all | solution.py:61
  209.2 2.9 %collective-permute-start.17 = (bf16[128,704]{1,0:T(8,128)(2,1)S(1)}, bf16[128,704]{1,0:T(8,128)(2,1)S(1)}, u32[]{:S(2)}, u32[]{:S(2)}) collective-permute-start(bf16[128,704]{1,0:T(8,128)(2,1)S(1)} %bitcast.31), channel_id=1, source_target_pairs={{0,16},{16,0},{1,17},{17,1},{2,18},{18,2},{3,19},{19,3},{4,20},{20... | collective-permute-start | bytes 540680 | tf_op jit(solution)/shard_map/ppermute | solution.py:457
  212.1 1.1 collective-permute-done.17.other_ref
  213.2 0.7 copy-done.9
  213.9 2.1 shard_map.106
  (58 shorter events, 0.7 us)
Async XLA Ops:
  0.6 29.3 %copy-start = (bf16[704,176]{0,1:T(8,128)(2,1)S(1)}, bf16[704,176]{0,1:T(8,128)(2,1)}, u32[]{:S(2)}) copy-start(bf16[704,176]{0,1:T(8,128)(2,1)} %param.14) | copy-start | bytes 743428
  5.8 15.2 %copy-start.15 = (f32[1408]{0:T(1024)S(1)}, f32[1408]{0:T(1024)}, u32[]{:S(2)}) copy-start(f32[1408]{0:T(1024)} %param.15) | copy-start | bytes 16900
  5.8 22.9 %all-to-all-start = ((bf16[8,176,384]{2,1,0:T(8,128)(2,1)}), bf16[8,176,384]{2,1,0:T(8,128)(2,1)S(1)}, u32[]{:S(2)}, u32[]{:S(2)}) async-start(bf16[8,176,384]{2,1,0:T(8,128)(2,1)} %shard_map.97), calls=%async_computation | async-start | bytes 2162688 | tf_op jit(solution)/shard_map/all_to_all | solution.py:65
  11.7 24.7 %collective-permute-start = (bf16[128,1408]{1,0:T(8,128)(2,1)}, bf16[128,1408]{1,0:T(8,128)(2,1)}, u32[]{:S(2)}, u32[]{:S(2)}) collective-permute-start(bf16[128,1408]{1,0:T(8,128)(2,1)} %get-tuple-element.31.refs_0_), channel_id=1, source_target_pairs={{0,32},{32,64},{64,96},{96,128},{128,160},{160,192},{192,224},{224... | collective-permute-start | bytes 1081352 | tf_op jit(solution)/shard_map/ppermute | solution.py:288
  13.4 23.1 %collective-permute-start.1 = (bf16[128,1408]{1,0:T(8,128)(2,1)}, bf16[128,1408]{1,0:T(8,128)(2,1)}, u32[]{:S(2)}, u32[]{:S(2)}) collective-permute-start(bf16[128,1408]{1,0:T(8,128)(2,1)} %get-tuple-element.31.refs_0_), channel_id=1, source_target_pairs={{0,224},{32,0},{64,32},{96,64},{128,96},{160,128},{192,160},{224,1... | collective-permute-start | bytes 1081352 | tf_op jit(solution)/shard_map/ppermute | solution.py:289
  28.6 38.0 %collective-permute-start.6 = (bf16[1408,384]{1,0:T(8,128)(2,1)S(1)}, bf16[1408,384]{1,0:T(8,128)(2,1)S(1)}, u32[]{:S(2)}, u32[]{:S(2)}) collective-permute-start(bf16[1408,384]{1,0:T(8,128)(2,1)S(1)} %bitcast.27), channel_id=1, source_target_pairs={{0,16},{16,0},{1,17},{17,1},{2,18},{18,2},{3,19},{19,3},{4,20},{20... | collective-permute-start | bytes 3244040 | tf_op jit(solution)/shard_map/ppermute | solution.py:343
  31.0 19.4 %copy-start.16 = (s32[1,192]{1,0:T(1,128)S(1)}, s32[1,192]{1,0:T(1,128)}, u32[]{:S(2)}) copy-start(s32[1,192]{1,0:T(1,128)} %param.10) | copy-start | bytes 2308
  31.0 33.0 %all-to-all-start.1 = ((bf16[8,88,704]{2,1,0:T(8,128)(2,1)}), bf16[8,88,704]{2,1,0:T(8,128)(2,1)S(1)}, u32[]{:S(2)}, u32[]{:S(2)}) async-start(bf16[8,88,704]{2,1,0:T(8,128)(2,1)} %broadcast_in_dim.4), calls=%async_computation.1 | async-start | bytes 2162688 | tf_op jit(solution)/shard_map/all_to_all | solution.py:61
  36.5 11.3 %collective-permute-start.2 = (bf16[128,1408]{1,0:T(8,128)(2,1)}, bf16[128,1408]{1,0:T(8,128)(2,1)}, u32[]{:S(2)}, u32[]{:S(2)}) collective-permute-start(bf16[128,1408]{1,0:T(8,128)(2,1)} %collective-permute-done.refs_1_), channel_id=1, source_target_pairs={{0,32},{32,64},{64,96},{96,128},{128,160},{160,192},{192,224},{224... | collective-permute-start | bytes 1081352 | tf_op jit(solution)/shard_map/ppermute | solution.py:288
  36.6 11.2 %collective-permute-start.3 = (bf16[128,1408]{1,0:T(8,128)(2,1)}, bf16[128,1408]{1,0:T(8,128)(2,1)}, u32[]{:S(2)}, u32[]{:S(2)}) collective-permute-start(bf16[128,1408]{1,0:T(8,128)(2,1)} %collective-permute-done.1.refs_6_), channel_id=1, source_target_pairs={{0,224},{32,0},{64,32},{96,64},{128,96},{160,128},{192,160},{224,1... | collective-permute-start | bytes 1081352 | tf_op jit(solution)/shard_map/ppermute | solution.py:289
  47.8 10.3 %collective-permute-start.4 = (bf16[128,1408]{1,0:T(8,128)(2,1)}, bf16[128,1408]{1,0:T(8,128)(2,1)}, u32[]{:S(2)}, u32[]{:S(2)}) collective-permute-start(bf16[128,1408]{1,0:T(8,128)(2,1)} %collective-permute-done.2.refs_2_), channel_id=1, source_target_pairs={{0,32},{32,64},{64,96},{96,128},{128,160},{160,192},{192,224},{224... | collective-permute-start | bytes 1081352 | tf_op jit(solution)/shard_map/ppermute | solution.py:288
  47.8 11.9 %collective-permute-start.5 = (bf16[128,1408]{1,0:T(8,128)(2,1)}, bf16[128,1408]{1,0:T(8,128)(2,1)}, u32[]{:S(2)}, u32[]{:S(2)}) collective-permute-start(bf16[128,1408]{1,0:T(8,128)(2,1)} %collective-permute-done.3.refs_5_), channel_id=1, source_target_pairs={{0,224},{32,0},{64,32},{96,64},{128,96},{160,128},{192,160},{224,1... | collective-permute-start | bytes 1081352 | tf_op jit(solution)/shard_map/ppermute | solution.py:289
  50.4 2.6 %collective-permute-start.12 = (s32[1,192]{1,0:T(1,128)S(1)}, s32[1,192]{1,0:T(1,128)S(1)}, u32[]{:S(2)}, u32[]{:S(2)}) collective-permute-start(s32[1,192]{1,0:T(1,128)S(1)} %copy-done.16), channel_id=1, source_target_pairs={{0,16},{16,0},{1,17},{17,1},{2,18},{18,2},{3,19},{19,3},{4,20},{20... | collective-permute-start | bytes 2312 | tf_op jit(solution)/shard_map/ppermute | solution.py:358
  59.7 13.5 %collective-permute-start.7 = (bf16[64,1408]{1,0:T(8,128)(2,1)}, bf16[64,1408]{1,0:T(8,128)(2,1)}, u32[]{:S(2)}, u32[]{:S(2)}) collective-permute-start(bf16[64,1408]{1,0:T(8,128)(2,1)} %slice.24), channel_id=1, source_target_pairs={{0,32},{32,64},{64,96},{96,128},{128,160},{160,192},{192,224},{224... | collective-permute-start | bytes 540680 | tf_op jit(solution)/shard_map/ppermute | solution.py:292
  61.3 11.9 %collective-permute-start.8 = (bf16[64,1408]{1,0:T(8,128)(2,1)}, bf16[64,1408]{1,0:T(8,128)(2,1)}, u32[]{:S(2)}, u32[]{:S(2)}) collective-permute-start(bf16[64,1408]{1,0:T(8,128)(2,1)} %slice.25), channel_id=1, source_target_pairs={{0,224},{32,0},{64,32},{96,64},{128,96},{160,128},{192,160},{224,1... | collective-permute-start | bytes 540680 | tf_op jit(solution)/shard_map/ppermute | solution.py:293
  64.0 22.3 %collective-permute-start.13 = (bf16[8,88,704]{2,1,0:T(8,128)(2,1)S(1)}, bf16[8,88,704]{2,1,0:T(8,128)(2,1)}, u32[]{:S(2)}, u32[]{:S(2)}) collective-permute-start(bf16[8,88,704]{2,1,0:T(8,128)(2,1)S(1)} %all-to-all-done.1), channel_id=1, source_target_pairs={{0,16},{16,0},{1,17},{17,1},{2,18},{18,2},{3,19},{19,3},{4,20},{20... | collective-permute-start | bytes 2973704 | tf_op jit(solution)/shard_map/ppermute | solution.py:350
  73.2 3.0 %copy-start.2 = (bf16[1024,704]{1,0:T(8,128)(2,1)S(1)}, bf16[1024,704]{1,0:T(8,128)(2,1)}, u32[]{:S(2)}) copy-start(bf16[1024,704]{1,0:T(8,128)(2,1)} %get-tuple-element.35) | copy-start | bytes 4325380
  76.2 1.6 copy-start.1
  76.2 4.3 %collective-permute-start.11 = (bf16[256,256]{1,0:T(8,128)(2,1)}, bf16[256,256]{1,0:T(8,128)(2,1)S(1)}, u32[]{:S(2)}, u32[]{:S(2)}) collective-permute-start(bf16[256,256]{1,0:T(8,128)(2,1)} %get-tuple-element.45.kvs_ref), channel_id=1, source_target_pairs={{0,16},{16,0},{1,17},{17,1},{2,18},{18,2},{3,19},{19,3},{4,20},{20... | collective-permute-start | bytes 393224 | tf_op jit(solution)/shard_map/ppermute | solution.py:392
  77.8 2.3 %copy-start.7 = (bf16[896,256]{1,0:T(8,128)(2,1)S(1)}, bf16[896,256]{1,0:T(8,128)(2,1)}, u32[]{:S(2)}) copy-start(bf16[896,256]{1,0:T(8,128)(2,1)} %get-tuple-element.43.kv_ref) | copy-start | bytes 1376260
  80.1 16.7 %collective-permute-start.9 = (bf16[896,256]{1,0:T(8,128)(2,1)S(1)}, bf16[896,256]{1,0:T(8,128)(2,1)S(1)}, u32[]{:S(2)}, u32[]{:S(2)}) collective-permute-start(bf16[896,256]{1,0:T(8,128)(2,1)S(1)} %copy-done.7), channel_id=1, source_target_pairs={{0,16},{16,0},{1,17},{17,1},{2,18},{18,2},{3,19},{19,3},{4,20},{20... | collective-permute-start | bytes 1376264 | tf_op jit(solution)/shard_map/ppermute | solution.py:382
  80.5 0.7 copy-start.12
  86.3 9.0 %copy-start.13 = (bf16[128,256]{1,0:T(8,128)(2,1)S(1)}, bf16[128,256]{1,0:T(8,128)(2,1)}, u32[]{:S(2)}) copy-start(bf16[128,256]{1,0:T(8,128)(2,1)} %get-tuple-element.44.last_ref) | copy-start | bytes 196612
  89.8 17.8 %all-to-all-start.2 = ((bf16[8,128,128]{2,1,0:T(8,128)(2,1)}), bf16[8,128,128]{2,1,0:T(8,128)(2,1)S(1)}, u32[]{:S(2)}, u32[]{:S(2)}) async-start(bf16[8,128,128]{2,1,0:T(8,128)(2,1)} %shard_map.101), calls=%async_computation.2 | async-start | bytes 524288 | tf_op jit(solution)/shard_map/all_to_all | solution.py:65
  95.4 1.4 collective-permute-start.10
  96.8 0.6 copy-start.14
  96.8 0.8 copy-start.8
  107.6 5.8 %copy-start.4 = (bf16[8,128,128]{2,1,0:T(8,128)(2,1)}, bf16[8,128,128]{2,1,0:T(8,128)(2,1)S(1)}, u32[]{:S(2)}) copy-start(bf16[8,128,128]{2,1,0:T(8,128)(2,1)S(1)} %all-to-all-done.2.got_ref) | copy-start | bytes 786436
  107.6 18.4 %all-to-all-start.3 = ((bf16[8,96,128]{2,1,0:T(8,128)(2,1)}), bf16[8,96,128]{2,1,0:T(8,128)(2,1)S(1)}, u32[]{:S(2)}, u32[]{:S(2)}) async-start(bf16[8,96,128]{2,1,0:T(8,128)(2,1)} %shard_map.100), calls=%async_computation.3 | async-start | bytes 393216 | tf_op jit(solution)/shard_map/all_to_all | solution.py:65
  126.0 6.1 %copy-start.17 = (bf16[48,1408]{1,0:T(8,128)(2,1)S(1)}, bf16[48,1408]{1,0:T(8,128)(2,1)}, u32[]{:S(2)}) copy-start(bf16[48,1408]{1,0:T(8,128)(2,1)} %get-tuple-element.50) | copy-start | bytes 405508
  126.0 0.7 copy-start.5
  126.7 32.1 %all-to-all-start.4 = ((bf16[8,96,704]{2,1,0:T(8,128)(2,1)}), bf16[8,96,704]{2,1,0:T(8,128)(2,1)S(1)}, u32[]{:S(2)}, u32[]{:S(2)}) async-start(bf16[8,96,704]{2,1,0:T(8,128)(2,1)} %get-tuple-element.58), calls=%async_computation.4 | async-start | bytes 2359296 | tf_op jit(solution)/shard_map/all_to_all | solution.py:65
  132.1 14.7 %collective-permute-start.14 = (bf16[48,1408]{1,0:T(8,128)(2,1)S(1)}, bf16[48,1408]{1,0:T(8,128)(2,1)S(1)}, u32[]{:S(2)}, u32[]{:S(2)}) collective-permute-start(bf16[48,1408]{1,0:T(8,128)(2,1)S(1)} %copy-done.17), channel_id=1, source_target_pairs={{0,8},{8,0},{1,9},{9,1},{2,10},{10,2},{3,11},{11,3},{4,12},{12,4},... | collective-permute-start | bytes 405512 | tf_op jit(solution)/shard_map/ppermute | solution.py:419
  135.7 15.4 %copy-start.3 = (bf16[1,128,1408]{2,1,0:T(8,128)(2,1)S(1)}, bf16[1,128,1408]{2,1,0:T(8,128)(2,1)}, u32[]{:S(2)}) copy-start(bf16[1,128,1408]{2,1,0:T(8,128)(2,1)} %param.8) | copy-start | bytes 1081348
  146.9 5.8 %copy-start.10 = (bf16[48,1408]{1,0:T(8,128)(2,1)}, bf16[48,1408]{1,0:T(8,128)(2,1)S(1)}, u32[]{:S(2)}) copy-start(bf16[48,1408]{1,0:T(8,128)(2,1)S(1)} %collective-permute-done.14.got_s_ref) | copy-start | bytes 405508
  149.8 5.6 %collective-permute-start.15 = (bf16[48,1408]{1,0:T(8,128)(2,1)}, bf16[48,1408]{1,0:T(8,128)(2,1)S(1)}, u32[]{:S(2)}, u32[]{:S(2)}) collective-permute-start(bf16[48,1408]{1,0:T(8,128)(2,1)} %get-tuple-element.53), channel_id=1, source_target_pairs={{0,8},{8,0},{1,9},{9,1},{2,10},{10,2},{3,11},{11,3},{4,12},{12,4},... | collective-permute-start | bytes 405512 | tf_op jit(solution)/shard_map/ppermute | solution.py:436
  155.4 0.6 copy-start.11
  177.8 4.0 %collective-permute-start.16 = (f32[128,704]{0,1:T(8,128)S(1)}, f32[128,704]{0,1:T(8,128)S(1)}, u32[]{:S(2)}, u32[]{:S(2)}) collective-permute-start(f32[128,704]{0,1:T(8,128)S(1)} %slice_select_fusion), channel_id=1, source_target_pairs={{0,16},{16,0},{1,17},{17,1},{2,18},{18,2},{3,19},{19,3},{4,20},{20... | collective-permute-start | bytes 1081352 | tf_op jit(solution)/shard_map/ppermute | solution.py:452
  209.2 3.9 %copy-start.6 = (bf16[8,16,704]{2,1,0:T(8,128)(2,1)}, bf16[8,16,704]{2,1,0:T(8,128)(2,1)S(1)}, u32[]{:S(2)}) copy-start(bf16[8,16,704]{2,1,0:T(8,128)(2,1)S(1)} %all_to_all.42) | copy-start | bytes 540676
  209.2 3.9 %collective-permute-start.17 = (bf16[128,704]{1,0:T(8,128)(2,1)S(1)}, bf16[128,704]{1,0:T(8,128)(2,1)S(1)}, u32[]{:S(2)}, u32[]{:S(2)}) collective-permute-start(bf16[128,704]{1,0:T(8,128)(2,1)S(1)} %bitcast.31), channel_id=1, source_target_pairs={{0,16},{16,0},{1,17},{17,1},{2,18},{18,2},{3,19},{19,3},{4,20},{20... | collective-permute-start | bytes 540680 | tf_op jit(solution)/shard_map/ppermute | solution.py:457
  213.2 0.7 copy-start.9

commit v2 on v1

--- a/solution.py
+++ b/solution.py
@@ -11,6 +11,7 @@
 
 HEAD_DIM = 88
 LANES = 128
+WIDE = 384
 CTX = 32
 BLOCK = 128
 TGT = 96
@@ -87,27 +88,32 @@
     perm_ref[...] = perm
 
 
-def head_kernel(z_ref, core_ref, target_ref, student_ref, out_ref):
+def head_kernel(z_ref, core_ref, target_ref, student_ref, turned_ref, out_ref):
     rows = target_ref.shape[2]
+    half = turned_ref.shape[1] // 2
     col = z_ref[0] * HEAD_DIM + iota((rows, LANES), 1)
     same = (iota((rows, LANES), 0) == col) & (iota((rows, LANES), 1) < HEAD_DIM)
     picked = jnp.where(same, 1.0, 0.0).astype(BF)
 
-    def fill(ref):
-        for k in range(3):
-            got = mm(ref[k], picked).astype(BF)
-            for d in range(N_DP):
-                out_ref[d, :, k * LANES : (k + 1) * LANES] = got
-
-    pl.when(core_ref[0] == 0)(lambda: fill(target_ref))
-    pl.when(core_ref[0] == 1)(lambda: fill(student_ref))
+    def fill(ref, at):
+        got = [mm(ref[k], picked).astype(BF) for k in range(3)]
+        turned = turned_ref[:, at : at + half]
+        rest = jnp.zeros((turned.shape[0], WIDE - half), BF)
+        for d in range(N_DP):
+            for k in range(3):
+                out_ref[d, :, k * LANES : (k + 1) * LANES] = got[k]
+            out_ref[d, :, WIDE : WIDE + half] = turned
+            out_ref[d, :, WIDE + half :] = rest
+
+    pl.when(core_ref[0] == 0)(lambda: fill(target_ref, 0))
+    pl.when(core_ref[0] == 1)(lambda: fill(student_ref, half))
 
 
 def seed_norm_kernel(sin_ref, cos_ref, bsin_ref, bcos_ref, mask_ref, lower_ref, upper_ref):
     half = sin_ref.shape[1]
     rows = 32
-    bsin = bsin_ref[0]
-    bcos = bcos_ref[0]
+    bsin = bsin_ref[pl.ds(pl.program_id(0), 1), :]
+    bcos = bcos_ref[pl.ds(pl.program_id(0), 1), :]
 
     def one(i, carry):
         at = pl.multiple_of(i * rows, rows)
@@ -127,34 +133,29 @@
     lax.fori_loop(0, BLOCK // rows, one, 0, unroll=2)
 
 
-def project_kernel(z_ref, *refs):
-    pieces = refs[: N_Z - 1]
-    target_ref, student_ref, query_ref, kv_ref, kvs_ref, rows_ref, ctx_ref = refs[N_Z - 1 :]
-    slots = [d for d in range(N_Z) if d != N_Z // 2]
-    for i in range(N_Z - 1):
+def seed_query_kernel(core_ref, lower_ref, upper_ref, mine_ref, other_ref, out_ref):
+    half = lower_ref.shape[1]
+    weight = jnp.where(core_ref[0] == 1, mine_ref[...], other_ref[...])
+    query = mm(lower_ref[...], weight[:half]) + mm(upper_ref[...], weight[half:])
+    out_ref[...] = query.astype(BF)
+
+
+def project_kernel(z_ref, core_ref, *refs):
+    pieces = refs[:N_Z]
+    mine_ref, other_ref, query_ref, kv_ref, kvs_ref, rows_ref, ctx_ref, target_ref = refs[N_Z:]
+    for i in range(N_Z):
         rows_ref[i * BLOCK : (i + 1) * BLOCK, :] = pieces[i][...]
         ctx_ref[i * CTX : (i + 1) * CTX, :] = pieces[i][:CTX, :]
-    for at, count in ((0, 2), (2, 2), (4, 2), (6, 1)):
-        rows = slice(at * BLOCK, (at + count) * BLOCK)
+    target_ref[...] = jnp.where(core_ref[0] == 0, mine_ref[...], other_ref[...])
+    student = jnp.where(core_ref[0] == 0, other_ref[:, LANES:], mine_ref[:, LANES:])
+    kvs_ref[...] = mm(ctx_ref[...], student).astype(BF)
+    for i in range(2):
+        rows = slice(i * 4 * BLOCK, (i + 1) * 4 * BLOCK)
         got = mm(rows_ref[rows, :], target_ref[...]).astype(BF)
         kv_ref[rows, :] = got[:, LANES:]
-        for k in range(count):
-            dest = lax.rem(z_ref[0] - slots[at + k] + N_Z, N_Z)
+        for k in range(4):
+            dest = lax.rem(z_ref[0] - (4 * i + k) + N_Z, N_Z)
             query_ref[dest] = got[k * BLOCK + CTX : (k + 1) * BLOCK, :LANES]
-    kvs_ref[...] = mm(ctx_ref[...], student_ref[:, LANES:]).astype(BF)
-
-
-def project_last_kernel(
-    first_ref, second_ref, kvs_early_ref, target_ref, student_ref, query_ref, kv_ref, kvs_ref, rows_ref
-):
-    early = (N_Z - 1) * CTX
-    kvs_ref[:early, :] = kvs_early_ref[...]
-    kvs_ref[early:, :] = mm(first_ref[:CTX, :], student_ref[:, LANES:]).astype(BF)
-    rows_ref[: BLOCK // 2, :] = first_ref[...]
-    rows_ref[BLOCK // 2 :, :] = second_ref[...]
-    got = mm(rows_ref[...], target_ref[...]).astype(BF)
-    kv_ref[...] = got[:, LANES:]
-    query_ref[...] = got[CTX:, :LANES]
 
 
 def softmax_rows(query, pairs):
@@ -168,34 +169,26 @@
     return mixed / total
 
 
-def attend_target_kernel(
-    z_ref, query_ref, query_last_ref, kv_ref, kv_other_ref, last_ref, last_other_ref, out_ref
-):
-    last = lax.rem(z_ref[0] + N_Z // 2, N_Z)
-
-    def one(j, carry):
-        query = jnp.where(j == last, query_last_ref[...], query_ref[j])
-        pairs = (kv_ref, kv_other_ref, last_ref, last_other_ref)
-        out_ref[j] = softmax_rows(query, [pair[...] for pair in pairs]).astype(BF)
-        return carry
-
-    lax.fori_loop(0, N_Z, one, 0)
+def attend_target_kernel(query_ref, kv_ref, kv_other_ref, out_ref):
+    rows = 4 * TGT
+    for i in range(2):
+        query = query_ref[4 * i : 4 * i + 4].reshape(rows, LANES)
+        mixed = softmax_rows(query, (kv_ref, kv_other_ref)).astype(BF)
+        out_ref[4 * i : 4 * i + 4] = mixed.reshape(4, TGT, LANES)
 
 
 def attend_student_kernel(core_ref, query_ref, kvs_ref, kvs_other_ref, listed_ref, out_ref):
-    lane = iota((BLOCK, LANES), 1)
-
-    def one(j, carry):
-        at = pl.multiple_of(j * BLOCK, BLOCK)
-        pairs = (kvs_ref[...], kvs_other_ref[...])
-        mixed = softmax_rows(query_ref[pl.ds(at, BLOCK), :], pairs)
-        place = (2 * j + core_ref[0]) * BLOCK + iota((BLOCK, listed_ref.shape[1]), 0)
+    rows = 4 * BLOCK
+    lane = iota((rows, LANES), 1)
+    slot = iota((rows, listed_ref.shape[1]), 0)
+    for i in range(2):
+        mixed = softmax_rows(query_ref[i * rows : (i + 1) * rows, :], (kvs_ref, kvs_other_ref))
+        block = lax.div(slot, BLOCK)
+        place = (2 * (4 * i + block) + core_ref[0]) * BLOCK + slot - block * BLOCK
         same = jnp.where(place == listed_ref[...], 1.0, 0.0)
         count = jnp.sum(same, axis=1, keepdims=True)
-        out_ref[j] = jnp.where(lane == HEAD_DIM, count, mixed).astype(BF)
-        return carry
-
-    lax.fori_loop(0, N_Z, one, 0)
+        mixed = jnp.where(lane == HEAD_DIM, count, mixed).astype(BF)
+        out_ref[4 * i : 4 * i + 4] = mixed.reshape(4, BLOCK, LANES)
 
 
 def divide(grp_ref, part_ref, keep_ref, send_ref):
@@ -206,8 +199,8 @@
 
 
 def output_student_kernel(
-    grp_ref, got_ref, perm_ref, student_ref, keep_ref, send_ref, mixed_ref, count_ref,
-    wide_ref, thin_ref, part_ref, all_count_ref,
+    grp_ref, core_ref, got_ref, perm_ref, mine_ref, other_ref, keep_ref, send_ref, mixed_ref,
+    count_ref, wide_ref, thin_ref, part_ref, all_count_ref,
 ):
     for h in range(N_Z):
         wide_ref[:, h * LANES : (h + 1) * LANES] = got_ref[h]
@@ -216,12 +209,16 @@
     all_count_ref[...] = jnp.broadcast_to(
         jnp.sum(jnp.where(lane == HEAD_DIM, chosen, 0.0), axis=1, keepdims=True), (TGT, LANES)
     )
+    thin_ref[...] = jnp.zeros(thin_ref.shape, F32)
     for h in range(N_Z):
-        thin_ref[:, h * HEAD_DIM : (h + 1) * HEAD_DIM] = chosen[:, h * LANES : h * LANES + HEAD_DIM]
+        at = (h // 4) * WIDE + (h % 4) * HEAD_DIM
+        thin_ref[:, at : at + HEAD_DIM] = chosen[:, h * LANES : h * LANES + HEAD_DIM]
     mixed = thin_ref[...].astype(BF)
     for d in range(N_DP):
         mixed_ref[d] = mixed
-    part_ref[...] = mm_nt(mixed, student_ref[...])
+    left = jnp.where(core_ref[0] == 0, mine_ref[...], other_ref[...])
+    right = jnp.where(core_ref[0] == 0, other_ref[...], mine_ref[...])
+    part_ref[...] = mm_nt(mixed[:, :WIDE], left) + mm_nt(mixed[:, WIDE:], right)
     divide(grp_ref, part_ref, keep_ref, send_ref)
     count_ref[...] = all_count_ref[pl.ds(pl.multiple_of(grp_ref[0] * OWN, OWN), OWN), :]
 
@@ -260,7 +257,8 @@
 
 
 def finish_kernel(core_ref, mine_ref, other_ref, out_ref):
-    total = jnp.zeros(out_ref.shape, F32)
+    half = out_ref.shape[1] // 2
+    total = jnp.zeros((out_ref.shape[0], 2 * WIDE), F32)
     for ref, flip in ((mine_ref, 0), (other_ref, 1)):
         side = core_ref[0] * (1 - 2 * flip) + flip
         row = iota((out_ref.shape[0], 16 * N_Z), 0)
@@ -269,12 +267,18 @@
         inner = lax.rem(col, 16)
         gather = jnp.where((inner < STRIPE) & (row == stripe * STRIPE + inner), 1.0, 0.0)
         total = total + mm(gather.astype(BF), ref[...])
-    out_ref[...] = total
-
-
-def blend_kernel(target_ref, student_ref, out_ref):
-    turned = jnp.transpose(student_ref[...].astype(F32))
-    out_ref[...] = MOMENTUM * target_ref[...].astype(F32) + (1.0 - MOMENTUM) * turned
+    out_ref[:, :half] = total[:, :half]
+    out_ref[:, half:] = total[:, WIDE : WIDE + half]
+
+
+def blend_kernel(core_ref, target_ref, mine_ref, other_ref, out_ref):
+    half = target_ref.shape[0] // 2
+    left = jnp.where(core_ref[0] == 0, mine_ref[...], other_ref[...])
+    right = jnp.where(core_ref[0] == 0, other_ref[...], mine_ref[...])
+    for i, part in enumerate((left, right)):
+        turned = jnp.transpose(part.astype(F32))[:half]
+        rows = slice(i * half, (i + 1) * half)
+        out_ref[rows, :] = MOMENTUM * target_ref[rows, :].astype(F32) + (1.0 - MOMENTUM) * turned
 
 
 def ring(rows, gates):
@@ -289,9 +293,8 @@
         above = lax.ppermute(above, "z", down)
         lower.append(below)
         upper.append(above)
-    first = lax.ppermute(below[: BLOCK // 2], "z", up)
-    second = lax.ppermute(above[BLOCK // 2 :], "z", down)
-    return [rows] + lower + upper[::-1], (first, second)
+    below = lax.ppermute(below, "z", up)
+    return [rows] + lower + [below] + upper[::-1]
 
 
 def body(
@@ -316,11 +319,11 @@
     tables = (
         jnp.sin(t_angle),
         jnp.cos(t_angle),
-        jnp.sin(b_angle)[:, None],
-        jnp.cos(b_angle)[:, None],
+        jnp.sin(b_angle),
+        jnp.cos(b_angle),
     )
     table = pl.BlockSpec((BLOCK, half), lambda j: (0, 0))
-    row = pl.BlockSpec((1, 1, half), lambda j: (j, 0, 0))
+    row = pl.BlockSpec((N_Z, half), lambda j: (0, 0))
     block = pl.BlockSpec((BLOCK, half), lambda j: (j, 0))
     seed_a, seed_b = call(
         seed_norm_kernel,
@@ -332,30 +335,18 @@
         *tables,
         mask_token.reshape(2, half),
     )
-    pieces, last = ring(moved, {2: tables, 3: (seed_a, seed_b)})
+    listed = predict_index
+    listed = jnp.concatenate([listed, lax.ppermute(listed, "core", SWAP)], axis=1)
+    pieces = ring(moved, {2: (tables, listed), 3: (seed_a, seed_b)})
 
     head = call(
         head_kernel,
-        sds((N_DP, width // N_DP, 3 * LANES), BF),
-        in_specs=[SMEM, SMEM, pl.BlockSpec(), pl.BlockSpec()],
-    )(z_at, core_at, after(target_qkv, moved), student_qkv)
-    weights = after(exchange(head, DP), seed_a).reshape(width, 3 * LANES)
+        sds((N_DP, width // N_DP, 2 * WIDE), BF),
+        in_specs=[SMEM, SMEM] + [pl.BlockSpec()] * 3,
+    )(z_at, core_at, after(target_qkv, moved), student_qkv, student_out.T)
+    weights = after(exchange(head, DP), seed_a).reshape(width, 2 * WIDE)
     swapped = lax.ppermute(weights, "core", SWAP)
-    target_w = jnp.where(core == 0, weights, swapped)
-    student_w = jnp.where(core == 0, swapped, weights)
-
-    cols = student_out.shape[1] // 2
-    turned = lax.dynamic_slice_in_dim(student_out.T, core * cols, cols, axis=0)
-    fetched = to_all(after(turned, weights), DP, N_DP)
-    fetched_other = lax.ppermute(fetched, "core", SWAP)
-    relaid_t = jnp.where(
-        core == 0,
-        jnp.stack([fetched, fetched_other], axis=1),
-        jnp.stack([fetched_other, fetched], axis=1),
-    ).reshape(width, student_out.shape[0])
-
-    listed = predict_index
-    listed = jnp.concatenate([listed, lax.ppermute(listed, "core", SWAP)], axis=1)
+
     rows_own = lax.dynamic_slice_in_dim(perm, CTX + grp * OWN, OWN, axis=0)
     tokens_own = mm(rows_own, tokens)
     places_own = jnp.sum(rows_own.astype(F32) * spot[None, :], axis=1)
@@ -363,70 +354,58 @@
     angle = places_own[:, None] * spacing[None, :]
     seeds = mask_token[None, :] + jnp.concatenate([jnp.sin(angle), jnp.cos(angle)], axis=1)
 
-    query_s = mm(seed_a, student_w[:half, :LANES]) + mm(seed_b, student_w[half:, :LANES])
-    query_s = query_s.astype(BF)
-
+    head_w = pl.BlockSpec((width, WIDE), lambda i: (0, 0))
+    out_w = pl.BlockSpec((width, WIDE), lambda i: (0, 1))
     query_t, kv, kvs = call(
         project_kernel,
         (
             sds((N_Z, TGT, LANES), BF),
-            sds(((N_Z - 1) * BLOCK, 2 * LANES), BF),
-            sds(((N_Z - 1) * CTX, 2 * LANES), BF),
+            sds((N_Z * BLOCK, 2 * LANES), BF),
+            sds((N_Z * CTX, 2 * LANES), BF),
         ),
         scratch=(
-            pltpu.VMEM(((N_Z - 1) * BLOCK, width), BF),
-            pltpu.VMEM(((N_Z - 1) * CTX, width), BF),
+            pltpu.VMEM((N_Z * BLOCK, width), BF),
+            pltpu.VMEM((N_Z * CTX, width), BF),
+            pltpu.VMEM((width, WIDE), BF),
         ),
-        in_specs=[SMEM] + [pl.BlockSpec()] * (N_Z + 1),
-    )(z_at, *pieces, target_w, student_w)
+        grid=(1,),
+        in_specs=[SMEM, SMEM] + [pl.BlockSpec()] * N_Z + [head_w] * 2,
+    )(z_at, core_at, *pieces, weights, swapped)
+    kvs_other = lax.ppermute(kvs, "core", SWAP)
     kv_other = lax.ppermute(kv, "core", SWAP)
-    query_last, kv_last, kvs = call(
-        project_last_kernel,
-        (
-            sds((TGT, LANES), BF),
-            sds((BLOCK, 2 * LANES), BF),
-            sds((N_Z * CTX, 2 * LANES), BF),
-        ),
-        scratch=(pltpu.VMEM((BLOCK, width), BF),),
-    )(*last, kvs, target_w, student_w)
-    kvs_other = lax.ppermute(kvs, "core", SWAP)
-    kv_last_other = lax.ppermute(kv_last, "core", SWAP)
+    query_w = pl.BlockSpec((width, LANES), lambda j: (0, 0))
+    query_s = call(
+        seed_query_kernel,
+        sds((N_Z * BLOCK, LANES), BF),
+        grid=(N_Z // 2,),
+        in_specs=[SMEM] + [pl.BlockSpec((2 * BLOCK, half), lambda j: (j, 0))] * 2 + [query_w] * 2,
+        out_specs=pl.BlockSpec((2 * BLOCK, LANES), lambda j: (j, 0)),
+    )(core_at, after(seed_a, kvs), seed_b, weights, swapped)
 
     mixed_s = call(
         attend_student_kernel, sds((N_Z, BLOCK, LANES), BF), in_specs=[SMEM] + [pl.BlockSpec()] * 4
     )(core_at, query_s, kvs, kvs_other, listed)
-    mixed_s = exchange(after(mixed_s, relaid_t), "z")
-    mixed_t = call(
-        attend_target_kernel, sds((N_Z, TGT, LANES), BF), in_specs=[SMEM] + [pl.BlockSpec()] * 6
-    )(z_at, query_t, query_last, kv, kv_other, kv_last, kv_last_other)
+    mixed_s = exchange(mixed_s, "z")
+    mixed_t = call(attend_target_kernel, sds((N_Z, TGT, LANES), BF))(query_t, kv, kv_other)
     mixed_t = exchange(after(mixed_t, mixed_s), "z")
     keep_s, send_s, mixed_c, count = call(
         output_student_kernel,
         (
             sds((OWN, width), BF),
             sds((OWN, width), BF),
-            sds((N_DP, TGT, N_Z * HEAD_DIM), BF),
+            sds((N_DP, TGT, 2 * WIDE), BF),
             sds((OWN, LANES), F32),
         ),
         scratch=(
             pltpu.VMEM((BLOCK, N_Z * LANES), BF),
-            pltpu.VMEM((TGT, N_Z * HEAD_DIM), F32),
+            pltpu.VMEM((TGT, 2 * WIDE), F32),
             pltpu.VMEM((TGT, width), F32),
             pltpu.VMEM((TGT, LANES), F32),
         ),
-        in_specs=[SMEM] + [pl.BlockSpec()] * 3,
-    )(grp_at, mixed_s, perm, relaid_t)
+        grid=(1,),
+        in_specs=[SMEM, SMEM] + [pl.BlockSpec()] * 2 + [out_w] * 2,
+    )(grp_at, core_at, mixed_s, perm, weights, swapped)
     got_s = lax.ppermute(send_s, "grp", SWAP)
-    target_blend = call(
-        blend_kernel,
-        sds((half, width), F32),
-        grid=(width // LANES,),
-        in_specs=[
-            pl.BlockSpec((half, LANES), lambda i: (0, i)),
-            pl.BlockSpec((LANES, half), lambda i: (i, 0)),
-        ],
-        out_specs=pl.BlockSpec((half, LANES), lambda i: (0, i)),
-    )(target_out, after(relaid_t, mixed_c))
     keep, send = call(
         output_target_kernel,
         (sds((OWN, width), BF), sds((OWN, width), BF)),
@@ -434,7 +413,8 @@
         in_specs=[SMEM] + [pl.BlockSpec()] * 2,
     )(grp_at, after(mixed_t, got_s), target_out)
     got = lax.ppermute(send, "grp", SWAP)
-    mixed_all = exchange(after(mixed_c, (mixed_t, target_blend)), DP).reshape(N_DP * TGT, N_Z * HEAD_DIM)
+    mixed_all = exchange(after(mixed_c, mixed_t), DP)
+    mixed_all = mixed_all.reshape(N_DP * TGT, 2 * WIDE)
     stripes = call(
         slope_kernel, sds((2 * N_DP, OWN, 256), BF), scratch=(pltpu.VMEM((OWN, width), F32),)
     )(keep, got, keep_s, got_s, tokens_own, seeds, count)
@@ -450,10 +430,18 @@
     grad_keep = jnp.where(core == 0, lower, upper)
     grad_send = jnp.where(core == 0, upper, lower)
     grad = grad_keep + lax.ppermute(grad_send, "core", SWAP)
-    grad = grad.astype(BF).reshape(N_Z, 16, N_Z * HEAD_DIM)
-    grad = lax.all_to_all(grad, "z", split_axis=0, concat_axis=0, tiled=True)
-    grad = jnp.sum(grad.astype(F32), axis=0).astype(BF)
-    grad = to_all(grad, "z", N_Z).reshape(16 * N_Z, N_Z * HEAD_DIM)
+    grad = grad.astype(BF).reshape(N_Z, 16, 2 * WIDE)
+    pieces = exchange(grad, "z")
+    turned = pl.BlockSpec((LANES, WIDE), lambda i: (i, 1))
+    target_blend = call(
+        blend_kernel,
+        sds((half, width), F32),
+        grid=(width // LANES,),
+        in_specs=[SMEM, pl.BlockSpec((half, LANES), lambda i: (0, i)), turned, turned],
+        out_specs=pl.BlockSpec((half, LANES), lambda i: (0, i)),
+    )(core_at, after(target_out, grad), weights, swapped)
+    grad = jnp.sum(pieces.astype(F32), axis=0).astype(BF)
+    grad = to_all(after(grad, target_blend), "z", N_Z).reshape(16 * N_Z, 2 * WIDE)
     other = lax.ppermute(grad, "core", SWAP)
     out_grad = call(
         finish_kernel,

time: 217 us -> 221 us (1.018)
  waiting for transfers between devices: 32.9 us -> 77.1 us
  blocking collectives: 45.6 us -> 14.3 us
  starting transfers between devices: 56.6 us -> 63 us
  other arithmetic: 11.8 us -> 6.63 us
  matrix products: 6.08 us -> 2.12 us
  local copies, waits for them, and re-layouts: 8.62 us -> 4.98 us
  Pallas kernels: 53.5 us -> 51.2 us
    all_to_all x2 -> x0, blocking collectives: 34.3 us -> none  [the longest x1 18.4 us: body(): lax.all_to_all(stripes, (*DP, 'grp'), split_axis=0, concat_axis=0, tiled=...]
    all_to_all x4 -> x5, waiting for transfers between devices: 1.92 us -> 27.2 us  [exchange(): return lax.all_to_all(pieces, axes, split_axis=0, concat_axis=0, tiled=True)]
    ppermute x3 -> x4, waiting for transfers between devices: 12.9 us -> 29.7 us  [ring(): below = lax.ppermute(below, 'z', up)]
    all_to_all x1, waiting for transfers between devices: 0.01 us -> 8.44 us  [body(): lax.all_to_all(stripes, (*DP, 'grp'), split_axis=0, concat_axis=0, tiled=...]
    all_to_all x1, starting transfers between devices: 5.47 us -> 12.3 us  [body(): lax.all_to_all(stripes, (*DP, 'grp'), split_axis=0, concat_axis=0, tiled=...]
    ppermute x4 -> x0, starting transfers between devices: 5.76 us -> none  [the longest x1 2.67 us: ring(): second = lax.ppermute(above[BLOCK // 2:], 'z', down)]
    select_n x2 -> x0, other arithmetic: 5.2 us -> none  [the longest x1 3.45 us: body(): jnp.where(core == 0, jnp.stack([fetched, fetched_other], axis=1), jnp.sta...]
    ppermute x1, waiting for transfers between devices: 11.2 us -> 6.29 us  [body(): got_s = lax.ppermute(send_s, 'grp', SWAP)]
  transfers between devices with their start and end apart: 23 -> 21, of which waited for: 9 -> 14; matrix products, arithmetic and copies ran while one was open for 10% -> 4% of each run, Pallas kernels for 21% -> 17%
where the time goes in v2:
time: 221 us; the launch traced here: 220 us
  waiting for transfers between devices  77.1 us (35%)
  starting transfers between devices  63 us (29%)
  Pallas kernels  51.2 us (23%)
  blocking collectives  14.3 us (6%)
  other arithmetic  6.63 us (3%)
  local copies, waits for them, and re-layouts  4.98 us (2%)
    ppermute x4, waiting for transfers between devices, ring(): below = lax.ppermute(below, 'z', up)  29.7 us
    all_to_all x5, waiting for transfers between devices, exchange(): return lax.all_to_all(pieces, axes, split_axis=0, concat_axis=0, tiled=True)  27.2 us
    all_to_all x5, starting transfers between devices, exchange(): return lax.all_to_all(pieces, axes, split_axis=0, concat_axis=0, tiled=True)  23.2 us
    all_to_all x1, blocking collectives, to_all(): return lax.all_to_all(copies, axes, split_axis=0, concat_axis=0, tiled=True)  14.3 us
    all_to_all x1, starting transfers between devices, body(): lax.all_to_all(stripes, (*DP, 'grp'), split_axis=0, concat_axis=0, tiled=...  12.3 us
    pallas_call x1, Pallas kernels, body(): call(blend_kernel, sds((half, width), F32), grid=(width // LANES,), in_sp...  8.84 us
    all_to_all x1, waiting for transfers between devices, body(): lax.all_to_all(stripes, (*DP, 'grp'), split_axis=0, concat_axis=0, tiled=...  8.44 us
    ppermute x3, starting transfers between devices, ring(): above = lax.ppermute(above, 'z', down)  8.37 us
  transfers between devices with their start and end apart: 21, of which 14 were waited for; matrix products, arithmetic and copies ran while one was open for 4% of the time, Pallas kernels for 17%

profile of v2, /device:TPU:1, one launch (start us, length us, event | category | flops | bytes accessed | tf_op | source)
XLA Modules:
  0.0 220.2 jit_solution(5332347672173056253)
XLA Ops:
  0.6 2.3 %shard_map.95 = (bf16[128,1408]{1,0:T(8,128)(2,1)}, bf16[128,128]{1,0:T(8,128)(2,1)}) custom-call(bf16[128,1408]{1,0:T(8,128)(2,1)} %bitcast.22, s32[1,128]{1,0:T(1,128)} %context_ref.1), custom_call_target="tpu_custom_call" | custom-call | flops 1000000 | bytes 1000000 | tf_op jit(solution)/shard_map/pallas_call | solution.py:311
  2.9 3.3 %shard_map.97 = bf16[8,176,768]{2,1,0:T(8,128)(2,1)} custom-call(s32[1]{0:T(128)} %bitcast.2.z_ref, s32[1]{0:T(128)} %bitcast.core_ref, bf16[3,176,704]{2,1,0:T(8,128)(2,1)} %target_ref, bf16[3,176,704]{2,1,0:T(8,128)(2,1)} %student_ref.1, bf16[176,704]{1,0:T(8,128)(2,1)} %bitcast.26), custom_call_target="tpu_custom_call" | custom-call | flops 1000000 | bytes 1000000 | tf_op jit(solution)/shard_map/pallas_call | solution.py:342
  6.2 6.0 %all-to-all-start = ((bf16[8,176,768]{2,1,0:T(8,128)(2,1)}), bf16[8,176,768]{2,1,0:T(8,128)(2,1)S(1)}, u32[]{:S(2)}, u32[]{:S(2)}) async-start(bf16[8,176,768]{2,1,0:T(8,128)(2,1)} %shard_map.97), calls=%async_computation | async-start | bytes 4325376 | tf_op jit(solution)/shard_map/all_to_all | solution.py:66
  12.2 0.7 reshape.51.mask_ref
  12.9 0.8 multiply_cosine_fusion.1
  13.7 2.2 fusion
  15.9 6.9 %shard_map.96 = (bf16[1024,704]{1,0:T(8,128)(2,1)}, bf16[1024,704]{1,0:T(8,128)(2,1)}) custom-call(f32[128,704]{1,0:T(8,128)} %get-tuple-element.59.sin_ref, f32[128,704]{1,0:T(8,128)} %get-tuple-element.58.cos_ref, f32[8,704]{1,0:T(8,128)} %get-tuple-element.57.bsin_ref, f32[8,704]{1,0:T(8,128)} %get-tuple-element.56.bcos_ref, f32[2,704]{1,0:T(2,128)} %reshape.51.mask_ref), custom_call_target="tpu_custom_call" | custom-call | flops 1000000 | bytes 1000000 | tf_op jit(solution)/shard_map/pallas_call | solution.py:328
  22.8 17.2 %all-to-all-done = bf16[8,176,768]{2,1,0:T(8,128)(2,1)S(1)} async-done(((bf16[8,176,768]{2,1,0:T(8,128)(2,1)}), bf16[8,176,768]{2,1,0:T(8,128)(2,1)S(1)}, u32[]{:S(2)}, u32[]{:S(2)}) %all-to-all-start) | async-done | bytes 2162720 | tf_op jit(solution)/shard_map/all_to_all | solution.py:66
  40.0 0.8 collective-permute-start.8
  40.8 1.6 collective-permute-start
  42.5 3.9 %collective-permute-start.1 = (bf16[128,1408]{1,0:T(8,128)(2,1)S(1)}, bf16[128,1408]{1,0:T(8,128)(2,1)S(1)}, u32[]{:S(2)}, u32[]{:S(2)}) collective-permute-start(bf16[128,1408]{1,0:T(8,128)(2,1)S(1)} %copy-done.6), channel_id=1, source_target_pairs={{0,224},{32,0},{64,32},{96,64},{128,96},{160,128},{192,160},{224,1... | collective-permute-start | bytes 1081352 | tf_op jit(solution)/shard_map/ppermute | solution.py:293
  46.4 0.4 collective-permute-start.2
  46.8 0.8 collective-permute-done.2
  47.7 0.6 pad_add_fusion.listed_ref
  48.3 6.8 %collective-permute-done.refs_1_ = bf16[128,1408]{1,0:T(8,128)(2,1)S(1)} collective-permute-done((bf16[128,1408]{1,0:T(8,128)(2,1)S(1)}, bf16[128,1408]{1,0:T(8,128)(2,1)S(1)}, u32[]{:S(2)}, u32[]{:S(2)}) %collective-permute-start) | collective-permute-done | bytes 360480 | tf_op jit(solution)/shard_map/ppermute | solution.py:292
  55.1 0.1 collective-permute-start.3
  55.2 2.7 %collective-permute-start.4 = (bf16[128,1408]{1,0:T(8,128)(2,1)S(1)}, bf16[128,1408]{1,0:T(8,128)(2,1)S(1)}, u32[]{:S(2)}, u32[]{:S(2)}) collective-permute-start(bf16[128,1408]{1,0:T(8,128)(2,1)S(1)} %collective-permute-done.1.refs_7_), channel_id=1, source_target_pairs={{0,224},{32,0},{64,32},{96,64},{128,96},{160,128},{192,160},{224,1... | collective-permute-start | bytes 1081352 | tf_op jit(solution)/shard_map/ppermute | solution.py:293
  57.8 7.8 %collective-permute-done.3.refs_2_ = bf16[128,1408]{1,0:T(8,128)(2,1)S(1)} collective-permute-done((bf16[128,1408]{1,0:T(8,128)(2,1)S(1)}, bf16[128,1408]{1,0:T(8,128)(2,1)S(1)}, u32[]{:S(2)}, u32[]{:S(2)}) %collective-permute-start.3) | collective-permute-done | bytes 360480 | tf_op jit(solution)/shard_map/ppermute | solution.py:292
  65.7 1.0 collective-permute-start.5
  66.7 1.8 collective-permute-start.7
  68.4 7.0 %collective-permute-done.5.refs_3_ = bf16[128,1408]{1,0:T(8,128)(2,1)S(1)} collective-permute-done((bf16[128,1408]{1,0:T(8,128)(2,1)S(1)}, bf16[128,1408]{1,0:T(8,128)(2,1)S(1)}, u32[]{:S(2)}, u32[]{:S(2)}) %collective-permute-start.5) | collective-permute-done | bytes 360480 | tf_op jit(solution)/shard_map/ppermute | solution.py:292
  75.5 0.7 copy-done.11
  76.2 8.0 %collective-permute-done.6.refs_4_ = bf16[128,1408]{1,0:T(8,128)(2,1)S(1)} collective-permute-done((bf16[128,1408]{1,0:T(8,128)(2,1)S(1)}, bf16[128,1408]{1,0:T(8,128)(2,1)S(1)}, u32[]{:S(2)}, u32[]{:S(2)}) %collective-permute-start.6) | collective-permute-done | bytes 360480 | tf_op jit(solution)/shard_map/ppermute | solution.py:296
  84.3 0.7 copy-done.13
  85.0 5.3 %shard_map.98 = (bf16[8,96,128]{2,1,0:T(8,128)(2,1)}, bf16[1024,256]{1,0:T(8,128)(2,1)}, bf16[256,256]{1,0:T(8,128)(2,1)}) custom-call(s32[1]{0:T(128)} %bitcast.2.z_ref, s32[1]{0:T(128)} %bitcast.core_ref, bf16[128,1408]{1,0:T(8,128)(2,1)} %get-tuple-element.28.refs_0_, bf16[128,1408]{1,0:T(8,128)(2,1)} %copy-done.7, bf16[128,1408]{1,0:T(8,128)(2,1)} %copy-done.9, ...), custom_call_target="tpu_custom_call" | custom-call | flops 1000000 | bytes 1000000 | tf_op jit(solution)/shard_map/pallas_call | solution.py:359
  90.3 3.2 %collective-permute-start.10 = (bf16[256,256]{1,0:T(8,128)(2,1)}, bf16[256,256]{1,0:T(8,128)(2,1)S(1)}, u32[]{:S(2)}, u32[]{:S(2)}) collective-permute-start(bf16[256,256]{1,0:T(8,128)(2,1)} %get-tuple-element.39.kvs_ref), channel_id=1, source_target_pairs={{0,16},{16,0},{1,17},{17,1},{2,18},{18,2},{3,19},{19,3},{4,20},{20... | collective-permute-start | bytes 393224 | tf_op jit(solution)/shard_map/ppermute | solution.py:374
  93.5 0.2 collective-permute-start.9
  93.7 4.5 %shard_map.100.query_ref = bf16[1024,128]{1,0:T(8,128)(2,1)} custom-call(s32[1]{0:T(128)} %bitcast.core_ref, bf16[1024,704]{1,0:T(8,128)(2,1)} %get-tuple-element.40.lower_ref, bf16[1024,704]{1,0:T(8,128)(2,1)} %get-tuple-element.32.upper_ref, bf16[1408,768]{1,0:T(8,128)(2,1)} %bitcast.17, bf16[1408,768]{1,0:T(8,128)(2,1)} %collective-permute-done.8.refs_9_.other_ref), custom_call_target="tpu_custom_call" | custom-call | flops 1000000 | bytes 1000000 | tf_op jit(solution)/shard_map/pallas_call | solution.py:377
  98.2 0.6 copy-done.17
  98.9 3.1 %shard_map.101 = bf16[8,128,128]{2,1,0:T(8,128)(2,1)} custom-call(s32[1]{0:T(128)} %bitcast.core_ref, bf16[1024,128]{1,0:T(8,128)(2,1)} %shard_map.100.query_ref, bf16[256,256]{1,0:T(8,128)(2,1)} %get-tuple-element.39.kvs_ref, bf16[256,256]{1,0:T(8,128)(2,1)} %copy-done.17, s32[1,384]{1,0:T(1,128)} %pad_add_fusion.listed_ref), custom_call_target="tpu_custom_call" | custom-call | flops 1000000 | bytes 1000000 | tf_op jit(solution)/shard_map/pallas_call | solution.py:385
  102.0 4.4 %all-to-all-start.1 = ((bf16[8,128,128]{2,1,0:T(8,128)(2,1)}), bf16[8,128,128]{2,1,0:T(8,128)(2,1)S(1)}, u32[]{:S(2)}, u32[]{:S(2)}) async-start(bf16[8,128,128]{2,1,0:T(8,128)(2,1)} %shard_map.101), calls=%async_computation.1 | async-start | bytes 524288 | tf_op jit(solution)/shard_map/all_to_all | solution.py:66
  106.4 0.0 copy-start.5
  106.4 0.8 copy-done.5
  107.2 5.3 %shard_map.99 = bf16[8,96,128]{2,1,0:T(8,128)(2,1)} custom-call(bf16[8,96,128]{2,1,0:T(8,128)(2,1)} %get-tuple-element.37.query_ref, bf16[1024,256]{1,0:T(8,128)(2,1)} %get-tuple-element.38.kv_ref, bf16[1024,256]{1,0:T(8,128)(2,1)} %copy-done.5), custom_call_target="tpu_custom_call" | custom-call | flops 1000000 | bytes 1000000 | tf_op jit(solution)/shard_map/pallas_call | solution.py:389
  112.5 5.1 %all-to-all-done.1.got_ref = bf16[8,128,128]{2,1,0:T(8,128)(2,1)S(1)} async-done(((bf16[8,128,128]{2,1,0:T(8,128)(2,1)}), bf16[8,128,128]{2,1,0:T(8,128)(2,1)S(1)}, u32[]{:S(2)}, u32[]{:S(2)}) %all-to-all-start.1) | async-done | bytes 262176 | tf_op jit(solution)/shard_map/all_to_all | solution.py:66
  117.6 3.4 %all-to-all-start.2 = ((bf16[8,96,128]{2,1,0:T(8,128)(2,1)}), bf16[8,96,128]{2,1,0:T(8,128)(2,1)S(1)}, u32[]{:S(2)}, u32[]{:S(2)}) async-start(bf16[8,96,128]{2,1,0:T(8,128)(2,1)} %shard_map.99), calls=%async_computation.2 | async-start | bytes 393216 | tf_op jit(solution)/shard_map/all_to_all | solution.py:66
  121.1 0.8 multiply_reduce_fusion
  121.9 3.9 %shard_map.102 = (bf16[48,1408]{1,0:T(8,128)(2,1)}, bf16[48,1408]{1,0:T(8,128)(2,1)}, bf16[8,96,768]{2,1,0:T(8,128)(2,1)}, f32[48,128]{1,0:T(8,128)}) custom-call(s32[1]{0:T(128)} %bitcast.1.grp_ref, s32[1]{0:T(128)} %bitcast.core_ref, bf16[8,128,128]{2,1,0:T(8,128)(2,1)} %copy-done.2, bf16[128,128]{1,0:T(8,128)(2,1)} %get-tuple-element.42.perm_ref, ...), custom_call_target="tpu_custom_call" | custom-call | flops 1000000 | bytes 1000000 | tf_op jit(solution)/shard_map/pallas_call | solution.py:391
  125.8 3.8 %all-to-all-done.2.got_ref = bf16[8,96,128]{2,1,0:T(8,128)(2,1)S(1)} async-done(((bf16[8,96,128]{2,1,0:T(8,128)(2,1)}), bf16[8,96,128]{2,1,0:T(8,128)(2,1)S(1)}, u32[]{:S(2)}, u32[]{:S(2)}) %all-to-all-start.2) | async-done | bytes 196640 | tf_op jit(solution)/shard_map/all_to_all | solution.py:66
  129.5 6.0 %all-to-all-start.3 = ((bf16[8,96,768]{2,1,0:T(8,128)(2,1)}), bf16[8,96,768]{2,1,0:T(8,128)(2,1)S(1)}, u32[]{:S(2)}, u32[]{:S(2)}) async-start(bf16[8,96,768]{2,1,0:T(8,128)(2,1)} %get-tuple-element.50), calls=%async_computation.3 | async-start | bytes 2359296 | tf_op jit(solution)/shard_map/all_to_all | solution.py:66
  135.6 0.6 multiply_sine_fusion
  136.2 2.7 %collective-permute-start.11 = (bf16[48,1408]{1,0:T(8,128)(2,1)S(1)}, bf16[48,1408]{1,0:T(8,128)(2,1)S(1)}, u32[]{:S(2)}, u32[]{:S(2)}) collective-permute-start(bf16[48,1408]{1,0:T(8,128)(2,1)S(1)} %copy-done.20), channel_id=1, source_target_pairs={{0,8},{8,0},{1,9},{9,1},{2,10},{10,2},{3,11},{11,3},{4,12},{12,4},... | collective-permute-start | bytes 405512 | tf_op jit(solution)/shard_map/ppermute | solution.py:408
  138.9 0.8 maximum_add_fusion.seeds_ref
  139.7 6.3 %collective-permute-done.11.got_s_ref = bf16[48,1408]{1,0:T(8,128)(2,1)S(1)} collective-permute-done((bf16[48,1408]{1,0:T(8,128)(2,1)S(1)}, bf16[48,1408]{1,0:T(8,128)(2,1)S(1)}, u32[]{:S(2)}, u32[]{:S(2)}) %collective-permute-start.11) | collective-permute-done | bytes 135200 | tf_op jit(solution)/shard_map/ppermute | solution.py:408
  146.0 3.0 %shard_map.103 = (bf16[48,1408]{1,0:T(8,128)(2,1)}, bf16[48,1408]{1,0:T(8,128)(2,1)}) custom-call(s32[1]{0:T(128)} %bitcast.1.grp_ref, bf16[8,96,128]{2,1,0:T(8,128)(2,1)} %copy-done.3, bf16[704,1408]{1,0:T(8,128)(2,1)} %target_ref.1), custom_call_target="tpu_custom_call" | custom-call | flops 1000000 | bytes 1000000 | tf_op jit(solution)/shard_map/pallas_call | solution.py:409
  149.0 3.5 %collective-permute-start.12 = (bf16[48,1408]{1,0:T(8,128)(2,1)}, bf16[48,1408]{1,0:T(8,128)(2,1)S(1)}, u32[]{:S(2)}, u32[]{:S(2)}) collective-permute-start(bf16[48,1408]{1,0:T(8,128)(2,1)} %get-tuple-element.46), channel_id=1, source_target_pairs={{0,8},{8,0},{1,9},{9,1},{2,10},{10,2},{3,11},{11,3},{4,12},{12,4},... | collective-permute-start | bytes 405512 | tf_op jit(solution)/shard_map/ppermute | solution.py:415
  152.5 1.6 fusion.2.tokens_ref
  154.1 2.2 collective-permute-done.12.got_ref
  156.3 0.6 copy-done.16
  157.0 2.7 %shard_map.104 = bf16[16,48,256]{2,1,0:T(8,128)(2,1)} custom-call(bf16[48,1408]{1,0:T(8,128)(2,1)} %get-tuple-element.45.keep_ref, bf16[48,1408]{1,0:T(8,128)(2,1)} %copy-done.16, bf16[48,1408]{1,0:T(8,128)(2,1)} %get-tuple-element.47.keep_s_ref, bf16[48,1408]{1,0:T(8,128)(2,1)} %copy-done.15, f32[48,1408]{1,0:T(8,128)} %fusion.2.tokens_ref, ...), custom_call_target="tpu_custom_call" | custom-call | flops 1000000 | bytes 1000000 | tf_op jit(solution)/shard_map/pallas_call | solution.py:418
  159.7 12.3 %all-to-all-start.4 = ((bf16[16,48,256]{2,1,0:T(8,128)(2,1)}), bf16[16,48,256]{2,1,0:T(8,128)(2,1)S(1)}, u32[]{:S(2)}, u32[]{:S(2)}) async-start(bf16[16,48,256]{2,1,0:T(8,128)(2,1)} %shard_map.104), calls=%async_computation.4 | async-start | bytes 786432 | tf_op jit(solution)/shard_map/all_to_all | solution.py:422
  171.9 8.4 %all-to-all-done.4 = bf16[16,48,256]{2,1,0:T(8,128)(2,1)S(1)} async-done(((bf16[16,48,256]{2,1,0:T(8,128)(2,1)}), bf16[16,48,256]{2,1,0:T(8,128)(2,1)S(1)}, u32[]{:S(2)}, u32[]{:S(2)}) %all-to-all-start.4) | async-done | bytes 393248 | tf_op jit(solution)/shard_map/all_to_all | solution.py:422
  180.4 0.5 fusion.6
  181.0 3.1 %collective-permute-start.13 = (f32[128,768]{1,0:T(8,128)S(1)}, f32[128,768]{1,0:T(8,128)S(1)}, u32[]{:S(2)}, u32[]{:S(2)}) collective-permute-start(f32[128,768]{1,0:T(8,128)S(1)} %slice_select_fusion), channel_id=1, source_target_pairs={{0,16},{16,0},{1,17},{17,1},{2,18},{18,2},{3,19},{19,3},{4,20},{20... | collective-permute-start | bytes 1179656 | tf_op jit(solution)/shard_map/ppermute | solution.py:432
  184.1 1.3 collective-permute-done.13
  185.4 0.7 add_convert_fusion
  186.1 3.4 %all-to-all-start.5 = ((bf16[8,16,768]{2,1,0:T(8,128)(2,1)}), bf16[8,16,768]{2,1,0:T(8,128)(2,1)S(1)}, u32[]{:S(2)}, u32[]{:S(2)}) async-start(bf16[8,16,768]{2,1,0:T(8,128)(2,1)} %bitcast.8), calls=%async_computation.5 | async-start | bytes 393216 | tf_op jit(solution)/shard_map/all_to_all | solution.py:66
  189.5 8.8 %shard_map.105 = f32[704,1408]{1,0:T(8,128)} custom-call(s32[1]{0:T(128)} %bitcast.core_ref, bf16[704,1408]{1,0:T(8,128)(2,1)} %target_ref.1, bf16[1408,768]{1,0:T(8,128)(2,1)} %bitcast.19, bf16[1408,768]{1,0:T(8,128)(2,1)} %collective-permute-done.8.refs_9_.other_ref), custom_call_target="tpu_custom_call" | custom-call | flops 1000000 | bytes 1000000 | tf_op jit(solution)/shard_map/pallas_call | solution.py:436
  198.4 1.1 all-to-all-done.5
  199.5 14.3 %all_to_all.35 = bf16[8,16,768]{2,1,0:T(8,128)(2,1)S(1)} all-to-all(bf16[8,16,768]{2,1,0:T(8,128)(2,1)S(1)} %broadcast_in_dim.2), channel_id=1, replica_groups=mesh['z'=8,'core'=2,'grp'=2,'ylo'=2,'x'=4] {'z'}, dimensions={0} | all-to-all | bytes 393216 | tf_op jit(solution)/shard_map/all_to_all | solution.py:62
  213.8 2.4 %collective-permute-start.14 = (bf16[128,768]{1,0:T(8,128)(2,1)S(1)}, bf16[128,768]{1,0:T(8,128)(2,1)S(1)}, u32[]{:S(2)}, u32[]{:S(2)}) collective-permute-start(bf16[128,768]{1,0:T(8,128)(2,1)S(1)} %bitcast.23), channel_id=1, source_target_pairs={{0,16},{16,0},{1,17},{17,1},{2,18},{18,2},{3,19},{19,3},{4,20},{20... | collective-permute-start | bytes 589832 | tf_op jit(solution)/shard_map/ppermute | solution.py:445
  216.2 1.1 collective-permute-done.14.other_ref
  217.3 0.7 copy-done.14
  218.0 2.2 shard_map.106
  (49 shorter events, 0.2 us)
Async XLA Ops:
  6.2 6.0 %copy-start.18 = (f32[1408]{0:T(1024)S(1)}, f32[1408]{0:T(1024)}, u32[]{:S(2)}) copy-start(f32[1408]{0:T(1024)} %param.15) | copy-start | bytes 16900
  6.2 33.8 %all-to-all-start = ((bf16[8,176,768]{2,1,0:T(8,128)(2,1)}), bf16[8,176,768]{2,1,0:T(8,128)(2,1)S(1)}, u32[]{:S(2)}, u32[]{:S(2)}) async-start(bf16[8,176,768]{2,1,0:T(8,128)(2,1)} %shard_map.97), calls=%async_computation | async-start | bytes 4325376 | tf_op jit(solution)/shard_map/all_to_all | solution.py:66
  12.2 28.6 %copy-start.6 = (bf16[128,1408]{1,0:T(8,128)(2,1)S(1)}, bf16[128,1408]{1,0:T(8,128)(2,1)}, u32[]{:S(2)}) copy-start(bf16[128,1408]{1,0:T(8,128)(2,1)} %get-tuple-element.28.refs_0_) | copy-start | bytes 1081348
  12.2 34.2 %copy-start.19 = (s32[1,192]{1,0:T(1,128)S(1)}, s32[1,192]{1,0:T(1,128)}, u32[]{:S(2)}) copy-start(s32[1,192]{1,0:T(1,128)} %param.10) | copy-start | bytes 2308
  40.0 45.0 %copy-start = (bf16[8,176,768]{2,1,0:T(8,128)(2,1)}, bf16[8,176,768]{2,1,0:T(8,128)(2,1)S(1)}, u32[]{:S(2)}) copy-start(bf16[8,176,768]{2,1,0:T(8,128)(2,1)S(1)} %all-to-all-done) | copy-start | bytes 6488068
  40.0 45.0 %collective-permute-start.8 = (bf16[1408,768]{1,0:T(8,128)(2,1)S(1)}, bf16[1408,768]{1,0:T(8,128)(2,1)}, u32[]{:S(2)}, u32[]{:S(2)}) collective-permute-start(bf16[1408,768]{1,0:T(8,128)(2,1)S(1)} %bitcast.15), channel_id=1, source_target_pairs={{0,16},{16,0},{1,17},{17,1},{2,18},{18,2},{3,19},{19,3},{4,20},{20... | collective-permute-start | bytes 6488072 | tf_op jit(solution)/shard_map/ppermute | solution.py:348
  40.8 14.3 %collective-permute-start = (bf16[128,1408]{1,0:T(8,128)(2,1)S(1)}, bf16[128,1408]{1,0:T(8,128)(2,1)S(1)}, u32[]{:S(2)}, u32[]{:S(2)}) collective-permute-start(bf16[128,1408]{1,0:T(8,128)(2,1)S(1)} %copy-done.6), channel_id=1, source_target_pairs={{0,32},{32,64},{64,96},{96,128},{128,160},{160,192},{192,224},{224... | collective-permute-start | bytes 1081352 | tf_op jit(solution)/shard_map/ppermute | solution.py:292
  42.5 12.6 %collective-permute-start.1 = (bf16[128,1408]{1,0:T(8,128)(2,1)S(1)}, bf16[128,1408]{1,0:T(8,128)(2,1)S(1)}, u32[]{:S(2)}, u32[]{:S(2)}) collective-permute-start(bf16[128,1408]{1,0:T(8,128)(2,1)S(1)} %copy-done.6), channel_id=1, source_target_pairs={{0,224},{32,0},{64,32},{96,64},{128,96},{160,128},{192,160},{224,1... | collective-permute-start | bytes 1081352 | tf_op jit(solution)/shard_map/ppermute | solution.py:293
  46.4 1.3 collective-permute-start.2
  55.1 29.9 %copy-start.7 = (bf16[128,1408]{1,0:T(8,128)(2,1)}, bf16[128,1408]{1,0:T(8,128)(2,1)S(1)}, u32[]{:S(2)}) copy-start(bf16[128,1408]{1,0:T(8,128)(2,1)S(1)} %collective-permute-done.refs_1_) | copy-start | bytes 1081348
  55.1 29.9 %copy-start.8 = (bf16[128,1408]{1,0:T(8,128)(2,1)}, bf16[128,1408]{1,0:T(8,128)(2,1)S(1)}, u32[]{:S(2)}) copy-start(bf16[128,1408]{1,0:T(8,128)(2,1)S(1)} %collective-permute-done.1.refs_7_) | copy-start | bytes 1081348
  55.1 10.6 %collective-permute-start.3 = (bf16[128,1408]{1,0:T(8,128)(2,1)S(1)}, bf16[128,1408]{1,0:T(8,128)(2,1)S(1)}, u32[]{:S(2)}, u32[]{:S(2)}) collective-permute-start(bf16[128,1408]{1,0:T(8,128)(2,1)S(1)} %collective-permute-done.refs_1_), channel_id=1, source_target_pairs={{0,32},{32,64},{64,96},{96,128},{128,160},{160,192},{192,224},{224... | collective-permute-start | bytes 1081352 | tf_op jit(solution)/shard_map/ppermute | solution.py:292
  55.2 10.5 %collective-permute-start.4 = (bf16[128,1408]{1,0:T(8,128)(2,1)S(1)}, bf16[128,1408]{1,0:T(8,128)(2,1)S(1)}, u32[]{:S(2)}, u32[]{:S(2)}) collective-permute-start(bf16[128,1408]{1,0:T(8,128)(2,1)S(1)} %collective-permute-done.1.refs_7_), channel_id=1, source_target_pairs={{0,224},{32,0},{64,32},{96,64},{128,96},{160,128},{192,160},{224,1... | collective-permute-start | bytes 1081352 | tf_op jit(solution)/shard_map/ppermute | solution.py:293
  65.7 19.3 %copy-start.9 = (bf16[128,1408]{1,0:T(8,128)(2,1)}, bf16[128,1408]{1,0:T(8,128)(2,1)S(1)}, u32[]{:S(2)}) copy-start(bf16[128,1408]{1,0:T(8,128)(2,1)S(1)} %collective-permute-done.3.refs_2_) | copy-start | bytes 1081348
  65.7 9.7 %copy-start.10 = (bf16[128,1408]{1,0:T(8,128)(2,1)}, bf16[128,1408]{1,0:T(8,128)(2,1)S(1)}, u32[]{:S(2)}) copy-start(bf16[128,1408]{1,0:T(8,128)(2,1)S(1)} %collective-permute-done.4.refs_6_) | copy-start | bytes 1081348
  65.7 9.7 %collective-permute-start.5 = (bf16[128,1408]{1,0:T(8,128)(2,1)S(1)}, bf16[128,1408]{1,0:T(8,128)(2,1)S(1)}, u32[]{:S(2)}, u32[]{:S(2)}) collective-permute-start(bf16[128,1408]{1,0:T(8,128)(2,1)S(1)} %collective-permute-done.3.refs_2_), channel_id=1, source_target_pairs={{0,32},{32,64},{64,96},{96,128},{128,160},{160,192},{192,224},{224... | collective-permute-start | bytes 1081352 | tf_op jit(solution)/shard_map/ppermute | solution.py:292
  66.7 8.8 %collective-permute-start.7 = (bf16[128,1408]{1,0:T(8,128)(2,1)S(1)}, bf16[128,1408]{1,0:T(8,128)(2,1)S(1)}, u32[]{:S(2)}, u32[]{:S(2)}) collective-permute-start(bf16[128,1408]{1,0:T(8,128)(2,1)S(1)} %collective-permute-done.4.refs_6_), channel_id=1, source_target_pairs={{0,224},{32,0},{64,32},{96,64},{128,96},{160,128},{192,160},{224,1... | collective-permute-start | bytes 1081352 | tf_op jit(solution)/shard_map/ppermute | solution.py:293
  75.4 0.8 copy-start.11
  75.4 8.8 %collective-permute-start.6 = (bf16[128,1408]{1,0:T(8,128)(2,1)S(1)}, bf16[128,1408]{1,0:T(8,128)(2,1)S(1)}, u32[]{:S(2)}, u32[]{:S(2)}) collective-permute-start(bf16[128,1408]{1,0:T(8,128)(2,1)S(1)} %collective-permute-done.5.refs_3_), channel_id=1, source_target_pairs={{0,32},{32,64},{64,96},{96,128},{128,160},{160,192},{192,224},{224... | collective-permute-start | bytes 1081352 | tf_op jit(solution)/shard_map/ppermute | solution.py:296
  76.2 8.0 %copy-start.12 = (bf16[128,1408]{1,0:T(8,128)(2,1)}, bf16[128,1408]{1,0:T(8,128)(2,1)S(1)}, u32[]{:S(2)}) copy-start(bf16[128,1408]{1,0:T(8,128)(2,1)S(1)} %collective-permute-done.7.refs_5_) | copy-start | bytes 1081348
  84.3 0.7 copy-start.13
  90.3 7.9 %collective-permute-start.10 = (bf16[256,256]{1,0:T(8,128)(2,1)}, bf16[256,256]{1,0:T(8,128)(2,1)S(1)}, u32[]{:S(2)}, u32[]{:S(2)}) collective-permute-start(bf16[256,256]{1,0:T(8,128)(2,1)} %get-tuple-element.39.kvs_ref), channel_id=1, source_target_pairs={{0,16},{16,0},{1,17},{17,1},{2,18},{18,2},{3,19},{19,3},{4,20},{20... | collective-permute-start | bytes 393224 | tf_op jit(solution)/shard_map/ppermute | solution.py:374
  93.5 12.9 %collective-permute-start.9 = (bf16[1024,256]{1,0:T(8,128)(2,1)}, bf16[1024,256]{1,0:T(8,128)(2,1)S(1)}, u32[]{:S(2)}, u32[]{:S(2)}) collective-permute-start(bf16[1024,256]{1,0:T(8,128)(2,1)} %get-tuple-element.38.kv_ref), channel_id=1, source_target_pairs={{0,16},{16,0},{1,17},{17,1},{2,18},{18,2},{3,19},{19,3},{4,20},{20... | collective-permute-start | bytes 1572872 | tf_op jit(solution)/shard_map/ppermute | solution.py:375
  98.2 0.6 copy-start.17
  102.0 15.7 %all-to-all-start.1 = ((bf16[8,128,128]{2,1,0:T(8,128)(2,1)}), bf16[8,128,128]{2,1,0:T(8,128)(2,1)S(1)}, u32[]{:S(2)}, u32[]{:S(2)}) async-start(bf16[8,128,128]{2,1,0:T(8,128)(2,1)} %shard_map.101), calls=%async_computation.1 | async-start | bytes 524288 | tf_op jit(solution)/shard_map/all_to_all | solution.py:66
  106.4 0.8 copy-start.5
  117.6 4.2 %copy-start.2 = (bf16[8,128,128]{2,1,0:T(8,128)(2,1)}, bf16[8,128,128]{2,1,0:T(8,128)(2,1)S(1)}, u32[]{:S(2)}) copy-start(bf16[8,128,128]{2,1,0:T(8,128)(2,1)S(1)} %all-to-all-done.1.got_ref) | copy-start | bytes 786436
  117.6 11.9 %all-to-all-start.2 = ((bf16[8,96,128]{2,1,0:T(8,128)(2,1)}), bf16[8,96,128]{2,1,0:T(8,128)(2,1)S(1)}, u32[]{:S(2)}, u32[]{:S(2)}) async-start(bf16[8,96,128]{2,1,0:T(8,128)(2,1)} %shard_map.99), calls=%async_computation.2 | async-start | bytes 393216 | tf_op jit(solution)/shard_map/all_to_all | solution.py:66
  125.8 10.4 %copy-start.20 = (bf16[48,1408]{1,0:T(8,128)(2,1)S(1)}, bf16[48,1408]{1,0:T(8,128)(2,1)}, u32[]{:S(2)}) copy-start(bf16[48,1408]{1,0:T(8,128)(2,1)} %get-tuple-element.43) | copy-start | bytes 405508
  129.5 10.2 %copy-start.3 = (bf16[8,96,128]{2,1,0:T(8,128)(2,1)}, bf16[8,96,128]{2,1,0:T(8,128)(2,1)S(1)}, u32[]{:S(2)}) copy-start(bf16[8,96,128]{2,1,0:T(8,128)(2,1)S(1)} %all-to-all-done.2.got_ref) | copy-start | bytes 589828
  129.5 30.1 %all-to-all-start.3 = ((bf16[8,96,768]{2,1,0:T(8,128)(2,1)}), bf16[8,96,768]{2,1,0:T(8,128)(2,1)S(1)}, u32[]{:S(2)}, u32[]{:S(2)}) async-start(bf16[8,96,768]{2,1,0:T(8,128)(2,1)} %get-tuple-element.50), calls=%async_computation.3 | async-start | bytes 2359296 | tf_op jit(solution)/shard_map/all_to_all | solution.py:66
  135.6 17.0 %copy-start.1 = (bf16[1,128,1408]{2,1,0:T(8,128)(2,1)S(1)}, bf16[1,128,1408]{2,1,0:T(8,128)(2,1)}, u32[]{:S(2)}) copy-start(bf16[1,128,1408]{2,1,0:T(8,128)(2,1)} %param.8) | copy-start | bytes 1081348
  136.2 9.8 %collective-permute-start.11 = (bf16[48,1408]{1,0:T(8,128)(2,1)S(1)}, bf16[48,1408]{1,0:T(8,128)(2,1)S(1)}, u32[]{:S(2)}, u32[]{:S(2)}) collective-permute-start(bf16[48,1408]{1,0:T(8,128)(2,1)S(1)} %copy-done.20), channel_id=1, source_target_pairs={{0,8},{8,0},{1,9},{9,1},{2,10},{10,2},{3,11},{11,3},{4,12},{12,4},... | collective-permute-start | bytes 405512 | tf_op jit(solution)/shard_map/ppermute | solution.py:408
  146.0 10.3 %copy-start.15 = (bf16[48,1408]{1,0:T(8,128)(2,1)}, bf16[48,1408]{1,0:T(8,128)(2,1)S(1)}, u32[]{:S(2)}) copy-start(bf16[48,1408]{1,0:T(8,128)(2,1)S(1)} %collective-permute-done.11.got_s_ref) | copy-start | bytes 405508
  149.0 7.4 %collective-permute-start.12 = (bf16[48,1408]{1,0:T(8,128)(2,1)}, bf16[48,1408]{1,0:T(8,128)(2,1)S(1)}, u32[]{:S(2)}, u32[]{:S(2)}) collective-permute-start(bf16[48,1408]{1,0:T(8,128)(2,1)} %get-tuple-element.46), channel_id=1, source_target_pairs={{0,8},{8,0},{1,9},{9,1},{2,10},{10,2},{3,11},{11,3},{4,12},{12,4},... | collective-permute-start | bytes 405512 | tf_op jit(solution)/shard_map/ppermute | solution.py:415
  156.3 0.7 copy-start.16
  159.7 20.7 %all-to-all-start.4 = ((bf16[16,48,256]{2,1,0:T(8,128)(2,1)}), bf16[16,48,256]{2,1,0:T(8,128)(2,1)S(1)}, u32[]{:S(2)}, u32[]{:S(2)}) async-start(bf16[16,48,256]{2,1,0:T(8,128)(2,1)} %shard_map.104), calls=%async_computation.4 | async-start | bytes 786432 | tf_op jit(solution)/shard_map/all_to_all | solution.py:422
  181.0 4.5 %collective-permute-start.13 = (f32[128,768]{1,0:T(8,128)S(1)}, f32[128,768]{1,0:T(8,128)S(1)}, u32[]{:S(2)}, u32[]{:S(2)}) collective-permute-start(f32[128,768]{1,0:T(8,128)S(1)} %slice_select_fusion), channel_id=1, source_target_pairs={{0,16},{16,0},{1,17},{17,1},{2,18},{18,2},{3,19},{19,3},{4,20},{20... | collective-permute-start | bytes 1179656 | tf_op jit(solution)/shard_map/ppermute | solution.py:432
  186.1 13.3 %all-to-all-start.5 = ((bf16[8,16,768]{2,1,0:T(8,128)(2,1)}), bf16[8,16,768]{2,1,0:T(8,128)(2,1)S(1)}, u32[]{:S(2)}, u32[]{:S(2)}) async-start(bf16[8,16,768]{2,1,0:T(8,128)(2,1)} %bitcast.8), calls=%async_computation.5 | async-start | bytes 393216 | tf_op jit(solution)/shard_map/all_to_all | solution.py:66
  213.8 3.5 %copy-start.4 = (bf16[8,16,768]{2,1,0:T(8,128)(2,1)}, bf16[8,16,768]{2,1,0:T(8,128)(2,1)S(1)}, u32[]{:S(2)}) copy-start(bf16[8,16,768]{2,1,0:T(8,128)(2,1)S(1)} %all_to_all.35) | copy-start | bytes 589828
  213.8 3.5 %collective-permute-start.14 = (bf16[128,768]{1,0:T(8,128)(2,1)S(1)}, bf16[128,768]{1,0:T(8,128)(2,1)S(1)}, u32[]{:S(2)}, u32[]{:S(2)}) collective-permute-start(bf16[128,768]{1,0:T(8,128)(2,1)S(1)} %bitcast.23), channel_id=1, source_target_pairs={{0,16},{16,0},{1,17},{17,1},{2,18},{18,2},{3,19},{19,3},{4,20},{20... | collective-permute-start | bytes 589832 | tf_op jit(solution)/shard_map/ppermute | solution.py:445
  217.3 0.7 copy-start.14

commit v3 on v2

--- a/solution.py
+++ b/solution.py
@@ -88,7 +88,7 @@
     perm_ref[...] = perm
 
 
-def head_kernel(z_ref, core_ref, target_ref, student_ref, turned_ref, out_ref):
+def head_kernel(z_ref, core_ref, target_ref, student_ref, turned_ref, head_ref, out_ref):
     rows = target_ref.shape[2]
     half = turned_ref.shape[1] // 2
     col = z_ref[0] * HEAD_DIM + iota((rows, LANES), 1)
@@ -101,9 +101,9 @@
         rest = jnp.zeros((turned.shape[0], WIDE - half), BF)
         for d in range(N_DP):
             for k in range(3):
-                out_ref[d, :, k * LANES : (k + 1) * LANES] = got[k]
-            out_ref[d, :, WIDE : WIDE + half] = turned
-            out_ref[d, :, WIDE + half :] = rest
+                head_ref[d, :, k * LANES : (k + 1) * LANES] = got[k]
+            out_ref[d, :, :half] = turned
+            out_ref[d, :, half:] = rest
 
     pl.when(core_ref[0] == 0)(lambda: fill(target_ref, 0))
     pl.when(core_ref[0] == 1)(lambda: fill(student_ref, half))
@@ -141,21 +141,36 @@
 
 
 def project_kernel(z_ref, core_ref, *refs):
-    pieces = refs[:N_Z]
-    mine_ref, other_ref, query_ref, kv_ref, kvs_ref, rows_ref, ctx_ref, target_ref = refs[N_Z:]
-    for i in range(N_Z):
+    pieces = refs[: N_Z - 1]
+    mine_ref, other_ref, query_ref, kv_ref, kvs_ref, rows_ref, ctx_ref, target_ref = refs[N_Z - 1 :]
+    slots = [d for d in range(N_Z) if d != N_Z // 2]
+    for i in range(N_Z - 1):
         rows_ref[i * BLOCK : (i + 1) * BLOCK, :] = pieces[i][...]
         ctx_ref[i * CTX : (i + 1) * CTX, :] = pieces[i][:CTX, :]
     target_ref[...] = jnp.where(core_ref[0] == 0, mine_ref[...], other_ref[...])
     student = jnp.where(core_ref[0] == 0, other_ref[:, LANES:], mine_ref[:, LANES:])
     kvs_ref[...] = mm(ctx_ref[...], student).astype(BF)
-    for i in range(2):
-        rows = slice(i * 4 * BLOCK, (i + 1) * 4 * BLOCK)
+    for at, count in ((0, 4), (4, 3)):
+        rows = slice(at * BLOCK, (at + count) * BLOCK)
         got = mm(rows_ref[rows, :], target_ref[...]).astype(BF)
         kv_ref[rows, :] = got[:, LANES:]
-        for k in range(4):
-            dest = lax.rem(z_ref[0] - (4 * i + k) + N_Z, N_Z)
+        for k in range(count):
+            dest = lax.rem(z_ref[0] - slots[at + k] + N_Z, N_Z)
             query_ref[dest] = got[k * BLOCK + CTX : (k + 1) * BLOCK, :LANES]
+
+
+def project_last_kernel(
+    z_ref, core_ref, last_ref, early_ref, kvs_early_ref, mine_ref, other_ref, query_ref, kv_ref, kvs_ref
+):
+    early = (N_Z - 1) * CTX
+    target = jnp.where(core_ref[0] == 0, mine_ref[...], other_ref[...])
+    student = jnp.where(core_ref[0] == 0, other_ref[:, LANES:], mine_ref[:, LANES:])
+    kvs_ref[:early, :] = kvs_early_ref[...]
+    kvs_ref[early:, :] = mm(last_ref[:CTX, :], student).astype(BF)
+    got = mm(last_ref[...], target).astype(BF)
+    kv_ref[...] = got[:, LANES:]
+    query_ref[...] = early_ref[...]
+    query_ref[lax.rem(z_ref[0] + N_Z // 2, N_Z)] = got[CTX:, :LANES]
 
 
 def softmax_rows(query, pairs):
@@ -169,41 +184,35 @@
     return mixed / total
 
 
-def attend_target_kernel(query_ref, kv_ref, kv_other_ref, out_ref):
+def attention_kernel(
+    core_ref, query_ref, kv_ref, kv_other_ref, last_ref, last_other_ref, query_s_ref, kvs_ref,
+    kvs_other_ref, listed_ref, out_ref,
+):
     rows = 4 * TGT
     for i in range(2):
         query = query_ref[4 * i : 4 * i + 4].reshape(rows, LANES)
-        mixed = softmax_rows(query, (kv_ref, kv_other_ref)).astype(BF)
-        out_ref[4 * i : 4 * i + 4] = mixed.reshape(4, TGT, LANES)
-
-
-def attend_student_kernel(core_ref, query_ref, kvs_ref, kvs_other_ref, listed_ref, out_ref):
+        mixed = softmax_rows(query, (kv_ref, kv_other_ref, last_ref, last_other_ref)).astype(BF)
+        out_ref[4 * i : 4 * i + 4, :TGT, :] = mixed.reshape(4, TGT, LANES)
     rows = 4 * BLOCK
     lane = iota((rows, LANES), 1)
     slot = iota((rows, listed_ref.shape[1]), 0)
     for i in range(2):
-        mixed = softmax_rows(query_ref[i * rows : (i + 1) * rows, :], (kvs_ref, kvs_other_ref))
+        mixed = softmax_rows(query_s_ref[i * rows : (i + 1) * rows, :], (kvs_ref, kvs_other_ref))
         block = lax.div(slot, BLOCK)
         place = (2 * (4 * i + block) + core_ref[0]) * BLOCK + slot - block * BLOCK
         same = jnp.where(place == listed_ref[...], 1.0, 0.0)
         count = jnp.sum(same, axis=1, keepdims=True)
         mixed = jnp.where(lane == HEAD_DIM, count, mixed).astype(BF)
-        out_ref[4 * i : 4 * i + 4] = mixed.reshape(4, BLOCK, LANES)
-
-
-def divide(grp_ref, part_ref, keep_ref, send_ref):
-    mine = pl.multiple_of(grp_ref[0] * OWN, OWN)
-    other = pl.multiple_of((1 - grp_ref[0]) * OWN, OWN)
-    keep_ref[...] = part_ref[pl.ds(mine, OWN), :].astype(BF)
-    send_ref[...] = part_ref[pl.ds(other, OWN), :].astype(BF)
-
-
-def output_student_kernel(
-    grp_ref, core_ref, got_ref, perm_ref, mine_ref, other_ref, keep_ref, send_ref, mixed_ref,
-    count_ref, wide_ref, thin_ref, part_ref, all_count_ref,
+        out_ref[4 * i : 4 * i + 4, TGT:, :] = mixed.reshape(4, BLOCK, LANES)
+
+
+def output_kernel(
+    grp_ref, core_ref, got_ref, perm_ref, out_ref, mine_ref, other_ref, keep_ref, send_ref, mixed_ref,
+    count_ref, wide_ref, thin_ref, thin_t_ref, part_ref, all_count_ref,
 ):
     for h in range(N_Z):
-        wide_ref[:, h * LANES : (h + 1) * LANES] = got_ref[h]
+        wide_ref[:, h * LANES : (h + 1) * LANES] = got_ref[h, TGT:, :]
+        thin_t_ref[:, h * HEAD_DIM : (h + 1) * HEAD_DIM] = got_ref[h, :TGT, :HEAD_DIM].astype(F32)
     chosen = mm(perm_ref[CTX:, :], wide_ref[...])
     lane = lax.rem(iota(chosen.shape, 1), LANES)
     all_count_ref[...] = jnp.broadcast_to(
@@ -218,25 +227,23 @@
         mixed_ref[d] = mixed
     left = jnp.where(core_ref[0] == 0, mine_ref[...], other_ref[...])
     right = jnp.where(core_ref[0] == 0, other_ref[...], mine_ref[...])
-    part_ref[...] = mm_nt(mixed[:, :WIDE], left) + mm_nt(mixed[:, WIDE:], right)
-    divide(grp_ref, part_ref, keep_ref, send_ref)
-    count_ref[...] = all_count_ref[pl.ds(pl.multiple_of(grp_ref[0] * OWN, OWN), OWN), :]
-
-
-def output_target_kernel(grp_ref, got_ref, out_ref, keep_ref, send_ref, thin_ref, part_ref):
-    for h in range(N_Z):
-        thin_ref[:, h * HEAD_DIM : (h + 1) * HEAD_DIM] = got_ref[h, :, :HEAD_DIM].astype(F32)
-    part_ref[...] = mm(thin_ref[...].astype(BF), out_ref[...])
-    divide(grp_ref, part_ref, keep_ref, send_ref)
+    part_ref[:TGT, :] = mm(thin_t_ref[...].astype(BF), out_ref[...])
+    part_ref[TGT:, :] = mm_nt(mixed[:, :WIDE], left) + mm_nt(mixed[:, WIDE:], right)
+    mine = pl.multiple_of(grp_ref[0] * OWN, OWN)
+    other = pl.multiple_of((1 - grp_ref[0]) * OWN, OWN)
+    keep_ref[:OWN, :] = part_ref[pl.ds(mine, OWN), :].astype(BF)
+    keep_ref[OWN:, :] = part_ref[pl.ds(TGT + mine, OWN), :].astype(BF)
+    send_ref[:OWN, :] = part_ref[pl.ds(other, OWN), :].astype(BF)
+    send_ref[OWN:, :] = part_ref[pl.ds(TGT + other, OWN), :].astype(BF)
+    count_ref[...] = all_count_ref[pl.ds(mine, OWN), :]
 
 
 def slope_kernel(
-    keep_ref, got_ref, keep_s_ref, got_s_ref, tokens_ref, seeds_ref, count_ref, out_ref, back_ref
+    keep_ref, got_ref, tokens_ref, seeds_ref, count_ref, out_ref, back_ref
 ):
-    target_sum = keep_ref[...].astype(F32) + got_ref[...].astype(F32)
-    student_sum = keep_s_ref[...].astype(F32) + got_s_ref[...].astype(F32)
-    wanted = normalized(tokens_ref[...] + target_sum)[0].astype(BF).astype(F32)
-    predicted, factor = normalized(seeds_ref[...] + student_sum)
+    both = keep_ref[...].astype(F32) + got_ref[...].astype(F32)
+    wanted = normalized(tokens_ref[...] + both[:OWN])[0].astype(BF).astype(F32)
+    predicted, factor = normalized(seeds_ref[...] + both[OWN:])
     slope = jnp.clip(predicted - wanted, -1.0, 1.0) * count_ref[:, :1]
     back_ref[...] = (
         slope
@@ -339,13 +346,15 @@
     listed = jnp.concatenate([listed, lax.ppermute(listed, "core", SWAP)], axis=1)
     pieces = ring(moved, {2: (tables, listed), 3: (seed_a, seed_b)})
 
-    head = call(
-        head_kernel,
-        sds((N_DP, width // N_DP, 2 * WIDE), BF),
-        in_specs=[SMEM, SMEM] + [pl.BlockSpec()] * 3,
+    piece = sds((N_DP, width // N_DP, WIDE), BF)
+    head, turned = call(
+        head_kernel, (piece, piece), in_specs=[SMEM, SMEM] + [pl.BlockSpec()] * 3
     )(z_at, core_at, after(target_qkv, moved), student_qkv, student_out.T)
-    weights = after(exchange(head, DP), seed_a).reshape(width, 2 * WIDE)
+    weights = exchange(head, DP)
+    weights = after(weights, seed_a).reshape(width, WIDE)
     swapped = lax.ppermute(weights, "core", SWAP)
+    out_mine = exchange(after(turned, weights), DP).reshape(width, WIDE)
+    out_other = lax.ppermute(out_mine, "core", SWAP)
 
     rows_own = lax.dynamic_slice_in_dim(perm, CTX + grp * OWN, OWN, axis=0)
     tokens_own = mm(rows_own, tokens)
@@ -354,25 +363,6 @@
     angle = places_own[:, None] * spacing[None, :]
     seeds = mask_token[None, :] + jnp.concatenate([jnp.sin(angle), jnp.cos(angle)], axis=1)
 
-    head_w = pl.BlockSpec((width, WIDE), lambda i: (0, 0))
-    out_w = pl.BlockSpec((width, WIDE), lambda i: (0, 1))
-    query_t, kv, kvs = call(
-        project_kernel,
-        (
-            sds((N_Z, TGT, LANES), BF),
-            sds((N_Z * BLOCK, 2 * LANES), BF),
-            sds((N_Z * CTX, 2 * LANES), BF),
-        ),
-        scratch=(
-            pltpu.VMEM((N_Z * BLOCK, width), BF),
-            pltpu.VMEM((N_Z * CTX, width), BF),
-            pltpu.VMEM((width, WIDE), BF),
-        ),
-        grid=(1,),
-        in_specs=[SMEM, SMEM] + [pl.BlockSpec()] * N_Z + [head_w] * 2,
-    )(z_at, core_at, *pieces, weights, swapped)
-    kvs_other = lax.ppermute(kvs, "core", SWAP)
-    kv_other = lax.ppermute(kv, "core", SWAP)
     query_w = pl.BlockSpec((width, LANES), lambda j: (0, 0))
     query_s = call(
         seed_query_kernel,
@@ -380,44 +370,61 @@
         grid=(N_Z // 2,),
         in_specs=[SMEM] + [pl.BlockSpec((2 * BLOCK, half), lambda j: (j, 0))] * 2 + [query_w] * 2,
         out_specs=pl.BlockSpec((2 * BLOCK, LANES), lambda j: (j, 0)),
-    )(core_at, after(seed_a, kvs), seed_b, weights, swapped)
-
-    mixed_s = call(
-        attend_student_kernel, sds((N_Z, BLOCK, LANES), BF), in_specs=[SMEM] + [pl.BlockSpec()] * 4
-    )(core_at, query_s, kvs, kvs_other, listed)
-    mixed_s = exchange(mixed_s, "z")
-    mixed_t = call(attend_target_kernel, sds((N_Z, TGT, LANES), BF))(query_t, kv, kv_other)
-    mixed_t = exchange(after(mixed_t, mixed_s), "z")
-    keep_s, send_s, mixed_c, count = call(
-        output_student_kernel,
+    )(core_at, seed_a, seed_b, weights, swapped)
+    early = pieces[: N_Z // 2] + pieces[N_Z // 2 + 1 :]
+    query_t, kv, kvs = call(
+        project_kernel,
         (
-            sds((OWN, width), BF),
-            sds((OWN, width), BF),
+            sds((N_Z, TGT, LANES), BF),
+            sds(((N_Z - 1) * BLOCK, 2 * LANES), BF),
+            sds(((N_Z - 1) * CTX, 2 * LANES), BF),
+        ),
+        scratch=(
+            pltpu.VMEM(((N_Z - 1) * BLOCK, width), BF),
+            pltpu.VMEM(((N_Z - 1) * CTX, width), BF),
+            pltpu.VMEM((width, WIDE), BF),
+        ),
+        in_specs=[SMEM, SMEM] + [pl.BlockSpec()] * (N_Z + 1),
+    )(z_at, core_at, *early, after(weights, query_s), swapped)
+    kv_other = lax.ppermute(kv, "core", SWAP)
+    query_t, kv_last, kvs = call(
+        project_last_kernel,
+        (
+            sds((N_Z, TGT, LANES), BF),
+            sds((BLOCK, 2 * LANES), BF),
+            sds((N_Z * CTX, 2 * LANES), BF),
+        ),
+        in_specs=[SMEM, SMEM] + [pl.BlockSpec()] * 5,
+    )(z_at, core_at, pieces[N_Z // 2], query_t, kvs, weights, swapped)
+    kvs_other = lax.ppermute(kvs, "core", SWAP)
+    last_other = lax.ppermute(kv_last, "core", SWAP)
+    mixed = call(
+        attention_kernel, sds((N_Z, TGT + BLOCK, LANES), BF), in_specs=[SMEM] + [pl.BlockSpec()] * 9
+    )(core_at, query_t, kv, kv_other, kv_last, last_other, query_s, kvs, kvs_other, listed)
+    mixed = exchange(after(mixed, out_mine), "z")
+    keep, send, mixed_c, count = call(
+        output_kernel,
+        (
+            sds((2 * OWN, width), BF),
+            sds((2 * OWN, width), BF),
             sds((N_DP, TGT, 2 * WIDE), BF),
             sds((OWN, LANES), F32),
         ),
         scratch=(
             pltpu.VMEM((BLOCK, N_Z * LANES), BF),
             pltpu.VMEM((TGT, 2 * WIDE), F32),
-            pltpu.VMEM((TGT, width), F32),
+            pltpu.VMEM((TGT, N_Z * HEAD_DIM), F32),
+            pltpu.VMEM((2 * TGT, width), F32),
             pltpu.VMEM((TGT, LANES), F32),
         ),
-        grid=(1,),
-        in_specs=[SMEM, SMEM] + [pl.BlockSpec()] * 2 + [out_w] * 2,
-    )(grp_at, core_at, mixed_s, perm, weights, swapped)
-    got_s = lax.ppermute(send_s, "grp", SWAP)
-    keep, send = call(
-        output_target_kernel,
-        (sds((OWN, width), BF), sds((OWN, width), BF)),
-        scratch=(pltpu.VMEM((TGT, N_Z * HEAD_DIM), F32), pltpu.VMEM((TGT, width), F32)),
-        in_specs=[SMEM] + [pl.BlockSpec()] * 2,
-    )(grp_at, after(mixed_t, got_s), target_out)
+        in_specs=[SMEM, SMEM] + [pl.BlockSpec()] * 5,
+    )(grp_at, core_at, mixed, perm, target_out, out_mine, out_other)
     got = lax.ppermute(send, "grp", SWAP)
-    mixed_all = exchange(after(mixed_c, mixed_t), DP)
+    mixed_all = exchange(mixed_c, DP)
     mixed_all = mixed_all.reshape(N_DP * TGT, 2 * WIDE)
     stripes = call(
         slope_kernel, sds((2 * N_DP, OWN, 256), BF), scratch=(pltpu.VMEM((OWN, width), F32),)
-    )(keep, got, keep_s, got_s, tokens_own, seeds, count)
+    )(keep, got, tokens_own, seeds, count)
     stripes = after(stripes, mixed_all)
     arrived = lax.all_to_all(stripes, (*DP, "grp"), split_axis=0, concat_axis=0, tiled=True)
     grad = lax.dot_general(
@@ -432,14 +439,14 @@
     grad = grad_keep + lax.ppermute(grad_send, "core", SWAP)
     grad = grad.astype(BF).reshape(N_Z, 16, 2 * WIDE)
     pieces = exchange(grad, "z")
-    turned = pl.BlockSpec((LANES, WIDE), lambda i: (i, 1))
+    turned = pl.BlockSpec((LANES, WIDE), lambda i: (i, 0))
     target_blend = call(
         blend_kernel,
         sds((half, width), F32),
         grid=(width // LANES,),
         in_specs=[SMEM, pl.BlockSpec((half, LANES), lambda i: (0, i)), turned, turned],
         out_specs=pl.BlockSpec((half, LANES), lambda i: (0, i)),
-    )(core_at, after(target_out, grad), weights, swapped)
+    )(core_at, after(target_out, grad), out_mine, out_other)
     grad = jnp.sum(pieces.astype(F32), axis=0).astype(BF)
     grad = to_all(after(grad, target_blend), "z", N_Z).reshape(16 * N_Z, 2 * WIDE)
     other = lax.ppermute(grad, "core", SWAP)

time: 221 us -> 195 us (0.88)
  waiting for transfers between devices: 77.1 us -> 61.3 us
  starting transfers between devices: 63 us -> 54.3 us
    ppermute x1, waiting for transfers between devices: 2.19 us -> 15.8 us  [body(): got = lax.ppermute(send, 'grp', SWAP)]
    ppermute x4, waiting for transfers between devices: 29.7 us -> 16.1 us  [ring(): below = lax.ppermute(below, 'z', up)]
    all_to_all x5, waiting for transfers between devices: 27.2 us -> 16.9 us  [exchange(): return lax.all_to_all(pieces, axes, split_axis=0, concat_axis=0, tiled=True)]
    all_to_all x1, starting transfers between devices: 12.3 us -> 5.86 us  [body(): lax.all_to_all(stripes, (*DP, 'grp'), split_axis=0, concat_axis=0, tiled=...]
    ppermute x1 -> x2, waiting for transfers between devices: 6.29 us -> 1.14 us  [the longest x1 1.14 us: body(): last_other = lax.ppermute(kv_last, 'core', SWAP)]
    ppermute x1, starting transfers between devices: 3.24 us -> 0.15 us  [body(): kvs_other = lax.ppermute(kvs, 'core', SWAP)]
    pallas_call x6 -> x5, Pallas kernels: 23.8 us -> 22.2 us  [the longest x1 6.18 us: body(): call(attention_kernel, sds((N_Z, TGT + BLOCK, LANES), BF), in_specs=[SMEM...]
  transfers between devices with their start and end apart: 21 -> 22, of which waited for: 14 -> 9; matrix products, arithmetic and copies ran while one was open for 4% -> 4% of each run, Pallas kernels for 17% -> 19%
where the time goes in v3:
time: 195 us; the launch traced here: 193 us
  waiting for transfers between devices  61.3 us (31%)
  starting transfers between devices  54.3 us (28%)
  Pallas kernels  49.4 us (25%)
  blocking collectives  14.3 us (7%)
  other arithmetic  6.68 us (3%)
  local copies, waits for them, and re-layouts  4.65 us (2%)
  matrix products  2.11 us (1%)
    all_to_all x5, starting transfers between devices, exchange(): return lax.all_to_all(pieces, axes, split_axis=0, concat_axis=0, tiled=True)  25.2 us
    all_to_all x5, waiting for transfers between devices, exchange(): return lax.all_to_all(pieces, axes, split_axis=0, concat_axis=0, tiled=True)  16.9 us
    ppermute x4, waiting for transfers between devices, ring(): below = lax.ppermute(below, 'z', up)  16.1 us
    ppermute x1, waiting for transfers between devices, body(): got = lax.ppermute(send, 'grp', SWAP)  15.8 us
    all_to_all x1, blocking collectives, to_all(): return lax.all_to_all(copies, axes, split_axis=0, concat_axis=0, tiled=True)  14.3 us
    ppermute x3, starting transfers between devices, ring(): above = lax.ppermute(above, 'z', down)  10 us
    all_to_all x1, waiting for transfers between devices, body(): lax.all_to_all(stripes, (*DP, 'grp'), split_axis=0, concat_axis=0, tiled=...  8.89 us
    pallas_call x1, Pallas kernels, body(): call(blend_kernel, sds((half, width), F32), grid=(width // LANES,), in_sp...  8.84 us
  transfers between devices with their start and end apart: 22, of which 9 were waited for; matrix products, arithmetic and copies ran while one was open for 4% of the time, Pallas kernels for 19%

profile of v3, /device:TPU:1, one launch (start us, length us, event | category | flops | bytes accessed | tf_op | source)
XLA Modules:
  0.0 193.4 jit_solution(6034289906293298325)
XLA Ops:
  0.6 2.3 %shard_map.95 = (bf16[128,1408]{1,0:T(8,128)(2,1)}, bf16[128,128]{1,0:T(8,128)(2,1)}) custom-call(bf16[128,1408]{1,0:T(8,128)(2,1)} %bitcast.25, s32[1,128]{1,0:T(1,128)} %context_ref.1), custom_call_target="tpu_custom_call" | custom-call | flops 1000000 | bytes 1000000 | tf_op jit(solution)/shard_map/pallas_call | solution.py:318
  2.9 3.3 %shard_map.97 = (bf16[8,176,384]{2,1,0:T(8,128)(2,1)}, bf16[8,176,384]{2,1,0:T(8,128)(2,1)}) custom-call(s32[1]{0:T(128)} %bitcast.2.z_ref, s32[1]{0:T(128)} %bitcast.core_ref, bf16[3,176,704]{2,1,0:T(8,128)(2,1)} %target_ref, bf16[3,176,704]{2,1,0:T(8,128)(2,1)} %student_ref.1, bf16[176,704]{1,0:T(8,128)(2,1)} %bitcast.29), custom_call_target="tpu_custom_call" | custom-call | flops 1000000 | bytes 1000000 | tf_op jit(solution)/shard_map/pallas_call | solution.py:350
  6.2 6.0 %all-to-all-start = ((bf16[8,176,384]{2,1,0:T(8,128)(2,1)}), bf16[8,176,384]{2,1,0:T(8,128)(2,1)S(1)}, u32[]{:S(2)}, u32[]{:S(2)}) async-start(bf16[8,176,384]{2,1,0:T(8,128)(2,1)} %get-tuple-element.38), calls=%async_computation | async-start | bytes 2162688 | tf_op jit(solution)/shard_map/all_to_all | solution.py:66
  12.2 1.7 collective-permute-start
  13.9 4.0 %collective-permute-start.1 = (bf16[128,1408]{1,0:T(8,128)(2,1)}, bf16[128,1408]{1,0:T(8,128)(2,1)}, u32[]{:S(2)}, u32[]{:S(2)}) collective-permute-start(bf16[128,1408]{1,0:T(8,128)(2,1)} %get-tuple-element.30.refs_0_), channel_id=1, source_target_pairs={{0,224},{32,0},{64,32},{96,64},{128,96},{160,128},{192,160},{224,1... | collective-permute-start | bytes 1081352 | tf_op jit(solution)/shard_map/ppermute | solution.py:300
  17.9 2.2 %fusion = (f32[128,704]{1,0:T(8,128)}, f32[128,704]{1,0:T(8,128)}) fusion(f32[704]{0:T(1024)S(1)} %multiply_exponential_fusion), kind=kLoop, calls=%fused_computation.2 | loop fusion | flops 90112 | bytes 723712 | tf_op jit(solution)/shard_map/cos | solution.py:328
  20.1 0.8 multiply_cosine_fusion.1
  20.9 0.7 reshape.54.mask_ref
  21.6 6.8 %shard_map.96 = (bf16[1024,704]{1,0:T(8,128)(2,1)}, bf16[1024,704]{1,0:T(8,128)(2,1)}) custom-call(f32[128,704]{1,0:T(8,128)} %get-tuple-element.63.sin_ref, f32[128,704]{1,0:T(8,128)} %get-tuple-element.62.cos_ref, f32[8,704]{1,0:T(8,128)} %get-tuple-element.61.bsin_ref, f32[8,704]{1,0:T(8,128)} %get-tuple-element.60.bcos_ref, f32[2,704]{1,0:T(2,128)} %reshape.54.mask_ref), custom_call_target="tpu_custom_call" | custom-call | flops 1000000 | bytes 1000000 | tf_op jit(solution)/shard_map/pallas_call | solution.py:335
  28.4 0.0 all-to-all-done
  28.4 1.3 collective-permute-start.8
  29.7 0.1 collective-permute-start.2
  29.8 5.3 %all-to-all-start.1 = ((bf16[8,176,384]{2,1,0:T(8,128)(2,1)}), bf16[8,176,384]{2,1,0:T(8,128)(2,1)S(1)}, u32[]{:S(2)}, u32[]{:S(2)}) async-start(bf16[8,176,384]{2,1,0:T(8,128)(2,1)} %get-tuple-element.48), calls=%async_computation.1 | async-start | bytes 2162688 | tf_op jit(solution)/shard_map/all_to_all | solution.py:66
  35.2 0.0 collective-permute-done.2
  35.2 0.7 pad_add_fusion.listed_ref
  35.8 0.0 collective-permute-done.refs_1_
  35.8 0.0 collective-permute-done.1.refs_6_
  35.8 0.0 collective-permute-start.3
  35.8 3.3 %collective-permute-start.4 = (bf16[128,1408]{1,0:T(8,128)(2,1)}, bf16[128,1408]{1,0:T(8,128)(2,1)}, u32[]{:S(2)}, u32[]{:S(2)}) collective-permute-start(bf16[128,1408]{1,0:T(8,128)(2,1)} %collective-permute-done.1.refs_6_), channel_id=1, source_target_pairs={{0,224},{32,0},{64,32},{96,64},{128,96},{160,128},{192,160},{224,1... | collective-permute-start | bytes 1081352 | tf_op jit(solution)/shard_map/ppermute | solution.py:300
  39.2 8.5 %collective-permute-done.3.refs_2_ = bf16[128,1408]{1,0:T(8,128)(2,1)S(1)} collective-permute-done((bf16[128,1408]{1,0:T(8,128)(2,1)}, bf16[128,1408]{1,0:T(8,128)(2,1)S(1)}, u32[]{:S(2)}, u32[]{:S(2)}) %collective-permute-start.3) | collective-permute-done | bytes 360480 | tf_op jit(solution)/shard_map/ppermute | solution.py:299
  47.7 2.7 %collective-permute-start.7 = (bf16[128,1408]{1,0:T(8,128)(2,1)}, bf16[128,1408]{1,0:T(8,128)(2,1)}, u32[]{:S(2)}, u32[]{:S(2)}) collective-permute-start(bf16[128,1408]{1,0:T(8,128)(2,1)} %collective-permute-done.4.refs_5_), channel_id=1, source_target_pairs={{0,224},{32,0},{64,32},{96,64},{128,96},{160,128},{192,160},{224,1... | collective-permute-start | bytes 1081352 | tf_op jit(solution)/shard_map/ppermute | solution.py:300
  50.4 7.6 %collective-permute-done.5.refs_3_ = bf16[128,1408]{1,0:T(8,128)(2,1)} collective-permute-done((bf16[128,1408]{1,0:T(8,128)(2,1)S(1)}, bf16[128,1408]{1,0:T(8,128)(2,1)}, u32[]{:S(2)}, u32[]{:S(2)}) %collective-permute-start.5) | collective-permute-done | bytes 360480 | tf_op jit(solution)/shard_map/ppermute | solution.py:299
  58.0 1.0 copy-done.1
  59.0 4.5 %shard_map.98.query_s_ref = bf16[1024,128]{1,0:T(8,128)(2,1)} custom-call(s32[1]{0:T(128)} %bitcast.core_ref, bf16[1024,704]{1,0:T(8,128)(2,1)} %get-tuple-element.33.lower_ref, bf16[1024,704]{1,0:T(8,128)(2,1)} %get-tuple-element.34.upper_ref, bf16[1408,384]{1,0:T(8,128)(2,1)} %bitcast.17, bf16[1408,384]{1,0:T(8,128)(2,1)} %copy-done.1), custom_call_target="tpu_custom_call" | custom-call | flops 1000000 | bytes 1000000 | tf_op jit(solution)/shard_map/pallas_call | solution.py:367
  63.5 0.0 collective-permute-done.7.refs_4_
  63.5 4.9 %shard_map.99 = (bf16[8,96,128]{2,1,0:T(8,128)(2,1)}, bf16[896,256]{1,0:T(8,128)(2,1)}, bf16[224,256]{1,0:T(8,128)(2,1)}) custom-call(s32[1]{0:T(128)} %bitcast.2.z_ref, s32[1]{0:T(128)} %bitcast.core_ref, bf16[128,1408]{1,0:T(8,128)(2,1)} %get-tuple-element.30.refs_0_, bf16[128,1408]{1,0:T(8,128)(2,1)} %collective-permute-done.refs_1_, ...), custom_call_target="tpu_custom_call" | custom-call | flops 1000000 | bytes 1000000 | tf_op jit(solution)/shard_map/pallas_call | solution.py:375
  68.4 1.8 collective-permute-start.9
  70.2 0.3 collective-permute-start.12
  70.5 3.0 %shard_map.100 = (bf16[8,96,128]{2,1,0:T(8,128)(2,1)}, bf16[128,256]{1,0:T(8,128)(2,1)}, bf16[256,256]{1,0:T(8,128)(2,1)}) custom-call(s32[1]{0:T(128)} %bitcast.2.z_ref, s32[1]{0:T(128)} %bitcast.core_ref, bf16[128,1408]{1,0:T(8,128)(2,1)} %collective-permute-done.6.last_ref, bf16[8,96,128]{2,1,0:T(8,128)(2,1)} %get-tuple-element.41.early_ref, ...), custom_call_target="tpu_custom_call" | custom-call | flops 1000000 | bytes 1000000 | tf_op jit(solution)/shard_map/pallas_call | solution.py:390
  73.5 0.2 collective-permute-start.11
  73.7 0.4 collective-permute-start.10
  74.1 1.1 collective-permute-done.10.last_other_ref
  75.2 0.0 copy-start.7
  75.2 0.6 copy-done.12
  75.8 0.1 copy-done.11
  75.9 0.1 copy-done.7
  76.0 6.2 %shard_map.101 = bf16[8,224,128]{2,1,0:T(8,128)(2,1)} custom-call(s32[1]{0:T(128)} %bitcast.core_ref, bf16[8,96,128]{2,1,0:T(8,128)(2,1)} %get-tuple-element.43.query_ref, bf16[896,256]{1,0:T(8,128)(2,1)} %get-tuple-element.44.kv_ref, bf16[896,256]{1,0:T(8,128)(2,1)} %copy-done.7, bf16[128,256]{1,0:T(8,128)(2,1)} %get-tuple-element.45.last_ref, ...), custom_call_target="tpu_custom_call" | custom-call | flops 1000000 | bytes 1000000 | tf_op jit(solution)/shard_map/pallas_call | solution.py:401
  82.2 5.6 %all-to-all-start.2 = ((bf16[8,224,128]{2,1,0:T(8,128)(2,1)}), bf16[8,224,128]{2,1,0:T(8,128)(2,1)S(1)}, u32[]{:S(2)}, u32[]{:S(2)}) async-start(bf16[8,224,128]{2,1,0:T(8,128)(2,1)} %shard_map.101), calls=%async_computation.2 | async-start | bytes 917504 | tf_op jit(solution)/shard_map/all_to_all | solution.py:66
  87.8 0.8 multiply_reduce_fusion
  88.6 15.7 %all-to-all-done.2.got_ref = bf16[8,224,128]{2,1,0:T(8,128)(2,1)S(1)} async-done(((bf16[8,224,128]{2,1,0:T(8,128)(2,1)}), bf16[8,224,128]{2,1,0:T(8,128)(2,1)S(1)}, u32[]{:S(2)}, u32[]{:S(2)}) %all-to-all-start.2) | async-done | bytes 458784 | tf_op jit(solution)/shard_map/all_to_all | solution.py:66
  104.3 0.8 copy-done.4
  105.1 4.8 %shard_map.102 = (bf16[96,1408]{1,0:T(8,128)(2,1)}, bf16[96,1408]{1,0:T(8,128)(2,1)}, bf16[8,96,768]{2,1,0:T(8,128)(2,1)}, f32[48,128]{1,0:T(8,128)}) custom-call(s32[1]{0:T(128)} %bitcast.1.grp_ref, s32[1]{0:T(128)} %bitcast.core_ref, bf16[8,224,128]{2,1,0:T(8,128)(2,1)} %copy-done.4, bf16[128,128]{1,0:T(8,128)(2,1)} %get-tuple-element.50.perm_ref, ...), custom_call_target="tpu_custom_call" | custom-call | flops 1000000 | bytes 1000000 | tf_op jit(solution)/shard_map/pallas_call | solution.py:405
  109.9 4.9 %all-to-all-start.3 = ((bf16[8,96,768]{2,1,0:T(8,128)(2,1)}), bf16[8,96,768]{2,1,0:T(8,128)(2,1)S(1)}, u32[]{:S(2)}, u32[]{:S(2)}) async-start(bf16[8,96,768]{2,1,0:T(8,128)(2,1)} %get-tuple-element.54), calls=%async_computation.3 | async-start | bytes 2359296 | tf_op jit(solution)/shard_map/all_to_all | solution.py:66
  114.8 0.6 multiply_sine_fusion
  115.4 2.7 %collective-permute-start.13 = (bf16[96,1408]{1,0:T(8,128)(2,1)S(1)}, bf16[96,1408]{1,0:T(8,128)(2,1)S(1)}, u32[]{:S(2)}, u32[]{:S(2)}) collective-permute-start(bf16[96,1408]{1,0:T(8,128)(2,1)S(1)} %copy-done.15), channel_id=1, source_target_pairs={{0,8},{8,0},{1,9},{9,1},{2,10},{10,2},{3,11},{11,3},{4,12},{12,4},... | collective-permute-start | bytes 811016 | tf_op jit(solution)/shard_map/ppermute | solution.py:422
  118.2 0.8 maximum_add_fusion.seeds_ref
  119.0 1.6 fusion.2.tokens_ref
  120.6 15.8 %collective-permute-done.13.got_ref = bf16[96,1408]{1,0:T(8,128)(2,1)S(1)} collective-permute-done((bf16[96,1408]{1,0:T(8,128)(2,1)S(1)}, bf16[96,1408]{1,0:T(8,128)(2,1)S(1)}, u32[]{:S(2)}, u32[]{:S(2)}) %collective-permute-start.13) | collective-permute-done | bytes 270368 | tf_op jit(solution)/shard_map/ppermute | solution.py:422
  136.4 0.7 copy-done.9
  137.1 2.6 %shard_map.103 = bf16[16,48,256]{2,1,0:T(8,128)(2,1)} custom-call(bf16[96,1408]{1,0:T(8,128)(2,1)} %get-tuple-element.51.keep_ref, bf16[96,1408]{1,0:T(8,128)(2,1)} %copy-done.9, f32[48,1408]{1,0:T(8,128)} %fusion.2.tokens_ref, f32[48,1408]{1,0:T(8,128)} %maximum_add_fusion.seeds_ref, f32[48,128]{1,0:T(8,128)} %get-tuple-element.53.count_ref), custom_call_target="tpu_custom_call" | custom-call | flops 1000000 | bytes 1000000 | tf_op jit(solution)/shard_map/pallas_call | solution.py:425
  139.7 5.9 %all-to-all-start.4 = ((bf16[16,48,256]{2,1,0:T(8,128)(2,1)}), bf16[16,48,256]{2,1,0:T(8,128)(2,1)S(1)}, u32[]{:S(2)}, u32[]{:S(2)}) async-start(bf16[16,48,256]{2,1,0:T(8,128)(2,1)} %shard_map.103), calls=%async_computation.4 | async-start | bytes 786432 | tf_op jit(solution)/shard_map/all_to_all | solution.py:429
  145.6 8.9 %all-to-all-done.4 = bf16[16,48,256]{2,1,0:T(8,128)(2,1)S(1)} async-done(((bf16[16,48,256]{2,1,0:T(8,128)(2,1)}), bf16[16,48,256]{2,1,0:T(8,128)(2,1)S(1)}, u32[]{:S(2)}, u32[]{:S(2)}) %all-to-all-start.4) | async-done | bytes 393248 | tf_op jit(solution)/shard_map/all_to_all | solution.py:429
  154.5 0.5 fusion.6
  155.0 2.3 %collective-permute-start.14 = (f32[128,768]{1,0:T(8,128)S(1)}, f32[128,768]{1,0:T(8,128)S(1)}, u32[]{:S(2)}, u32[]{:S(2)}) collective-permute-start(f32[128,768]{1,0:T(8,128)S(1)} %slice_select_fusion), channel_id=1, source_target_pairs={{0,16},{16,0},{1,17},{17,1},{2,18},{18,2},{3,19},{19,3},{4,20},{20... | collective-permute-start | bytes 1179656 | tf_op jit(solution)/shard_map/ppermute | solution.py:439
  157.3 1.3 collective-permute-done.14
  158.7 0.7 add_convert_fusion
  159.4 3.4 %all-to-all-start.5 = ((bf16[8,16,768]{2,1,0:T(8,128)(2,1)}), bf16[8,16,768]{2,1,0:T(8,128)(2,1)S(1)}, u32[]{:S(2)}, u32[]{:S(2)}) async-start(bf16[8,16,768]{2,1,0:T(8,128)(2,1)} %bitcast.9), calls=%async_computation.5 | async-start | bytes 393216 | tf_op jit(solution)/shard_map/all_to_all | solution.py:66
  162.8 8.8 %shard_map.104 = f32[704,1408]{1,0:T(8,128)} custom-call(s32[1]{0:T(128)} %bitcast.core_ref, bf16[704,1408]{1,0:T(8,128)(2,1)} %target_ref.1, bf16[1408,384]{1,0:T(8,128)(2,1)} %bitcast.22, bf16[1408,384]{1,0:T(8,128)(2,1)} %copy-done.3), custom_call_target="tpu_custom_call" | custom-call | flops 1000000 | bytes 1000000 | tf_op jit(solution)/shard_map/pallas_call | solution.py:443
  171.6 1.1 all-to-all-done.5
  172.8 14.3 %all_to_all.35 = bf16[8,16,768]{2,1,0:T(8,128)(2,1)S(1)} all-to-all(bf16[8,16,768]{2,1,0:T(8,128)(2,1)S(1)} %broadcast_in_dim.2), channel_id=1, replica_groups=mesh['z'=8,'core'=2,'grp'=2,'ylo'=2,'x'=4] {'z'}, dimensions={0} | all-to-all | bytes 393216 | tf_op jit(solution)/shard_map/all_to_all | solution.py:62
  187.0 2.4 %collective-permute-start.15 = (bf16[128,768]{1,0:T(8,128)(2,1)S(1)}, bf16[128,768]{1,0:T(8,128)(2,1)S(1)}, u32[]{:S(2)}, u32[]{:S(2)}) collective-permute-start(bf16[128,768]{1,0:T(8,128)(2,1)S(1)} %bitcast.26), channel_id=1, source_target_pairs={{0,16},{16,0},{1,17},{17,1},{2,18},{18,2},{3,19},{19,3},{4,20},{20... | collective-permute-start | bytes 589832 | tf_op jit(solution)/shard_map/ppermute | solution.py:452
  189.5 1.1 collective-permute-done.15.other_ref
  190.5 0.7 copy-done.10
  191.2 2.2 %shard_map.105 = f32[176,704]{1,0:T(8,128)} custom-call(s32[1]{0:T(128)} %bitcast.core_ref, bf16[128,768]{1,0:T(8,128)(2,1)} %bitcast.27, bf16[128,768]{1,0:T(8,128)(2,1)} %copy-done.10), custom_call_target="tpu_custom_call" | custom-call | flops 1000000 | bytes 1000000 | tf_op jit(solution)/shard_map/pallas_call | solution.py:453
  (40 shorter events, 0.2 us)
Async XLA Ops:
  6.2 14.7 %copy-start.13 = (f32[1408]{0:T(1024)S(1)}, f32[1408]{0:T(1024)}, u32[]{:S(2)}) copy-start(f32[1408]{0:T(1024)} %param.15) | copy-start | bytes 16900
  6.2 22.2 %all-to-all-start = ((bf16[8,176,384]{2,1,0:T(8,128)(2,1)}), bf16[8,176,384]{2,1,0:T(8,128)(2,1)S(1)}, u32[]{:S(2)}, u32[]{:S(2)}) async-start(bf16[8,176,384]{2,1,0:T(8,128)(2,1)} %get-tuple-element.38), calls=%async_computation | async-start | bytes 2162688 | tf_op jit(solution)/shard_map/all_to_all | solution.py:66
  12.2 17.6 %copy-start.14 = (s32[1,192]{1,0:T(1,128)S(1)}, s32[1,192]{1,0:T(1,128)}, u32[]{:S(2)}) copy-start(s32[1,192]{1,0:T(1,128)} %param.10) | copy-start | bytes 2308
  12.2 23.7 %collective-permute-start = (bf16[128,1408]{1,0:T(8,128)(2,1)}, bf16[128,1408]{1,0:T(8,128)(2,1)}, u32[]{:S(2)}, u32[]{:S(2)}) collective-permute-start(bf16[128,1408]{1,0:T(8,128)(2,1)} %get-tuple-element.30.refs_0_), channel_id=1, source_target_pairs={{0,32},{32,64},{64,96},{96,128},{128,160},{160,192},{192,224},{224... | collective-permute-start | bytes 1081352 | tf_op jit(solution)/shard_map/ppermute | solution.py:299
  13.9 21.9 %collective-permute-start.1 = (bf16[128,1408]{1,0:T(8,128)(2,1)}, bf16[128,1408]{1,0:T(8,128)(2,1)}, u32[]{:S(2)}, u32[]{:S(2)}) collective-permute-start(bf16[128,1408]{1,0:T(8,128)(2,1)} %get-tuple-element.30.refs_0_), channel_id=1, source_target_pairs={{0,224},{32,0},{64,32},{96,64},{128,96},{160,128},{192,160},{224,1... | collective-permute-start | bytes 1081352 | tf_op jit(solution)/shard_map/ppermute | solution.py:300
  28.4 29.6 %copy-start = (bf16[8,176,384]{2,1,0:T(8,128)(2,1)}, bf16[8,176,384]{2,1,0:T(8,128)(2,1)S(1)}, u32[]{:S(2)}) copy-start(bf16[8,176,384]{2,1,0:T(8,128)(2,1)S(1)} %all-to-all-done) | copy-start | bytes 3244036
  28.4 29.6 %collective-permute-start.8 = (bf16[1408,384]{1,0:T(8,128)(2,1)S(1)}, bf16[1408,384]{1,0:T(8,128)(2,1)S(1)}, u32[]{:S(2)}, u32[]{:S(2)}) collective-permute-start(bf16[1408,384]{1,0:T(8,128)(2,1)S(1)} %bitcast.16), channel_id=1, source_target_pairs={{0,16},{16,0},{1,17},{17,1},{2,18},{18,2},{3,19},{19,3},{4,20},{20... | collective-permute-start | bytes 3244040 | tf_op jit(solution)/shard_map/ppermute | solution.py:355
  29.7 5.4 %collective-permute-start.2 = (s32[1,192]{1,0:T(1,128)S(1)}, s32[1,192]{1,0:T(1,128)S(1)}, u32[]{:S(2)}, u32[]{:S(2)}) collective-permute-start(s32[1,192]{1,0:T(1,128)S(1)} %copy-done.14), channel_id=1, source_target_pairs={{0,16},{16,0},{1,17},{17,1},{2,18},{18,2},{3,19},{19,3},{4,20},{20... | collective-permute-start | bytes 2312 | tf_op jit(solution)/shard_map/ppermute | solution.py:346
  29.8 40.4 %all-to-all-start.1 = ((bf16[8,176,384]{2,1,0:T(8,128)(2,1)}), bf16[8,176,384]{2,1,0:T(8,128)(2,1)S(1)}, u32[]{:S(2)}, u32[]{:S(2)}) async-start(bf16[8,176,384]{2,1,0:T(8,128)(2,1)} %get-tuple-element.48), calls=%async_computation.1 | async-start | bytes 2162688 | tf_op jit(solution)/shard_map/all_to_all | solution.py:66
  35.8 11.8 %collective-permute-start.3 = (bf16[128,1408]{1,0:T(8,128)(2,1)}, bf16[128,1408]{1,0:T(8,128)(2,1)S(1)}, u32[]{:S(2)}, u32[]{:S(2)}) collective-permute-start(bf16[128,1408]{1,0:T(8,128)(2,1)} %collective-permute-done.refs_1_), channel_id=1, source_target_pairs={{0,32},{32,64},{64,96},{96,128},{128,160},{160,192},{192,224},{224... | collective-permute-start | bytes 1081352 | tf_op jit(solution)/shard_map/ppermute | solution.py:299
  35.8 11.8 %collective-permute-start.4 = (bf16[128,1408]{1,0:T(8,128)(2,1)}, bf16[128,1408]{1,0:T(8,128)(2,1)}, u32[]{:S(2)}, u32[]{:S(2)}) collective-permute-start(bf16[128,1408]{1,0:T(8,128)(2,1)} %collective-permute-done.1.refs_6_), channel_id=1, source_target_pairs={{0,224},{32,0},{64,32},{96,64},{128,96},{160,128},{192,160},{224,1... | collective-permute-start | bytes 1081352 | tf_op jit(solution)/shard_map/ppermute | solution.py:300
  47.7 10.3 %copy-start.8 = (bf16[128,1408]{1,0:T(8,128)(2,1)}, bf16[128,1408]{1,0:T(8,128)(2,1)S(1)}, u32[]{:S(2)}) copy-start(bf16[128,1408]{1,0:T(8,128)(2,1)S(1)} %collective-permute-done.3.refs_2_) | copy-start | bytes 1081348
  47.7 10.3 %collective-permute-start.5 = (bf16[128,1408]{1,0:T(8,128)(2,1)S(1)}, bf16[128,1408]{1,0:T(8,128)(2,1)}, u32[]{:S(2)}, u32[]{:S(2)}) collective-permute-start(bf16[128,1408]{1,0:T(8,128)(2,1)S(1)} %collective-permute-done.3.refs_2_), channel_id=1, source_target_pairs={{0,32},{32,64},{64,96},{96,128},{128,160},{160,192},{192,224},{224... | collective-permute-start | bytes 1081352 | tf_op jit(solution)/shard_map/ppermute | solution.py:299
  47.7 15.8 %collective-permute-start.7 = (bf16[128,1408]{1,0:T(8,128)(2,1)}, bf16[128,1408]{1,0:T(8,128)(2,1)}, u32[]{:S(2)}, u32[]{:S(2)}) collective-permute-start(bf16[128,1408]{1,0:T(8,128)(2,1)} %collective-permute-done.4.refs_5_), channel_id=1, source_target_pairs={{0,224},{32,0},{64,32},{96,64},{128,96},{160,128},{192,160},{224,1... | collective-permute-start | bytes 1081352 | tf_op jit(solution)/shard_map/ppermute | solution.py:300
  58.0 12.5 %collective-permute-start.6 = (bf16[128,1408]{1,0:T(8,128)(2,1)}, bf16[128,1408]{1,0:T(8,128)(2,1)}, u32[]{:S(2)}, u32[]{:S(2)}) collective-permute-start(bf16[128,1408]{1,0:T(8,128)(2,1)} %collective-permute-done.5.refs_3_), channel_id=1, source_target_pairs={{0,32},{32,64},{64,96},{96,128},{128,160},{160,192},{192,224},{224... | collective-permute-start | bytes 1081352 | tf_op jit(solution)/shard_map/ppermute | solution.py:303
  58.0 1.0 copy-start.1
  68.4 6.8 %collective-permute-start.9 = (bf16[896,256]{1,0:T(8,128)(2,1)}, bf16[896,256]{1,0:T(8,128)(2,1)S(1)}, u32[]{:S(2)}, u32[]{:S(2)}) collective-permute-start(bf16[896,256]{1,0:T(8,128)(2,1)} %get-tuple-element.44.kv_ref), channel_id=1, source_target_pairs={{0,16},{16,0},{1,17},{17,1},{2,18},{18,2},{3,19},{19,3},{4,20},{20... | collective-permute-start | bytes 1376264 | tf_op jit(solution)/shard_map/ppermute | solution.py:389
  70.2 3.3 %copy-start.2 = (bf16[8,176,384]{2,1,0:T(8,128)(2,1)}, bf16[8,176,384]{2,1,0:T(8,128)(2,1)S(1)}, u32[]{:S(2)}) copy-start(bf16[8,176,384]{2,1,0:T(8,128)(2,1)S(1)} %all-to-all-done.1) | copy-start | bytes 3244036
  70.2 18.4 %collective-permute-start.12 = (bf16[1408,384]{1,0:T(8,128)(2,1)S(1)}, bf16[1408,384]{1,0:T(8,128)(2,1)S(1)}, u32[]{:S(2)}, u32[]{:S(2)}) collective-permute-start(bf16[1408,384]{1,0:T(8,128)(2,1)S(1)} %bitcast.20), channel_id=1, source_target_pairs={{0,16},{16,0},{1,17},{17,1},{2,18},{18,2},{3,19},{19,3},{4,20},{20... | collective-permute-start | bytes 3244040 | tf_op jit(solution)/shard_map/ppermute | solution.py:357
  73.5 1.7 collective-permute-start.11
  73.7 1.5 collective-permute-start.10
  75.2 0.6 copy-start.12
  75.2 0.7 copy-start.11
  75.2 0.8 copy-start.7
  82.2 22.1 %all-to-all-start.2 = ((bf16[8,224,128]{2,1,0:T(8,128)(2,1)}), bf16[8,224,128]{2,1,0:T(8,128)(2,1)S(1)}, u32[]{:S(2)}, u32[]{:S(2)}) async-start(bf16[8,224,128]{2,1,0:T(8,128)(2,1)} %shard_map.101), calls=%async_computation.2 | async-start | bytes 917504 | tf_op jit(solution)/shard_map/all_to_all | solution.py:66
  88.6 15.7 %copy-start.3 = (bf16[1408,384]{1,0:T(8,128)(2,1)}, bf16[1408,384]{1,0:T(8,128)(2,1)S(1)}, u32[]{:S(2)}) copy-start(bf16[1408,384]{1,0:T(8,128)(2,1)S(1)} %collective-permute-done.12.other_ref) | copy-start | bytes 3244036
  104.3 0.8 copy-start.4
  109.9 5.5 %copy-start.15 = (bf16[96,1408]{1,0:T(8,128)(2,1)S(1)}, bf16[96,1408]{1,0:T(8,128)(2,1)}, u32[]{:S(2)}) copy-start(bf16[96,1408]{1,0:T(8,128)(2,1)} %get-tuple-element.52) | copy-start | bytes 811012
  109.9 9.1 %copy-start.5 = (bf16[1,128,1408]{2,1,0:T(8,128)(2,1)S(1)}, bf16[1,128,1408]{2,1,0:T(8,128)(2,1)}, u32[]{:S(2)}) copy-start(bf16[1,128,1408]{2,1,0:T(8,128)(2,1)} %param.8) | copy-start | bytes 1081348
  109.9 29.8 %all-to-all-start.3 = ((bf16[8,96,768]{2,1,0:T(8,128)(2,1)}), bf16[8,96,768]{2,1,0:T(8,128)(2,1)S(1)}, u32[]{:S(2)}, u32[]{:S(2)}) async-start(bf16[8,96,768]{2,1,0:T(8,128)(2,1)} %get-tuple-element.54), calls=%async_computation.3 | async-start | bytes 2359296 | tf_op jit(solution)/shard_map/all_to_all | solution.py:66
  115.4 21.0 %collective-permute-start.13 = (bf16[96,1408]{1,0:T(8,128)(2,1)S(1)}, bf16[96,1408]{1,0:T(8,128)(2,1)S(1)}, u32[]{:S(2)}, u32[]{:S(2)}) collective-permute-start(bf16[96,1408]{1,0:T(8,128)(2,1)S(1)} %copy-done.15), channel_id=1, source_target_pairs={{0,8},{8,0},{1,9},{9,1},{2,10},{10,2},{3,11},{11,3},{4,12},{12,4},... | collective-permute-start | bytes 811016 | tf_op jit(solution)/shard_map/ppermute | solution.py:422
  136.4 0.7 copy-start.9
  139.7 14.8 %all-to-all-start.4 = ((bf16[16,48,256]{2,1,0:T(8,128)(2,1)}), bf16[16,48,256]{2,1,0:T(8,128)(2,1)S(1)}, u32[]{:S(2)}, u32[]{:S(2)}) async-start(bf16[16,48,256]{2,1,0:T(8,128)(2,1)} %shard_map.103), calls=%async_computation.4 | async-start | bytes 786432 | tf_op jit(solution)/shard_map/all_to_all | solution.py:429
  155.0 3.6 %collective-permute-start.14 = (f32[128,768]{1,0:T(8,128)S(1)}, f32[128,768]{1,0:T(8,128)S(1)}, u32[]{:S(2)}, u32[]{:S(2)}) collective-permute-start(f32[128,768]{1,0:T(8,128)S(1)} %slice_select_fusion), channel_id=1, source_target_pairs={{0,16},{16,0},{1,17},{17,1},{2,18},{18,2},{3,19},{19,3},{4,20},{20... | collective-permute-start | bytes 1179656 | tf_op jit(solution)/shard_map/ppermute | solution.py:439
  159.4 13.3 %all-to-all-start.5 = ((bf16[8,16,768]{2,1,0:T(8,128)(2,1)}), bf16[8,16,768]{2,1,0:T(8,128)(2,1)S(1)}, u32[]{:S(2)}, u32[]{:S(2)}) async-start(bf16[8,16,768]{2,1,0:T(8,128)(2,1)} %bitcast.9), calls=%async_computation.5 | async-start | bytes 393216 | tf_op jit(solution)/shard_map/all_to_all | solution.py:66
  187.0 3.5 %copy-start.6 = (bf16[8,16,768]{2,1,0:T(8,128)(2,1)}, bf16[8,16,768]{2,1,0:T(8,128)(2,1)S(1)}, u32[]{:S(2)}) copy-start(bf16[8,16,768]{2,1,0:T(8,128)(2,1)S(1)} %all_to_all.35) | copy-start | bytes 589828
  187.0 3.5 %collective-permute-start.15 = (bf16[128,768]{1,0:T(8,128)(2,1)S(1)}, bf16[128,768]{1,0:T(8,128)(2,1)S(1)}, u32[]{:S(2)}, u32[]{:S(2)}) collective-permute-start(bf16[128,768]{1,0:T(8,128)(2,1)S(1)} %bitcast.26), channel_id=1, source_target_pairs={{0,16},{16,0},{1,17},{17,1},{2,18},{18,2},{3,19},{19,3},{4,20},{20... | collective-permute-start | bytes 589832 | tf_op jit(solution)/shard_map/ppermute | solution.py:452
  190.5 0.7 copy-start.10
